TPU v7x, 32 devices: a whole 2x2x4 slice. The times are simulated.
32 devices in a mesh: groups: 2 (over x), gx: 16 (over z, y, core).
Axes of the slice: x: 2, y: 2, z: 4, core: 2. Of those that a mesh axis runs over, the one named last changes fastest.
Arguments:
- volume: bfloat16 [32, 64, 16, 256], P(None, ('groups', 'gx')), parts along dimension 1, may hold values from -6 to 6
- weight_two: bfloat16 [32, 32, 3, 3, 3], replicated, may hold values from -0.21875 to 0.21875
- weight_three: bfloat16 [64, 32, 3, 3, 3], replicated, may hold values from -0.21875 to 0.21875
- cotangent: bfloat16 [64, 32, 8, 128], P(None, ('groups', 'gx')), parts along dimension 1, may hold values from -6 to 6
Outputs:
- features_three: bfloat16 [64, 32, 8, 128], P(None, ('groups', 'gx')), parts along dimension 1
- grad_three: float32 [128, 32, 3, 3, 3], P(('groups', 'gx')), parts along dimension 0
- grad_two: float32 [64, 32, 3, 3, 3], P('groups'), parts along dimension 0
- grad_volume: bfloat16 [32, 64, 16, 256], P(None, ('groups', 'gx')), parts along dimension 1
There are 2 independent parts, one for each index of `groups`. A program takes and returns all parts, laid end to end along the dimension named above; an argument that names none is the same for every part. Nothing has to cross between parts.
All inputs are finite; a program needn't handle non-finite values.
Results may differ from a plain program's by a relative error of at most 0.012.
Values may be sent and summed in bfloat16 or wider, within the bound.
No kernel may reach another device: no remote copies, remote signals or barrier semaphores. Data moves between devices by JAX's collectives and lax.ppermute only.
A program may use at most 128 MiB of HBM per device.

v0:
```python
import functools

import jax
import jax.numpy as jnp
from jax import lax
from jax.experimental import pallas as pl
from jax.experimental.pallas import tpu as pltpu
from jax.sharding import PartitionSpec as P

BF = jnp.bfloat16
F32 = jnp.float32
LANES = 128
VMEM = pl.BlockSpec(memory_space=pltpu.VMEM)


def dot(a, b):
    return jnp.dot(a, b, preferred_element_type=F32)


def dot_nt(a, b):
    return lax.dot_general(a, b, (((1,), (1,)), ((), ())), preferred_element_type=F32)


def iota(shape, dim):
    return lax.broadcasted_iota(jnp.int32, shape, dim)


def place(rows, lanes, offset):
    return (iota((rows, lanes), 1) == iota((rows, lanes), 0) + offset).astype(F32).astype(BF)


def moved(x, step, width):
    lanes = x.shape[1]
    w = iota(x.shape, 1) % width
    rolled = pltpu.roll(x, (-step) % lanes, 1)
    edge = width - 1 if step > 0 else 0
    return jnp.where(w == edge, 0.0, rolled)


def taps_sum(y, rows, width):
    return y[rows : 2 * rows] + moved(y[:rows], -1, width) + moved(y[2 * rows :], 1, width)


def tap(d, h, w):
    return d * 9 + h * 3 + w


def unpack(src_ref, f_ref, halves):
    for half in range(halves):
        f_ref[half] = src_ref[:, half * LANES : (half + 1) * LANES].astype(F32)


def row_of(f_ref, start, count, stride, halves):
    parts = [f_ref[half, pl.ds(start, count, stride=stride), :] for half in range(halves)]
    whole = parts[0] if halves == 1 else jnp.concatenate(parts, axis=1)
    return whole.astype(BF)


def prep_kernel(C, F, H, W, w2, w3, x, cot, ka, kb, k3f, k3b, vown, cown, xf, cf):
    span = 4 * C
    ka[...] = jnp.zeros(ka.shape, BF)
    kb[...] = jnp.zeros(kb.shape, BF)
    k3f[...] = jnp.zeros(k3f.shape, BF)
    stacks = [w2[dt * 9 : dt * 9 + 9].reshape(9 * C, C) for dt in range(3)]
    eye_c = place(C, C, 0)
    zero_c = jnp.zeros((C, C), BF)
    for d in range(2):
        t_a = sum(dot(stacks[dt], place(C, span, (dt + d) * C)) for dt in range(3)).astype(BF)
        rows = []
        for wt in range(3):
            for ht in range(3):
                three = [w2[tap(2 - dt, 2 - ht, 2 - wt)] for dt in range(3)]
                rows += ([zero_c] + three) if d else (three + [zero_c])
        t_b = dot_nt(eye_c, jnp.concatenate(rows, axis=0)).astype(BF)
        for wt in range(3):
            for h in range(2):
                at = (wt * 4 + d * 2 + h) * C
                for ht in range(3):
                    lane = (h + ht) * span
                    g = ht * 3 + wt
                    ka[at : at + C, lane : lane + span] = t_a[g * C : g * C + C]
                    q = wt * 3 + ht
                    kb[at : at + C, lane : lane + span] = t_b[:, q * span : q * span + span]
    zero_f = jnp.zeros((C, F), BF)
    rows = []
    for wt in range(3):
        for ht in range(3):
            rows += [w3[tap(dt, ht, wt)] for dt in range(3)] + [zero_f]
    t_f = dot_nt(place(F, F, 0), jnp.concatenate(rows, axis=0)).astype(BF)
    for wt in range(3):
        for h in range(2):
            at = (wt * 2 + h) * F
            for ht in range(3):
                lane = (h + ht) * span
                q = wt * 3 + ht
                k3f[at : at + F, lane : lane + span] = t_f[:, q * span : q * span + span]
    wide = 4 * F
    picked = [
        jnp.concatenate([w3[tap(2 - dt, 2 - ht, 2 - wt)] for wt in range(3) for dt in range(3)], axis=0)
        for ht in range(3)
    ]
    for h in range(2):
        t_u = sum(dot(picked[ht], place(F, wide, (ht + h) * F)) for ht in range(3)).astype(BF)
        for wt in range(3):
            at = (wt * 2 + h) * C
            for dt in range(3):
                q = wt * 3 + dt
                k3b[at : at + C, dt * wide : dt * wide + wide] = t_u[q * C : q * C + C]
    halves = W // LANES
    unpack(x, xf, halves)
    for h in range(H):
        for d in range(2):
            vown[(h * 2 + d) * C : (h * 2 + d + 1) * C, :] = row_of(xf, d * H + h, C, 2 * H, halves)
    low = H // 2
    unpack(cot, cf, W // 2 // LANES)
    for h in range(low):
        cown[h * F : h * F + F, :] = row_of(cf, h, F, low, W // 2 // LANES)


def forward_kernel(C, F, H, W, xl, xr, cl, cr, vown, cown, ka, k3b, send_l, send_r, vv, cc, xf, cf, bp):
    halves, low, wide = W // LANES, H // 2, W // 2
    for plane, src in ((0, xl), (3, xr)):
        unpack(src, xf, halves)
        for h in range(H):
            tile = row_of(xf, h, C, H, halves)
            for b in range(low):
                j = h + 1 - 2 * b
                if 0 <= j < 4:
                    at = (j * 4 + plane) * C
                    vv[at : at + C, b * W : b * W + W] = tile
    for h in range(H):
        tile = vown[h * 2 * C : (h + 1) * 2 * C, :]
        for b in range(low):
            j = h + 1 - 2 * b
            if 0 <= j < 4:
                at = (j * 4 + 1) * C
                vv[at : at + 2 * C, b * W : b * W + W] = tile
    vv[: 4 * C, :W] = jnp.zeros((4 * C, W), BF)
    vv[12 * C :, (low - 1) * W :] = jnp.zeros((4 * C, W), BF)
    pairs = low // 2
    for plane, src in ((0, cl), (1, None), (2, cr)):
        if src is not None:
            unpack(src, cf, wide // LANES)
        for h in range(low):
            tile = cown[h * F : h * F + F, :] if src is None else row_of(cf, h, F, low, wide // LANES)
            for b in range(pairs):
                j = h + 1 - 2 * b
                if 0 <= j < 4:
                    at = (plane * 4 + j) * F
                    cc[at : at + F, b * wide : b * wide + wide] = tile
        cc[plane * 4 * F : plane * 4 * F + F, :wide] = jnp.zeros((F, wide), BF)
        cc[(plane * 4 + 3) * F : (plane * 4 + 4) * F, (pairs - 1) * wide :] = jnp.zeros((F, wide), BF)
    y = dot(k3b[...], cc[...])
    bp[...] = taps_sum(y, 2 * C, wide).astype(BF)
    eighth = jnp.where(iota((W, wide), 0) // 2 == iota((W, wide), 1), 0.125, 0.0).astype(BF)
    spread = jnp.where(iota((wide, W), 1) // 2 == iota((wide, W), 0), 0.125, 0.0).astype(BF)
    quarter = low // 2
    for b in range(low):
        y = dot(ka[...], vv[:, b * W : b * W + W])
        before = taps_sum(y, 4 * C, W)
        sigma = jax.nn.sigmoid(before)
        active = (before * sigma).astype(BF)
        sums = dot(active, eighth)
        pooled = (sums[:C] + sums[C : 2 * C] + sums[2 * C : 3 * C] + sums[3 * C :]).astype(BF)
        back = dot(bp[(b % 2) * C : (b % 2) * C + C, (b // 2) * wide : (b // 2) * wide + wide], spread)
        slope = sigma * (1.0 + before * (1.0 - sigma))
        grad = jnp.concatenate([back] * 4, axis=0) * slope
        grad = grad.astype(BF)
        send_l[b * 2 * C : (b + 1) * 2 * C, :] = grad[: 2 * C]
        send_r[b * 2 * C : (b + 1) * 2 * C, :] = grad[2 * C :]
        at, lane = H * C + (b % quarter) * C, (b // quarter) * wide
        send_l[at : at + C, lane : lane + wide] = pooled
        send_r[at : at + C, lane : lane + wide] = pooled


def grads_kernel(C, F, H, W, send_l, send_r, vv, cc, r2, r3, gg, ps):
    low, wide = H // 2, W // 2
    for b in range(low):
        for d, src in ((0, send_l), (1, send_r)):
            tile = src[b * 2 * C : (b + 1) * 2 * C, :]
            up = tile.astype(F32)
            for wt in range(3):
                val = tile if wt == 1 else moved(up, 1 - wt, W).astype(BF)
                at = (wt * 2 + d) * 2 * C
                gg[at : at + 2 * C, b * W : b * W + W] = val
    p2 = dot_nt(gg[...], vv[...])
    span = 4 * C
    for wt in range(3):
        for ht in range(3):
            parts = []
            for d in range(2):
                at = (wt * 4 + d * 2) * C
                parts.append(
                    p2[at : at + C, ht * span : ht * span + span]
                    + p2[at + C : at + 2 * C, (ht + 1) * span : (ht + 2) * span]
                )
            r2[wt * 3 + ht] = parts[0] + pltpu.roll(parts[1], span - C, 1)
    quarter = low // 2
    ps[...] = jnp.zeros(ps.shape, BF)
    for b in range(low // 2):
        for q in range(2):
            h = 2 * b + q
            at, lane = H * C + (h % quarter) * C, (h // quarter) * wide
            tile = send_l[at : at + C, lane : lane + wide]
            up = tile.astype(F32)
            for wt in range(3):
                val = tile if wt == 1 else moved(up, wt - 1, wide).astype(BF)
                to = (q * 4 + wt) * C
                ps[to : to + C, b * wide : b * wide + wide] = val
    p3 = dot_nt(cc[...], ps[...])
    for dt in range(3):
        for ht in range(3):
            first = ((2 - dt) * 4 + 2 - ht) * F
            second = first + F
            r3[dt * 3 + ht] = p3[first : first + F, :span] + p3[second : second + F, span:]


def backward_kernel(C, F, H, W, recv_l, recv_r, send_l, send_r, kb, k3f, gv, ft, gw, pp, zf, ff):
    low, wide = H // 2, W // 2
    quarter = low // 2
    sources = (recv_l, send_l, send_r, recv_r)
    gw[: 4 * C, :W] = jnp.zeros((4 * C, W), BF)
    gw[12 * C :, (low - 1) * W :] = jnp.zeros((4 * C, W), BF)
    for plane, src in enumerate(sources):
        for h in range(H):
            tile = src[h * C : h * C + C, :]
            for b in range(low):
                j = h + 1 - 2 * b
                if 0 <= j < 4:
                    at = (j * 4 + plane) * C
                    gw[at : at + C, b * W : b * W + W] = tile
    for b in range(low):
        y = dot(kb[...], gw[:, b * W : b * W + W])
        out = taps_sum(y, 4 * C, W)
        for d in range(2):
            for q in range(2):
                at = (d * 2 + q) * C
                for half in range(W // LANES):
                    zf[half, pl.ds(d * H + 2 * b + q, C, stride=2 * H), :] = out[
                        at : at + C, half * LANES : (half + 1) * LANES
                    ]
    for half in range(W // LANES):
        gv[:, half * LANES : (half + 1) * LANES] = zf[half].astype(BF)
    pp[...] = jnp.zeros(pp.shape, BF)
    for plane, src in ((0, recv_l), (1, send_l), (2, recv_r)):
        for h in range(low):
            at, lane = H * C + (h % quarter) * C, (h // quarter) * wide
            tile = src[at : at + C, lane : lane + wide]
            for b in range(low // 2):
                j = h + 1 - 2 * b
                if 0 <= j < 4:
                    to = (j * 4 + plane) * C
                    pp[to : to + C, b * wide : b * wide + wide] = tile
    y = dot(k3f[...], pp[...])
    out = taps_sum(y, 2 * F, wide)
    for b in range(low // 2):
        for q in range(2):
            for half in range(wide // LANES):
                lane = b * wide + half * LANES
                ff[half, pl.ds(2 * b + q, F, stride=low), :] = out[q * F : q * F + F, lane : lane + LANES]
    for half in range(wide // LANES):
        ft[:, half * LANES : (half + 1) * LANES] = ff[half].astype(BF)


def call(body, outs, scratch, flops, name, *args):
    moved_bytes = sum(a.size * a.dtype.itemsize for a in args)
    return pl.pallas_call(
        body,
        out_shape=outs,
        in_specs=[VMEM] * len(args),
        out_specs=jax.tree.map(lambda _: VMEM, outs),
        scratch_shapes=scratch,
        cost_estimate=pl.CostEstimate(flops=flops, bytes_accessed=moved_bytes, transcendentals=0),
        name=name,
    )(*args)


def exchange(to_left, to_right, axis):
    count = lax.axis_size(axis)
    from_left = lax.ppermute(to_right, axis, [(i, i + 1) for i in range(count - 1)])
    from_right = lax.ppermute(to_left, axis, [(i + 1, i) for i in range(count - 1)])
    return from_left, from_right


def reduce_both(full, parts, axis):
    count = lax.axis_size(axis)
    if count & (count - 1):
        return lax.psum(full, axis), lax.psum_scatter(parts, axis, scatter_dimension=1, tiled=True)
    g, o, lanes = parts.shape
    each = o // count
    index = lax.axis_index(axis)
    left = parts.reshape(g, count, each, lanes)
    step = 1
    while step < count:
        bit = (index // step) % 2
        split = left.reshape(g, left.shape[1] // 2, 2, each, lanes)
        keep = lax.dynamic_index_in_dim(split, bit, 2, keepdims=False)
        give = lax.dynamic_index_in_dim(split, 1 - bit, 2, keepdims=False)
        mine = full.astype(BF)
        packet = jnp.concatenate([mine.reshape(-1, lanes), give.astype(BF).reshape(-1, lanes)], axis=0)
        got = lax.ppermute(packet, axis, [(i, i ^ step) for i in range(count)])
        rows = full.shape[0] * full.shape[1]
        full = mine.astype(F32) + got[:rows].reshape(full.shape).astype(F32)
        left = keep + got[rows:].reshape(keep.shape).astype(F32)
        step *= 2
    return full, left[:, 0]


def local(volume, weight_two, weight_three, cotangent):
    C, planes, H, W = volume.shape
    F, _, low, wide = cotangent.shape
    assert planes == 2 and 2 * low == H and 2 * wide == W
    sds = jax.ShapeDtypeStruct
    w2 = jnp.transpose(weight_two, (2, 3, 4, 0, 1)).reshape(27, C, C)
    w3 = jnp.transpose(weight_three, (2, 3, 4, 1, 0)).reshape(27, C, F)
    x = volume.reshape(C * 2 * H, W)
    cot = cotangent.reshape(F * low, wide)
    first = volume[:, 0].reshape(C * H, W)
    last = volume[:, 1].reshape(C * H, W)
    xl, xr = exchange(first, last, "gx")
    cl, cr = exchange(cot, cot, "gx")
    halves, low_halves = W // LANES, wide // LANES
    bind = lambda body: functools.partial(body, C, F, H, W)
    ka, kb, k3f, k3b, vown, cown = call(
        bind(prep_kernel),
        (
            sds((12 * C, 16 * C), BF),
            sds((12 * C, 16 * C), BF),
            sds((6 * F, 16 * C), BF),
            sds((6 * C, 12 * F), BF),
            sds((H * 2 * C, W), BF),
            sds((low * F, wide), BF),
        ),
        [pltpu.VMEM((halves, C * 2 * H, LANES), F32), pltpu.VMEM((low_halves, F * low, LANES), F32)],
        400_000_000,
        "prep",
        w2,
        w3,
        x,
        cot,
    )
    send_l, send_r, vv, cc = call(
        bind(forward_kernel),
        (
            sds((H * C + low // 2 * C, W), BF),
            sds((H * C + low // 2 * C, W), BF),
            sds((16 * C, low * W), BF),
            sds((12 * F, low // 2 * wide), BF),
        ),
        [
            pltpu.VMEM((halves, C * H, LANES), F32),
            pltpu.VMEM((low_halves, F * low, LANES), F32),
            pltpu.VMEM((2 * C, low // 2 * wide), BF),
        ],
        1_500_000_000,
        "forward",
        xl,
        xr,
        cl,
        cr,
        vown,
        cown,
        ka,
        k3b,
    )
    recv_l, recv_r = exchange(send_l, send_r, "gx")
    r2, r3 = call(
        bind(grads_kernel),
        (sds((9, C, 4 * C), F32), sds((9, F, 4 * C), F32)),
        [pltpu.VMEM((12 * C, low * W), BF), pltpu.VMEM((8 * C, low // 2 * wide), BF)],
        1_200_000_000,
        "grads",
        send_l,
        send_r,
        vv,
        cc,
    )
    g2, g3 = reduce_both(r2, r3, "gx")
    gv, ft = call(
        bind(backward_kernel),
        (sds((C * 2 * H, W), BF), sds((F * low, wide), BF)),
        [
            pltpu.VMEM((16 * C, low * W), BF),
            pltpu.VMEM((16 * C, low // 2 * wide), BF),
            pltpu.VMEM((halves, C * 2 * H, LANES), F32),
            pltpu.VMEM((low_halves, F * low, LANES), F32),
        ],
        1_200_000_000,
        "backward",
        recv_l,
        recv_r,
        send_l,
        send_r,
        kb,
        k3f,
    )
    g2 = g2.reshape(3, 3, C, 4, C)[:, :, :, :3]
    grad_two = jnp.transpose(g2, (2, 4, 3, 1, 0))
    g3 = g3.reshape(3, 3, g3.shape[1], 4, C)[:, :, :, :3]
    grad_three = jnp.transpose(g3, (2, 4, 0, 1, 3))
    return (
        ft.reshape(F, 1, low, wide),
        grad_three,
        grad_two,
        gv.reshape(C, 2, H, W),
    )


def solution(mesh):
    return jax.shard_map(
        local,
        mesh=mesh,
        in_specs=(
            P(None, ("groups", "gx"), None, None),
            P(),
            P(),
            P(None, ("groups", "gx"), None, None),
        ),
        out_specs=(
            P(None, ("groups", "gx"), None, None),
            P(("groups", "gx"), None, None, None, None),
            P("groups", None, None, None, None),
            P(None, ("groups", "gx"), None, None),
        ),
        check_vma=False,
    )
```

profile of v0, /device:TPU:13, one launch (start us, length us, event | category | flops | bytes accessed | tf_op | source)
XLA Modules:
  0.0 63.1 jit_solution(16206879630452481971)
XLA Ops:
  0.6 1.1 %fusion.3 = (bf16[32,1,16,256]{3,2,1,0:T(8,128)(2,1)S(1)}, bf16[32,1,16,256]{3,2,1,0:T(8,128)(2,1)S(1)}) fusion(bf16[32,2,16,256]{3,2,1,0:T(8,128)(2,1)} %param.4), kind=kLoop, calls=%fused_computation.25 | loop fusion | bytes 1048576 | tf_op jit(solution)/shard_map/slice | solution.py:318
  1.7 3.7 %collective-permute-start = (bf16[512,256]{1,0:T(8,128)(2,1)S(1)}, bf16[512,256]{1,0:T(8,128)(2,1)S(1)}, u32[]{:S(2)}, u32[]{:S(2)}) collective-permute-start(bf16[512,256]{1,0:T(8,128)(2,1)S(1)} %bitcast.66), channel_id=1, source_target_pairs={{0,1},{1,2},{2,3},{3,4},{4,5},{5,6},{6,7},{7,8},{8,9},{9,10},{10,1... | collective-permute-start | bytes 786440 | tf_op jit(solution)/shard_map/ppermute | solution.py:280
  5.4 1.9 %collective-permute-start.1 = (bf16[512,256]{1,0:T(8,128)(2,1)S(1)}, bf16[512,256]{1,0:T(8,128)(2,1)S(1)}, u32[]{:S(2)}, u32[]{:S(2)}) collective-permute-start(bf16[512,256]{1,0:T(8,128)(2,1)S(1)} %bitcast.65), channel_id=1, source_target_pairs={{1,0},{2,1},{3,2},{4,3},{5,4},{6,5},{7,6},{8,7},{9,8},{10,9},{11,1... | collective-permute-start | bytes 786440 | tf_op jit(solution)/shard_map/ppermute | solution.py:281
  7.4 4.5 %collective-permute-start.2 = (bf16[512,128]{1,0:T(8,128)(2,1)}, bf16[512,128]{1,0:T(8,128)(2,1)S(1)}, u32[]{:S(2)}, u32[]{:S(2)}) collective-permute-start(bf16[512,128]{1,0:T(8,128)(2,1)} %bitcast.77), channel_id=1, source_target_pairs={{0,1},{1,2},{2,3},{3,4},{4,5},{5,6},{6,7},{7,8},{8,9},{9,10},{10,1... | collective-permute-start | bytes 393224 | tf_op jit(solution)/shard_map/ppermute | solution.py:280
  11.9 1.9 %collective-permute-start.3 = (bf16[512,128]{1,0:T(8,128)(2,1)}, bf16[512,128]{1,0:T(8,128)(2,1)S(1)}, u32[]{:S(2)}, u32[]{:S(2)}) collective-permute-start(bf16[512,128]{1,0:T(8,128)(2,1)} %bitcast.78), channel_id=1, source_target_pairs={{1,0},{2,1},{3,2},{4,3},{5,4},{6,5},{7,6},{8,7},{9,8},{10,9},{11,1... | collective-permute-start | bytes 393224 | tf_op jit(solution)/shard_map/ppermute | solution.py:281
  13.9 3.6 %prep.1 = (bf16[384,512]{1,0:T(8,128)(2,1)}, bf16[384,512]{1,0:T(8,128)(2,1)}, bf16[384,512]{1,0:T(8,128)(2,1)}, bf16[192,768]{1,0:T(8,128)(2,1)}, bf16[1024,256]{1,0:T(8,128)(2,1)}, /*index=5*/bf16[512,128]{1,0:T(8,128)(2,1)}) custom-call(bf16[27,32,32]{2,1,0:T(8,128)(2,1)} %bitcast.75, bf16[27,32,64]{2,1,0:T(8,128)(2,1)} %bitcast.76, ...), custom_call_target="tpu_custom_call" | custom-call | flops 400000000 | bytes 821248 | tf_op jit(solution)/shard_map/prep/pallas_call | solution.py:267
  17.4 1.9 %collective-permute-done.3.cr = bf16[512,128]{1,0:T(8,128)(2,1)S(1)} collective-permute-done((bf16[512,128]{1,0:T(8,128)(2,1)}, bf16[512,128]{1,0:T(8,128)(2,1)S(1)}, u32[]{:S(2)}, u32[]{:S(2)}) %collective-permute-start.3) | collective-permute-done | bytes 131104 | tf_op jit(solution)/shard_map/ppermute | solution.py:281
  19.3 0.6 %copy-done.8 = bf16[512,128]{1,0:T(8,128)(2,1)} copy-done((bf16[512,128]{1,0:T(8,128)(2,1)}, bf16[512,128]{1,0:T(8,128)(2,1)S(1)}, u32[]{:S(2)}) %copy-start.8) | copy-done | bytes 131096
  20.0 0.1 copy-done.5
  20.2 7.3 %forward.1 = (bf16[640,256]{1,0:T(8,128)(2,1)}, bf16[640,256]{1,0:T(8,128)(2,1)}, bf16[512,2048]{1,0:T(8,128)(2,1)}, bf16[768,512]{1,0:T(8,128)(2,1)}) custom-call(bf16[512,256]{1,0:T(8,128)(2,1)} %copy-done.5, bf16[512,256]{1,0:T(8,128)(2,1)} %copy-done.6, bf16[512,128]{1,0:T(8,128)(2,1)} %copy-done.7, bf16[512,128]{1,0:T(8,128)(2,1)} %copy-done.8, ...), custom_call_target="tpu_custom_call" | custom-call | flops 1500000000 | bytes 2129920 | tf_op jit(solution)/shard_map/forward/pallas_call | solution.py:267
  27.5 3.9 %grads.1 = (f32[9,32,128]{2,1,0:T(8,128)}, f32[9,64,128]{2,1,0:T(8,128)}) custom-call(bf16[640,256]{1,0:T(8,128)(2,1)} %get-tuple-element.23.send_l, bf16[640,256]{1,0:T(8,128)(2,1)} %get-tuple-element.22.send_r, bf16[512,2048]{1,0:T(8,128)(2,1)} %get-tuple-element.27.vv, bf16[768,512]{1,0:T(8,128)(2,1)} %get-tuple-element.28.cc), custom_call_target="tpu_custom_call" | custom-call | flops 1200000000 | bytes 3538944 | tf_op jit(solution)/shard_map/grads/pallas_call | solution.py:267
  31.4 1.0 %convert_element_type.108 = bf16[9,32,128]{2,1,0:T(8,128)(2,1)S(1)} convert(f32[9,32,128]{2,1,0:T(8,128)} %get-tuple-element.30) | non-fusion elementwise | flops 36864 | bytes 221184 | tf_op jit(solution)/shard_map/convert_element_type | solution.py:299
  32.4 0.9 %dynamic-slice_convert_fusion = bf16[9,8,1,4,128]{4,3,2,1,0:T(4,128)(2,1)S(1)} fusion(f32[9,8,2,4,128]{4,3,2,1,0:T(4,128)} %bitcast.69, s32[]{:T(128)S(6)} %select_n.60), kind=kLoop, calls=%fused_computation.10 | loop fusion | bytes 147460 | tf_op jit(solution)/shard_map/convert_element_type | solution.py:300
  33.4 0.1 collective-permute-start.6
  33.5 0.9 %constant_dynamic-slice_fusion.1 = f32[9,8,1,4,128]{4,3,2,1,0:T(4,128)S(1)} fusion(f32[9,8,2,4,128]{4,3,2,1,0:T(4,128)} %bitcast.70, s32[]{:T(128)S(6)} %select_n.59), kind=kLoop, calls=%fused_computation.24 | loop fusion | bytes 294916 | tf_op jit(solution)/shard_map/jit(dynamic_index_in_dim)/dynamic_slice | solution.py:297
  34.5 0.3 collective-permute-done.6
  34.8 0.1 copy_add_fusion
  34.9 0.1 dynamic-slice_convert_fusion.1
  35.2 0.1 constant_dynamic-slice_fusion
  35.3 4.3 %collective-permute-done.7 = bf16[432,128]{1,0:T(8,128)(2,1)S(1)} collective-permute-done((bf16[432,128]{1,0:T(8,128)(2,1)S(1)}, bf16[432,128]{1,0:T(8,128)(2,1)S(1)}, u32[]{:S(2)}, u32[]{:S(2)}) %collective-permute-start.7) | collective-permute-done | bytes 110624 | tf_op jit(solution)/shard_map/ppermute | solution.py:301
  39.8 0.2 collective-permute-start.8
  40.0 4.7 %collective-permute-start.4 = (bf16[640,256]{1,0:T(8,128)(2,1)S(1)}, bf16[640,256]{1,0:T(8,128)(2,1)S(1)}, u32[]{:S(2)}, u32[]{:S(2)}) collective-permute-start(bf16[640,256]{1,0:T(8,128)(2,1)S(1)} %copy-done.2), channel_id=1, source_target_pairs={{0,1},{1,2},{2,3},{3,4},{4,5},{5,6},{6,7},{7,8},{8,9},{9,10},{10,1... | collective-permute-start | bytes 983048 | tf_op jit(solution)/shard_map/ppermute | solution.py:280
  44.7 1.9 %collective-permute-start.5 = (bf16[640,256]{1,0:T(8,128)(2,1)S(1)}, bf16[640,256]{1,0:T(8,128)(2,1)S(1)}, u32[]{:S(2)}, u32[]{:S(2)}) collective-permute-start(bf16[640,256]{1,0:T(8,128)(2,1)S(1)} %copy-done.1), channel_id=1, source_target_pairs={{1,0},{2,1},{3,2},{4,3},{5,4},{6,5},{7,6},{8,7},{9,8},{10,9},{11,1... | collective-permute-start | bytes 983048 | tf_op jit(solution)/shard_map/ppermute | solution.py:281
  46.8 0.8 %collective-permute-start.9 = (bf16[324,128]{1,0:T(8,128)(2,1)S(1)}, bf16[324,128]{1,0:T(8,128)(2,1)S(1)}, u32[]{:S(2)}, u32[]{:S(2)}) collective-permute-start(bf16[324,128]{1,0:T(8,128)(2,1)S(1)} %pad_maximum_fusion.3), channel_id=1, source_target_pairs={{0,8},{1,9},{2,10},{3,11},{4,12},{5,13},{6,14},{7,15},{8,0},{9,1},... | collective-permute-start | bytes 248840 | tf_op jit(solution)/shard_map/ppermute | solution.py:301
  47.7 1.1 %collective-permute-done.4.recv_l = bf16[640,256]{1,0:T(8,128)(2,1)S(1)} collective-permute-done((bf16[640,256]{1,0:T(8,128)(2,1)S(1)}, bf16[640,256]{1,0:T(8,128)(2,1)S(1)}, u32[]{:S(2)}, u32[]{:S(2)}) %collective-permute-start.4) | collective-permute-done | bytes 327712 | tf_op jit(solution)/shard_map/ppermute | solution.py:280
  48.7 7.2 %collective-permute-done.5.recv_r = bf16[640,256]{1,0:T(8,128)(2,1)S(1)} collective-permute-done((bf16[640,256]{1,0:T(8,128)(2,1)S(1)}, bf16[640,256]{1,0:T(8,128)(2,1)S(1)}, u32[]{:S(2)}, u32[]{:S(2)}) %collective-permute-start.5) | collective-permute-done | bytes 327712 | tf_op jit(solution)/shard_map/ppermute | solution.py:281
  55.9 0.7 %copy-done.4 = bf16[640,256]{1,0:T(8,128)(2,1)} copy-done((bf16[640,256]{1,0:T(8,128)(2,1)}, bf16[640,256]{1,0:T(8,128)(2,1)S(1)}, u32[]{:S(2)}) %copy-start.4) | copy-done | bytes 327704
  56.7 4.5 %backward.1 = (bf16[1024,256]{1,0:T(8,128)(2,1)}, bf16[512,128]{1,0:T(8,128)(2,1)}) custom-call(bf16[640,256]{1,0:T(8,128)(2,1)} %copy-done.3, bf16[640,256]{1,0:T(8,128)(2,1)} %copy-done.4, bf16[640,256]{1,0:T(8,128)(2,1)} %get-tuple-element.23.send_l, bf16[640,256]{1,0:T(8,128)(2,1)} %get-tuple-element.22.send_r, bf16[384,512]{1,0:T(8,128)(2,1)} %get-tuple-element.24.kb, ...), custom_call_target="tpu_custom_call" | custom-call | flops 1200000000 | bytes 2097152 | tf_op jit(solution)/shard_map/backward/pallas_call | solution.py:267
  61.2 0.1 reshape_squeeze.11
  61.3 0.6 %copy.25 = f32[4,32,3,3,3]{1,0,4,3,2:T(4,128)} copy(f32[4,32,3,3,3]{1,4,0,3,2:T(4,128)S(1)} %slice_bitcast_fusion) | data formatting | bytes 27648
  62.0 0.3 reshape.114
  62.3 0.8 %copy.30 = f32[3,3,32,3,32]{4,2,0,1,3:T(8,128)} copy(f32[3,3,32,3,32]{4,3,2,1,0:T(4,128)S(1)} %bitcast.50) | data formatting | bytes 221184
  (47 shorter events, 0.5 us)
Async XLA Ops:
  1.7 17.6 %collective-permute-start = (bf16[512,256]{1,0:T(8,128)(2,1)S(1)}, bf16[512,256]{1,0:T(8,128)(2,1)S(1)}, u32[]{:S(2)}, u32[]{:S(2)}) collective-permute-start(bf16[512,256]{1,0:T(8,128)(2,1)S(1)} %bitcast.66), channel_id=1, source_target_pairs={{0,1},{1,2},{2,3},{3,4},{4,5},{5,6},{6,7},{7,8},{8,9},{9,10},{10,1... | collective-permute-start | bytes 786440 | tf_op jit(solution)/shard_map/ppermute | solution.py:280
  5.4 13.9 %collective-permute-start.1 = (bf16[512,256]{1,0:T(8,128)(2,1)S(1)}, bf16[512,256]{1,0:T(8,128)(2,1)S(1)}, u32[]{:S(2)}, u32[]{:S(2)}) collective-permute-start(bf16[512,256]{1,0:T(8,128)(2,1)S(1)} %bitcast.65), channel_id=1, source_target_pairs={{1,0},{2,1},{3,2},{4,3},{5,4},{6,5},{7,6},{8,7},{9,8},{10,9},{11,1... | collective-permute-start | bytes 786440 | tf_op jit(solution)/shard_map/ppermute | solution.py:281
  7.4 10.1 %collective-permute-start.2 = (bf16[512,128]{1,0:T(8,128)(2,1)}, bf16[512,128]{1,0:T(8,128)(2,1)S(1)}, u32[]{:S(2)}, u32[]{:S(2)}) collective-permute-start(bf16[512,128]{1,0:T(8,128)(2,1)} %bitcast.77), channel_id=1, source_target_pairs={{0,1},{1,2},{2,3},{3,4},{4,5},{5,6},{6,7},{7,8},{8,9},{9,10},{10,1... | collective-permute-start | bytes 393224 | tf_op jit(solution)/shard_map/ppermute | solution.py:280
  11.9 7.4 %collective-permute-start.3 = (bf16[512,128]{1,0:T(8,128)(2,1)}, bf16[512,128]{1,0:T(8,128)(2,1)S(1)}, u32[]{:S(2)}, u32[]{:S(2)}) collective-permute-start(bf16[512,128]{1,0:T(8,128)(2,1)} %bitcast.78), channel_id=1, source_target_pairs={{1,0},{2,1},{3,2},{4,3},{5,4},{6,5},{7,6},{8,7},{9,8},{10,9},{11,1... | collective-permute-start | bytes 393224 | tf_op jit(solution)/shard_map/ppermute | solution.py:281
  17.4 1.9 %copy-start.7 = (bf16[512,128]{1,0:T(8,128)(2,1)}, bf16[512,128]{1,0:T(8,128)(2,1)S(1)}, u32[]{:S(2)}) copy-start(bf16[512,128]{1,0:T(8,128)(2,1)S(1)} %collective-permute-done.2.cl) | copy-start | bytes 393220
  19.3 0.7 %copy-start.8 = (bf16[512,128]{1,0:T(8,128)(2,1)}, bf16[512,128]{1,0:T(8,128)(2,1)S(1)}, u32[]{:S(2)}) copy-start(bf16[512,128]{1,0:T(8,128)(2,1)S(1)} %collective-permute-done.3.cr) | copy-start | bytes 393220
  19.3 0.8 %copy-start.5 = (bf16[512,256]{1,0:T(8,128)(2,1)}, bf16[512,256]{1,0:T(8,128)(2,1)S(1)}, u32[]{:S(2)}) copy-start(bf16[512,256]{1,0:T(8,128)(2,1)S(1)} %collective-permute-done.xl) | copy-start | bytes 786436
  19.3 0.8 %copy-start.6 = (bf16[512,256]{1,0:T(8,128)(2,1)}, bf16[512,256]{1,0:T(8,128)(2,1)S(1)}, u32[]{:S(2)}) copy-start(bf16[512,256]{1,0:T(8,128)(2,1)S(1)} %collective-permute-done.1.xr) | copy-start | bytes 786436
  31.4 3.7 %copy-start = (f32[9,32,128]{2,1,0:T(8,128)S(1)}, f32[9,32,128]{2,1,0:T(8,128)}, u32[]{:S(2)}) copy-start(f32[9,32,128]{2,1,0:T(8,128)} %get-tuple-element.30) | copy-start | bytes 442372
  31.4 8.6 %copy-start.2 = (bf16[640,256]{1,0:T(8,128)(2,1)S(1)}, bf16[640,256]{1,0:T(8,128)(2,1)}, u32[]{:S(2)}) copy-start(bf16[640,256]{1,0:T(8,128)(2,1)} %get-tuple-element.22.send_r) | copy-start | bytes 983044
  31.4 13.3 %copy-start.1 = (bf16[640,256]{1,0:T(8,128)(2,1)S(1)}, bf16[640,256]{1,0:T(8,128)(2,1)}, u32[]{:S(2)}) copy-start(bf16[640,256]{1,0:T(8,128)(2,1)} %get-tuple-element.23.send_l) | copy-start | bytes 983044
  33.4 1.4 %collective-permute-start.6 = (bf16[576,128]{1,0:T(8,128)(2,1)S(1)}, bf16[576,128]{1,0:T(8,128)(2,1)S(1)}, u32[]{:S(2)}, u32[]{:S(2)}) collective-permute-start(bf16[576,128]{1,0:T(8,128)(2,1)S(1)} %pad_maximum_fusion), channel_id=1, source_target_pairs={{0,1},{1,0},{2,3},{3,2},{4,5},{5,4},{6,7},{7,6},{8,9},{9,8},{10,11... | collective-permute-start | bytes 442376 | tf_op jit(solution)/shard_map/ppermute | solution.py:301
  35.1 4.5 %collective-permute-start.7 = (bf16[432,128]{1,0:T(8,128)(2,1)S(1)}, bf16[432,128]{1,0:T(8,128)(2,1)S(1)}, u32[]{:S(2)}, u32[]{:S(2)}) collective-permute-start(bf16[432,128]{1,0:T(8,128)(2,1)S(1)} %pad_maximum_fusion.1), channel_id=1, source_target_pairs={{0,2},{1,3},{2,0},{3,1},{4,6},{5,7},{6,4},{7,5},{8,10},{9,11},{10,... | collective-permute-start | bytes 331784 | tf_op jit(solution)/shard_map/ppermute | solution.py:301
  39.8 6.9 %collective-permute-start.8 = (bf16[360,128]{1,0:T(8,128)(2,1)S(1)}, bf16[360,128]{1,0:T(8,128)(2,1)S(1)}, u32[]{:S(2)}, u32[]{:S(2)}) collective-permute-start(bf16[360,128]{1,0:T(8,128)(2,1)S(1)} %pad_maximum_fusion.2), channel_id=1, source_target_pairs={{0,4},{1,5},{2,6},{3,7},{4,0},{5,1},{6,2},{7,3},{8,12},{9,13},{10,... | collective-permute-start | bytes 276488 | tf_op jit(solution)/shard_map/ppermute | solution.py:301
  40.0 8.7 %collective-permute-start.4 = (bf16[640,256]{1,0:T(8,128)(2,1)S(1)}, bf16[640,256]{1,0:T(8,128)(2,1)S(1)}, u32[]{:S(2)}, u32[]{:S(2)}) collective-permute-start(bf16[640,256]{1,0:T(8,128)(2,1)S(1)} %copy-done.2), channel_id=1, source_target_pairs={{0,1},{1,2},{2,3},{3,4},{4,5},{5,6},{6,7},{7,8},{8,9},{9,10},{10,1... | collective-permute-start | bytes 983048 | tf_op jit(solution)/shard_map/ppermute | solution.py:280
  44.7 11.2 %collective-permute-start.5 = (bf16[640,256]{1,0:T(8,128)(2,1)S(1)}, bf16[640,256]{1,0:T(8,128)(2,1)S(1)}, u32[]{:S(2)}, u32[]{:S(2)}) collective-permute-start(bf16[640,256]{1,0:T(8,128)(2,1)S(1)} %copy-done.1), channel_id=1, source_target_pairs={{1,0},{2,1},{3,2},{4,3},{5,4},{6,5},{7,6},{8,7},{9,8},{10,9},{11,1... | collective-permute-start | bytes 983048 | tf_op jit(solution)/shard_map/ppermute | solution.py:281
  46.8 14.3 %collective-permute-start.9 = (bf16[324,128]{1,0:T(8,128)(2,1)S(1)}, bf16[324,128]{1,0:T(8,128)(2,1)S(1)}, u32[]{:S(2)}, u32[]{:S(2)}) collective-permute-start(bf16[324,128]{1,0:T(8,128)(2,1)S(1)} %pad_maximum_fusion.3), channel_id=1, source_target_pairs={{0,8},{1,9},{2,10},{3,11},{4,12},{5,13},{6,14},{7,15},{8,0},{9,1},... | collective-permute-start | bytes 248840 | tf_op jit(solution)/shard_map/ppermute | solution.py:301
  48.7 7.2 %copy-start.3 = (bf16[640,256]{1,0:T(8,128)(2,1)}, bf16[640,256]{1,0:T(8,128)(2,1)S(1)}, u32[]{:S(2)}) copy-start(bf16[640,256]{1,0:T(8,128)(2,1)S(1)} %collective-permute-done.4.recv_l) | copy-start | bytes 983044
  55.9 0.7 %copy-start.4 = (bf16[640,256]{1,0:T(8,128)(2,1)}, bf16[640,256]{1,0:T(8,128)(2,1)S(1)}, u32[]{:S(2)}) copy-start(bf16[640,256]{1,0:T(8,128)(2,1)S(1)} %collective-permute-done.5.recv_r) | copy-start | bytes 983044
where the time goes:
time: 63.5 us; the launch traced here: 63.1 us
  starting transfers between devices  20 us (31%)
  Pallas kernels  19.3 us (30%)
  waiting for transfers between devices  14.8 us (23%)
  local copies, waits for them, and re-layouts  6.66 us (10%)
  other arithmetic  1.29 us (2%)
  between operations  1.07 us (2%)
    pallas_call x4, Pallas kernels, call(): pl.pallas_call(body, out_shape=outs, in_specs=[VMEM] * len(args), out_spe...  19.3 us
    ppermute x3, starting transfers between devices, exchange(): lax.ppermute(to_right, axis, [(i, i + 1) for i in range(count - 1)])  13 us
    ppermute x3, waiting for transfers between devices, exchange(): lax.ppermute(to_left, axis, [(i + 1, i) for i in range(count - 1)])  9.07 us
    ppermute x3, starting transfers between devices, exchange(): lax.ppermute(to_left, axis, [(i + 1, i) for i in range(count - 1)])  5.76 us
    ppermute x4, waiting for transfers between devices, reduce_both(): got = lax.ppermute(packet, axis, [(i, i ^ step) for i in range(count)])  4.68 us
    unnamed x21, local copies, waits for them, and re-layouts  3.03 us
  transfers between devices with their start and end apart: 10, of which 5 were waited for; matrix products, arithmetic and copies ran while one was open for 2% of the time, Pallas kernels for 13%

commit v1 on v0

--- a/solution.py
+++ b/solution.py
@@ -50,9 +50,9 @@
         f_ref[half] = src_ref[:, half * LANES : (half + 1) * LANES].astype(F32)
 
 
-def row_of(f_ref, start, count, stride, halves):
-    parts = [f_ref[half, pl.ds(start, count, stride=stride), :] for half in range(halves)]
-    whole = parts[0] if halves == 1 else jnp.concatenate(parts, axis=1)
+def row_of(f_ref, start, count, stride, first, last):
+    parts = [f_ref[half, pl.ds(start, count, stride=stride), :] for half in range(first, last)]
+    whole = parts[0] if len(parts) == 1 else jnp.concatenate(parts, axis=1)
     return whole.astype(BF)
 
 
@@ -110,24 +110,40 @@
     unpack(x, xf, halves)
     for h in range(H):
         for d in range(2):
-            vown[(h * 2 + d) * C : (h * 2 + d + 1) * C, :] = row_of(xf, d * H + h, C, 2 * H, halves)
+            vown[(h * 2 + d) * C : (h * 2 + d + 1) * C, :] = row_of(xf, d * H + h, C, 2 * H, 0, halves)
     low = H // 2
     unpack(cot, cf, W // 2 // LANES)
     for h in range(low):
-        cown[h * F : h * F + F, :] = row_of(cf, h, F, low, W // 2 // LANES)
-
-
-def forward_kernel(C, F, H, W, xl, xr, cl, cr, vown, cown, ka, k3b, send_l, send_r, vv, cc, xf, cf, bp):
+        cown[h * F : h * F + F, :] = row_of(cf, h, F, low, 0, W // 2 // LANES)
+
+
+def parity():
+    return lax.axis_index("gx") % 2
+
+
+def forward_kernel(C, F, H, W, a1, a2, vown, cown, ka, k3b, g, p1, p2, vv, cc, xf, bp):
     halves, low, wide = W // LANES, H // 2, W // 2
-    for plane, src in ((0, xl), (3, xr)):
-        unpack(src, xf, halves)
+    total = halves + wide // LANES
+    odd = parity()
+    pairs = low // 2
+    for src, flip in ((a1, odd), (a2, 1 - odd)):
+        unpack(src, xf, total)
+        plane = 3 - 3 * flip
         for h in range(H):
-            tile = row_of(xf, h, C, H, halves)
+            tile = row_of(xf, h, C, H, 0, halves)
             for b in range(low):
                 j = h + 1 - 2 * b
                 if 0 <= j < 4:
-                    at = (j * 4 + plane) * C
-                    vv[at : at + C, b * W : b * W + W] = tile
+                    at = pl.multiple_of((j * 4 + plane) * C, C)
+                    vv[pl.ds(at, C), b * W : b * W + W] = tile
+        plane = 2 - 2 * flip
+        for h in range(low):
+            tile = row_of(xf, h, F, low, halves, total)
+            for b in range(pairs):
+                j = h + 1 - 2 * b
+                if 0 <= j < 4:
+                    at = pl.multiple_of((plane * 4 + j) * F, F)
+                    cc[pl.ds(at, F), b * wide : b * wide + wide] = tile
     for h in range(H):
         tile = vown[h * 2 * C : (h + 1) * 2 * C, :]
         for b in range(low):
@@ -137,17 +153,13 @@
                 vv[at : at + 2 * C, b * W : b * W + W] = tile
     vv[: 4 * C, :W] = jnp.zeros((4 * C, W), BF)
     vv[12 * C :, (low - 1) * W :] = jnp.zeros((4 * C, W), BF)
-    pairs = low // 2
-    for plane, src in ((0, cl), (1, None), (2, cr)):
-        if src is not None:
-            unpack(src, cf, wide // LANES)
-        for h in range(low):
-            tile = cown[h * F : h * F + F, :] if src is None else row_of(cf, h, F, low, wide // LANES)
-            for b in range(pairs):
-                j = h + 1 - 2 * b
-                if 0 <= j < 4:
-                    at = (plane * 4 + j) * F
-                    cc[at : at + F, b * wide : b * wide + wide] = tile
+    for h in range(low):
+        tile = cown[h * F : h * F + F, :]
+        for b in range(pairs):
+            j = h + 1 - 2 * b
+            if 0 <= j < 4:
+                cc[(4 + j) * F : (5 + j) * F, b * wide : b * wide + wide] = tile
+    for plane in range(3):
         cc[plane * 4 * F : plane * 4 * F + F, :wide] = jnp.zeros((F, wide), BF)
         cc[(plane * 4 + 3) * F : (plane * 4 + 4) * F, (pairs - 1) * wide :] = jnp.zeros((F, wide), BF)
     y = dot(k3b[...], cc[...])
@@ -166,18 +178,19 @@
         slope = sigma * (1.0 + before * (1.0 - sigma))
         grad = jnp.concatenate([back] * 4, axis=0) * slope
         grad = grad.astype(BF)
-        send_l[b * 2 * C : (b + 1) * 2 * C, :] = grad[: 2 * C]
-        send_r[b * 2 * C : (b + 1) * 2 * C, :] = grad[2 * C :]
         at, lane = H * C + (b % quarter) * C, (b // quarter) * wide
-        send_l[at : at + C, lane : lane + wide] = pooled
-        send_r[at : at + C, lane : lane + wide] = pooled
-
-
-def grads_kernel(C, F, H, W, send_l, send_r, vv, cc, r2, r3, gg, ps):
+        for d in range(2):
+            g[d, b * 2 * C : (b + 1) * 2 * C, :] = grad[d * 2 * C : (d + 1) * 2 * C]
+            g[d, at : at + C, lane : lane + wide] = pooled
+    p1[...] = g[1 - odd]
+    p2[...] = g[odd]
+
+
+def grads_kernel(C, F, H, W, count, g, vv, cc, packet, keep, gg, ps, r3):
     low, wide = H // 2, W // 2
     for b in range(low):
-        for d, src in ((0, send_l), (1, send_r)):
-            tile = src[b * 2 * C : (b + 1) * 2 * C, :]
+        for d in range(2):
+            tile = g[d, b * 2 * C : (b + 1) * 2 * C, :]
             up = tile.astype(F32)
             for wt in range(3):
                 val = tile if wt == 1 else moved(up, 1 - wt, W).astype(BF)
@@ -194,41 +207,60 @@
                     p2[at : at + C, ht * span : ht * span + span]
                     + p2[at + C : at + 2 * C, (ht + 1) * span : (ht + 2) * span]
                 )
-            r2[wt * 3 + ht] = parts[0] + pltpu.roll(parts[1], span - C, 1)
+            to = (wt * 3 + ht) * C
+            packet[to : to + C, :] = (parts[0] + pltpu.roll(parts[1], span - C, 1)).astype(BF)
     quarter = low // 2
     ps[...] = jnp.zeros(ps.shape, BF)
     for b in range(low // 2):
         for q in range(2):
             h = 2 * b + q
             at, lane = H * C + (h % quarter) * C, (h // quarter) * wide
-            tile = send_l[at : at + C, lane : lane + wide]
+            tile = g[0, at : at + C, lane : lane + wide]
             up = tile.astype(F32)
             for wt in range(3):
                 val = tile if wt == 1 else moved(up, wt - 1, wide).astype(BF)
                 to = (q * 4 + wt) * C
                 ps[to : to + C, b * wide : b * wide + wide] = val
     p3 = dot_nt(cc[...], ps[...])
+    tiles = []
     for dt in range(3):
         for ht in range(3):
             first = ((2 - dt) * 4 + 2 - ht) * F
             second = first + F
-            r3[dt * 3 + ht] = p3[first : first + F, :span] + p3[second : second + F, span:]
-
-
-def backward_kernel(C, F, H, W, recv_l, recv_r, send_l, send_r, kb, k3f, gv, ft, gw, pp, zf, ff):
+            tiles.append(p3[first : first + F, :span] + p3[second : second + F, span:])
+    each = F // count
+    row, col = iota((F, F), 0), iota((F, F), 1)
+    chunk, index, step = row // each, jnp.zeros((F, F), jnp.int32), 1
+    while step < count:
+        index = index * 2 + chunk % 2
+        chunk, step = chunk // 2, step * 2
+    order = (col == index * each + row % each).astype(F32).astype(BF)
+    r3[...] = dot(order, jnp.concatenate(tiles, axis=1).astype(BF))
+    half = F // 2
+    odd = parity()
+    for q in range(9):
+        to = 9 * C + q * half
+        lanes = slice(q * span, q * span + span)
+        packet[to : to + half, :] = r3[pl.ds(pl.multiple_of((1 - odd) * half, half), half), lanes].astype(BF)
+        keep[q] = r3[pl.ds(pl.multiple_of(odd * half, half), half), lanes]
+
+
+def backward_kernel(C, F, H, W, b1, b2, g, kb, k3f, gv, ft, gw, pp, zf, ff):
     low, wide = H // 2, W // 2
     quarter = low // 2
-    sources = (recv_l, send_l, send_r, recv_r)
+    odd = parity()
+    near, far = 3 - 3 * odd, 3 * odd
+    sources = ((near, b1), (far, b2), (1, g.at[0]), (2, g.at[1]))
     gw[: 4 * C, :W] = jnp.zeros((4 * C, W), BF)
     gw[12 * C :, (low - 1) * W :] = jnp.zeros((4 * C, W), BF)
-    for plane, src in enumerate(sources):
+    for plane, src in sources:
         for h in range(H):
             tile = src[h * C : h * C + C, :]
             for b in range(low):
                 j = h + 1 - 2 * b
                 if 0 <= j < 4:
-                    at = (j * 4 + plane) * C
-                    gw[at : at + C, b * W : b * W + W] = tile
+                    at = pl.multiple_of((j * 4 + plane) * C, C)
+                    gw[pl.ds(at, C), b * W : b * W + W] = tile
     for b in range(low):
         y = dot(kb[...], gw[:, b * W : b * W + W])
         out = taps_sum(y, 4 * C, W)
@@ -242,15 +274,16 @@
     for half in range(W // LANES):
         gv[:, half * LANES : (half + 1) * LANES] = zf[half].astype(BF)
     pp[...] = jnp.zeros(pp.shape, BF)
-    for plane, src in ((0, recv_l), (1, send_l), (2, recv_r)):
+    near, far = 2 - 2 * odd, 2 * odd
+    for plane, src in ((near, b1), (far, b2), (1, g.at[0])):
         for h in range(low):
             at, lane = H * C + (h % quarter) * C, (h // quarter) * wide
             tile = src[at : at + C, lane : lane + wide]
             for b in range(low // 2):
                 j = h + 1 - 2 * b
                 if 0 <= j < 4:
-                    to = (j * 4 + plane) * C
-                    pp[to : to + C, b * wide : b * wide + wide] = tile
+                    to = pl.multiple_of((j * 4 + plane) * C, C)
+                    pp[pl.ds(to, C), b * wide : b * wide + wide] = tile
     y = dot(k3f[...], pp[...])
     out = taps_sum(y, 2 * F, wide)
     for b in range(low // 2):
@@ -271,56 +304,58 @@
         out_specs=jax.tree.map(lambda _: VMEM, outs),
         scratch_shapes=scratch,
         cost_estimate=pl.CostEstimate(flops=flops, bytes_accessed=moved_bytes, transcendentals=0),
+        compiler_params=pltpu.CompilerParams(vmem_limit_bytes=24 * 2**20),
         name=name,
     )(*args)
 
 
-def exchange(to_left, to_right, axis):
+def swap(near, far, axis):
     count = lax.axis_size(axis)
-    from_left = lax.ppermute(to_right, axis, [(i, i + 1) for i in range(count - 1)])
-    from_right = lax.ppermute(to_left, axis, [(i + 1, i) for i in range(count - 1)])
-    return from_left, from_right
-
-
-def reduce_both(full, parts, axis):
+    pairs = [(i, i + 1) for i in range(1, count - 1, 2)]
+    got_far = lax.ppermute(far, axis, pairs + [(b, a) for a, b in pairs])
+    pairs = [(i, i + 1) for i in range(0, count - 1, 2)]
+    got_near = lax.ppermute(near, axis, pairs + [(b, a) for a, b in pairs])
+    return got_near, got_far
+
+
+def reduce_both(packet, keep, rows, axis):
     count = lax.axis_size(axis)
-    if count & (count - 1):
-        return lax.psum(full, axis), lax.psum_scatter(parts, axis, scatter_dimension=1, tiled=True)
-    g, o, lanes = parts.shape
-    each = o // count
     index = lax.axis_index(axis)
-    left = parts.reshape(g, count, each, lanes)
     step = 1
+    full = packet[:rows]
     while step < count:
-        bit = (index // step) % 2
-        split = left.reshape(g, left.shape[1] // 2, 2, each, lanes)
-        keep = lax.dynamic_index_in_dim(split, bit, 2, keepdims=False)
-        give = lax.dynamic_index_in_dim(split, 1 - bit, 2, keepdims=False)
-        mine = full.astype(BF)
-        packet = jnp.concatenate([mine.reshape(-1, lanes), give.astype(BF).reshape(-1, lanes)], axis=0)
         got = lax.ppermute(packet, axis, [(i, i ^ step) for i in range(count)])
-        rows = full.shape[0] * full.shape[1]
-        full = mine.astype(F32) + got[:rows].reshape(full.shape).astype(F32)
-        left = keep + got[rows:].reshape(keep.shape).astype(F32)
+        full = full.astype(F32) + got[:rows].astype(F32)
+        keep = keep + got[rows:].reshape(keep.shape).astype(F32)
         step *= 2
-    return full, left[:, 0]
+        if step < count:
+            full = full.astype(BF)
+            half = keep.shape[1] // 2
+            bit = (index // step) % 2
+            give = lax.dynamic_slice_in_dim(keep, (1 - bit) * half, half, 1)
+            keep = lax.dynamic_slice_in_dim(keep, bit * half, half, 1)
+            packet = jnp.concatenate([full, give.astype(BF).reshape(-1, full.shape[1])], axis=0)
+    return full, keep
 
 
 def local(volume, weight_two, weight_three, cotangent):
     C, planes, H, W = volume.shape
     F, _, low, wide = cotangent.shape
+    count = lax.axis_size("gx")
     assert planes == 2 and 2 * low == H and 2 * wide == W
+    assert count & (count - 1) == 0 and F % count == 0 and C * H == F * low
     sds = jax.ShapeDtypeStruct
+    odd = lax.axis_index("gx") % 2
     w2 = jnp.transpose(weight_two, (2, 3, 4, 0, 1)).reshape(27, C, C)
     w3 = jnp.transpose(weight_three, (2, 3, 4, 1, 0)).reshape(27, C, F)
     x = volume.reshape(C * 2 * H, W)
     cot = cotangent.reshape(F * low, wide)
-    first = volume[:, 0].reshape(C * H, W)
-    last = volume[:, 1].reshape(C * H, W)
-    xl, xr = exchange(first, last, "gx")
-    cl, cr = exchange(cot, cot, "gx")
+    near = lax.dynamic_index_in_dim(volume, 1 - odd, 1, keepdims=False).reshape(C * H, W)
+    far = lax.dynamic_index_in_dim(volume, odd, 1, keepdims=False).reshape(C * H, W)
+    with jax.named_scope("halo_a"):
+        a1, a2 = swap(jnp.concatenate([near, cot], axis=1), jnp.concatenate([far, cot], axis=1), "gx")
     halves, low_halves = W // LANES, wide // LANES
-    bind = lambda body: functools.partial(body, C, F, H, W)
+    bind = lambda body, *more: functools.partial(body, C, F, H, W, *more)
     ka, kb, k3f, k3b, vown, cown = call(
         bind(prep_kernel),
         (
@@ -339,43 +374,46 @@
         x,
         cot,
     )
-    send_l, send_r, vv, cc = call(
+    rows = H * C + low // 2 * C
+    g, p1, p2, vv, cc = call(
         bind(forward_kernel),
         (
-            sds((H * C + low // 2 * C, W), BF),
-            sds((H * C + low // 2 * C, W), BF),
+            sds((2, rows, W), BF),
+            sds((rows, W), BF),
+            sds((rows, W), BF),
             sds((16 * C, low * W), BF),
             sds((12 * F, low // 2 * wide), BF),
         ),
         [
-            pltpu.VMEM((halves, C * H, LANES), F32),
-            pltpu.VMEM((low_halves, F * low, LANES), F32),
+            pltpu.VMEM((halves + low_halves, C * H, LANES), F32),
             pltpu.VMEM((2 * C, low // 2 * wide), BF),
         ],
         1_500_000_000,
         "forward",
-        xl,
-        xr,
-        cl,
-        cr,
+        a1,
+        a2,
         vown,
         cown,
         ka,
         k3b,
     )
-    recv_l, recv_r = exchange(send_l, send_r, "gx")
-    r2, r3 = call(
-        bind(grads_kernel),
-        (sds((9, C, 4 * C), F32), sds((9, F, 4 * C), F32)),
-        [pltpu.VMEM((12 * C, low * W), BF), pltpu.VMEM((8 * C, low // 2 * wide), BF)],
+    with jax.named_scope("halo_b"):
+        b1, b2 = swap(p1, p2, "gx")
+    packet, keep = call(
+        bind(grads_kernel, count),
+        (sds((9 * C + 9 * F // 2, 4 * C), BF), sds((9, F // 2, 4 * C), F32)),
+        [
+            pltpu.VMEM((12 * C, low * W), BF),
+            pltpu.VMEM((8 * C, low // 2 * wide), BF),
+            pltpu.VMEM((F, 36 * C), F32),
+        ],
         1_200_000_000,
         "grads",
-        send_l,
-        send_r,
+        g,
         vv,
         cc,
     )
-    g2, g3 = reduce_both(r2, r3, "gx")
+    g2, g3 = reduce_both(packet, keep, 9 * C, "gx")
     gv, ft = call(
         bind(backward_kernel),
         (sds((C * 2 * H, W), BF), sds((F * low, wide), BF)),
@@ -387,10 +425,9 @@
         ],
         1_200_000_000,
         "backward",
-        recv_l,
-        recv_r,
-        send_l,
-        send_r,
+        b1,
+        b2,
+        g,
         kb,
         k3f,
     )

time: 63.5 us -> 48.6 us (0.77)
  the two profiles are of different devices: /device:TPU:13 before, /device:TPU:19 now
where the time goes in v1:
time: 48.6 us; the launch traced here: 48.4 us
  waiting for transfers between devices  22.6 us (47%)
  starting transfers between devices  10.3 us (21%)
  Pallas kernels  10.3 us (21%)
  local copies, waits for them, and re-layouts  3.11 us (6%)
  other arithmetic  1.15 us (2%)
  between operations  0.94 us (2%)
    ppermute x2, waiting for transfers between devices, swap(): got_far = lax.ppermute(far, axis, pairs + [(b, a) for a, b in pairs])  17.7 us
    pallas_call x4, Pallas kernels, call(): pl.pallas_call(body, out_shape=outs, in_specs=[VMEM] * len(args), out_spe...  10.3 us
    ppermute x2, starting transfers between devices, swap(): got_far = lax.ppermute(far, axis, pairs + [(b, a) for a, b in pairs])  4.95 us
    ppermute x4, waiting for transfers between devices, reduce_both(): got = lax.ppermute(packet, axis, [(i, i ^ step) for i in range(count)])  4.89 us
    ppermute x4, starting transfers between devices, reduce_both(): got = lax.ppermute(packet, axis, [(i, i ^ step) for i in range(count)])  3.31 us
    ppermute x2, starting transfers between devices, swap(): got_near = lax.ppermute(near, axis, pairs + [(b, a) for a, b in pairs])  2.02 us
    unnamed x10, local copies, waits for them, and re-layouts  1.47 us
    dynamic_slice x1, local copies, waits for them, and re-layouts, local(): lax.dynamic_index_in_dim(volume, odd, 1, keepdims=False).reshape(C * H, W)  1.16 us
  transfers between devices with their start and end apart: 8, of which 4 were waited for; matrix products, arithmetic and copies ran while one was open for 0% of the time, Pallas kernels for 9%

profile of v1, /device:TPU:19, one launch (start us, length us, event | category | flops | bytes accessed | tf_op | source)
XLA Modules:
  0.0 48.4 jit_solution(14357301346684159887)
XLA Ops:
  0.6 0.0 copy-start
  0.6 0.0 copy-start.1
  0.7 1.2 %constant_dynamic-slice_fusion = (bf16[32,1,16,256]{3,2,1,0:T(8,128)(2,1)S(1)}, bf16[32,1,16,256]{3,2,1,0:T(8,128)(2,1)S(1)}) fusion(bf16[32,2,16,256]{3,2,1,0:T(8,128)(2,1)} %param.4, s32[]{:T(128)S(6)} %select_n.56, s32[]{:T(128)S(6)} %select_n.55), kind=kLoop, calls=%fused_computation.21 | loop fusion | bytes 1048584 | tf_op jit(solution)/shard_map/jit(dynamic_index_in_dim)/dynamic_slice | solution.py:354
  1.9 1.0 %pad_maximum_fusion = (bf16[512,384]{1,0:T(8,128)(2,1)S(1)}, bf16[512,384]{1,0:T(8,128)(2,1)S(1)}) fusion(bf16[512,128]{1,0:T(8,128)(2,1)} %bitcast.35, bf16[512,256]{1,0:T(8,128)(2,1)S(1)} %bitcast.40, bf16[512,256]{1,0:T(8,128)(2,1)S(1)} %bitcast.41), kind=kLoop, calls=%fused_computation | loop fusion | flops 1376256 | bytes 1441792 | tf_op jit(solution)/shard_map/halo_a/concatenate | solution.py:356
  2.8 0.7 %collective-permute-start = (bf16[512,384]{1,0:T(8,128)(2,1)S(1)}, bf16[512,384]{1,0:T(8,128)(2,1)S(1)}, u32[]{:S(2)}, u32[]{:S(2)}) collective-permute-start(bf16[512,384]{1,0:T(8,128)(2,1)S(1)} %get-tuple-element.41), channel_id=1, source_target_pairs={{0,1},{2,3},{4,5},{6,7},{8,9},{10,11},{12,13},{14,15},{1,0},{3,2},... | collective-permute-start | bytes 1179656 | tf_op jit(solution)/shard_map/halo_a/ppermute | solution.py:317
  3.6 3.0 %collective-permute-start.1 = (bf16[512,384]{1,0:T(8,128)(2,1)S(1)}, bf16[512,384]{1,0:T(8,128)(2,1)S(1)}, u32[]{:S(2)}, u32[]{:S(2)}) collective-permute-start(bf16[512,384]{1,0:T(8,128)(2,1)S(1)} %get-tuple-element.40), channel_id=1, source_target_pairs={{1,2},{3,4},{5,6},{7,8},{9,10},{11,12},{13,14},{2,1},{4,3},{6,5},{... | collective-permute-start | bytes 1179656 | tf_op jit(solution)/shard_map/halo_a/ppermute | solution.py:315
  6.6 0.0 copy-done
  6.6 0.0 copy-done.1
  6.6 0.0 copy-done.2
  6.7 0.0 copy-done.3
  6.7 1.4 %prep.1 = (bf16[384,512]{1,0:T(8,128)(2,1)S(1)}, bf16[384,512]{1,0:T(8,128)(2,1)S(1)}, bf16[384,512]{1,0:T(8,128)(2,1)S(1)}, bf16[192,768]{1,0:T(8,128)(2,1)S(1)...) custom-call(bf16[27,32,32]{2,1,0:T(8,128)(2,1)S(1)} %bitcast.37, bf16[27,32,64]{2,1,0:T(8,128)(2,1)S(1)} %bitcast.38, ...), custom_call_target="tpu_custom_call" | custom-call | flops 400000000 | bytes 821248 | tf_op jit(solution)/shard_map/prep/pallas_call | solution.py:300
  8.1 0.0 collective-permute-done.a1
  8.1 8.8 %collective-permute-done.1.a2 = bf16[512,384]{1,0:T(8,128)(2,1)S(1)} collective-permute-done((bf16[512,384]{1,0:T(8,128)(2,1)S(1)}, bf16[512,384]{1,0:T(8,128)(2,1)S(1)}, u32[]{:S(2)}, u32[]{:S(2)}) %collective-permute-start.1) | collective-permute-done | bytes 393248 | tf_op jit(solution)/shard_map/halo_a/ppermute | solution.py:315
  16.9 4.4 %forward.1 = (bf16[2,640,256]{2,1,0:T(8,128)(2,1)S(1)}, bf16[640,256]{1,0:T(8,128)(2,1)S(1)}, bf16[640,256]{1,0:T(8,128)(2,1)S(1)}, bf16[512,2048]{1,0:T(8,128)(2,1)S(1)}, bf16[768,512]{1,0:T(8,128)(2,1)S(1)}) custom-call(bf16[512,384]{1,0:T(8,128)(2,1)S(1)} %collective-permute-done.a1, bf16[512,384]{1,0:T(8,128)(2,1)S(1)} %collective-permute-done.1.a2, ...), custom_call_target="tpu_custom_call" | custom-call | flops 1500000000 | bytes 2129920 | tf_op jit(solution)/shard_map/forward/pallas_call | solution.py:300
  21.3 1.5 %grads.1 = (bf16[576,128]{1,0:T(8,128)(2,1)S(1)}, f32[9,32,128]{2,1,0:T(8,128)S(1)}) custom-call(bf16[2,640,256]{2,1,0:T(8,128)(2,1)S(1)} %get-tuple-element.25.g, bf16[512,2048]{1,0:T(8,128)(2,1)S(1)} %get-tuple-element.29.vv, bf16[768,512]{1,0:T(8,128)(2,1)S(1)} %get-tuple-element.30.cc), custom_call_target="tpu_custom_call" | custom-call | flops 1200000000 | bytes 3538944 | tf_op jit(solution)/shard_map/grads/pallas_call | solution.py:300
  22.7 0.1 collective-permute-start.4
  22.9 1.3 %collective-permute-done.4 = bf16[576,128]{1,0:T(8,128)(2,1)S(1)} collective-permute-done((bf16[576,128]{1,0:T(8,128)(2,1)S(1)}, bf16[576,128]{1,0:T(8,128)(2,1)S(1)}, u32[]{:S(2)}, u32[]{:S(2)}) %collective-permute-start.4) | collective-permute-done | bytes 147488 | tf_op jit(solution)/shard_map/ppermute | solution.py:327
  24.3 1.0 %collective-permute-start.5 = (bf16[432,128]{1,0:T(8,128)(2,1)S(1)}, bf16[432,128]{1,0:T(8,128)(2,1)S(1)}, u32[]{:S(2)}, u32[]{:S(2)}) collective-permute-start(bf16[432,128]{1,0:T(8,128)(2,1)S(1)} %pad_maximum_fusion.2), channel_id=1, source_target_pairs={{0,2},{1,3},{2,0},{3,1},{4,6},{5,7},{6,4},{7,5},{8,10},{9,11},{10,... | collective-permute-start | bytes 331784 | tf_op jit(solution)/shard_map/ppermute | solution.py:327
  25.3 3.6 %collective-permute-done.5 = bf16[432,128]{1,0:T(8,128)(2,1)S(1)} collective-permute-done((bf16[432,128]{1,0:T(8,128)(2,1)S(1)}, bf16[432,128]{1,0:T(8,128)(2,1)S(1)}, u32[]{:S(2)}, u32[]{:S(2)}) %collective-permute-start.5) | collective-permute-done | bytes 110624 | tf_op jit(solution)/shard_map/ppermute | solution.py:327
  28.9 1.4 %collective-permute-start.6 = (bf16[360,128]{1,0:T(8,128)(2,1)S(1)}, bf16[360,128]{1,0:T(8,128)(2,1)S(1)}, u32[]{:S(2)}, u32[]{:S(2)}) collective-permute-start(bf16[360,128]{1,0:T(8,128)(2,1)S(1)} %pad_maximum_fusion.3), channel_id=1, source_target_pairs={{0,4},{1,5},{2,6},{3,7},{4,0},{5,1},{6,2},{7,3},{8,12},{9,13},{10,... | collective-permute-start | bytes 276488 | tf_op jit(solution)/shard_map/ppermute | solution.py:327
  30.3 1.3 %collective-permute-start.2 = (bf16[640,256]{1,0:T(8,128)(2,1)S(1)}, bf16[640,256]{1,0:T(8,128)(2,1)S(1)}, u32[]{:S(2)}, u32[]{:S(2)}) collective-permute-start(bf16[640,256]{1,0:T(8,128)(2,1)S(1)} %get-tuple-element.23), channel_id=1, source_target_pairs={{0,1},{2,3},{4,5},{6,7},{8,9},{10,11},{12,13},{14,15},{1,0},{3,2},... | collective-permute-start | bytes 983048 | tf_op jit(solution)/shard_map/halo_b/ppermute | solution.py:317
  31.6 1.9 %collective-permute-start.3 = (bf16[640,256]{1,0:T(8,128)(2,1)S(1)}, bf16[640,256]{1,0:T(8,128)(2,1)S(1)}, u32[]{:S(2)}, u32[]{:S(2)}) collective-permute-start(bf16[640,256]{1,0:T(8,128)(2,1)S(1)} %get-tuple-element.24), channel_id=1, source_target_pairs={{1,2},{3,4},{5,6},{7,8},{9,10},{11,12},{13,14},{2,1},{4,3},{6,5},{... | collective-permute-start | bytes 983048 | tf_op jit(solution)/shard_map/halo_b/ppermute | solution.py:315
  33.5 0.0 collective-permute-done.6
  33.6 0.9 %collective-permute-start.7 = (bf16[324,128]{1,0:T(8,128)(2,1)S(1)}, bf16[324,128]{1,0:T(8,128)(2,1)S(1)}, u32[]{:S(2)}, u32[]{:S(2)}) collective-permute-start(bf16[324,128]{1,0:T(8,128)(2,1)S(1)} %pad_maximum_fusion.4), channel_id=1, source_target_pairs={{0,8},{1,9},{2,10},{3,11},{4,12},{5,13},{6,14},{7,15},{8,0},{9,1},... | collective-permute-start | bytes 248840 | tf_op jit(solution)/shard_map/ppermute | solution.py:327
  34.5 0.0 collective-permute-done.2.b1
  34.5 8.9 %collective-permute-done.3.b2 = bf16[640,256]{1,0:T(8,128)(2,1)S(1)} collective-permute-done((bf16[640,256]{1,0:T(8,128)(2,1)S(1)}, bf16[640,256]{1,0:T(8,128)(2,1)S(1)}, u32[]{:S(2)}, u32[]{:S(2)}) %collective-permute-start.3) | collective-permute-done | bytes 327712 | tf_op jit(solution)/shard_map/halo_b/ppermute | solution.py:315
  43.4 3.0 %backward.1 = (bf16[1024,256]{1,0:T(8,128)(2,1)}, bf16[512,128]{1,0:T(8,128)(2,1)}) custom-call(bf16[640,256]{1,0:T(8,128)(2,1)S(1)} %collective-permute-done.2.b1, bf16[640,256]{1,0:T(8,128)(2,1)S(1)} %collective-permute-done.3.b2, bf16[2,640,256]{2,1,0:T(8,128)(2,1)S(1)} %get-tuple-element.25.g, bf16[384,512]{1,0:T(8,128)(2,1)S(1)} %get-tuple-element.26.kb, ...), custom_call_target="tpu_custom_call" | custom-call | flops 1200000000 | bytes 2097152 | tf_op jit(solution)/shard_map/backward/pallas_call | solution.py:300
  46.5 0.0 collective-permute-done.7
  46.5 0.3 reshape.72
  46.8 0.8 %copy.15 = f32[3,3,32,3,32]{4,2,0,1,3:T(8,128)} copy(f32[3,3,32,3,32]{4,3,2,1,0:T(4,128)S(1)} %bitcast.39) | data formatting | bytes 221184
  47.7 0.1 reshape.71
  47.8 0.6 %copy.16 = f32[3,3,4,3,32]{4,2,3,1,0:T(4,128)} copy(f32[3,3,4,3,32]{4,3,2,1,0:T(4,128)S(1)} %bitcast.43) | data formatting | bytes 27648
  (21 shorter events, 0.3 us)
Async XLA Ops:
  0.6 6.0 %copy-start = (bf16[32,2,16,256]{3,2,1,0:T(8,128)(2,1)S(1)}, bf16[32,2,16,256]{3,2,1,0:T(8,128)(2,1)}, u32[]{:S(2)}) copy-start(bf16[32,2,16,256]{3,2,1,0:T(8,128)(2,1)} %param.4) | copy-start | bytes 1572868
  0.6 6.0 %copy-start.1 = (bf16[64,1,8,128]{3,2,1,0:T(8,128)(2,1)S(1)}, bf16[64,1,8,128]{3,2,1,0:T(8,128)(2,1)}, u32[]{:S(2)}) copy-start(bf16[64,1,8,128]{3,2,1,0:T(8,128)(2,1)} %param.7) | copy-start | bytes 393220
  0.7 6.0 %copy-start.2 = (bf16[32,32,3,3,3]{1,0,4,3,2:T(8,128)(2,1)S(1)}, bf16[32,32,3,3,3]{1,0,4,3,2:T(8,128)(2,1)}, u32[]{:S(2)}) copy-start(bf16[32,32,3,3,3]{1,0,4,3,2:T(8,128)(2,1)} %param.5) | copy-start | bytes 165892
  0.7 6.0 %copy-start.3 = (bf16[64,32,3,3,3]{0,1,4,3,2:T(8,128)(2,1)S(1)}, bf16[64,32,3,3,3]{0,1,4,3,2:T(8,128)(2,1)}, u32[]{:S(2)}) copy-start(bf16[64,32,3,3,3]{0,1,4,3,2:T(8,128)(2,1)} %param.6) | copy-start | bytes 331780
  2.8 5.3 %collective-permute-start = (bf16[512,384]{1,0:T(8,128)(2,1)S(1)}, bf16[512,384]{1,0:T(8,128)(2,1)S(1)}, u32[]{:S(2)}, u32[]{:S(2)}) collective-permute-start(bf16[512,384]{1,0:T(8,128)(2,1)S(1)} %get-tuple-element.41), channel_id=1, source_target_pairs={{0,1},{2,3},{4,5},{6,7},{8,9},{10,11},{12,13},{14,15},{1,0},{3,2},... | collective-permute-start | bytes 1179656 | tf_op jit(solution)/shard_map/halo_a/ppermute | solution.py:317
  3.6 13.3 %collective-permute-start.1 = (bf16[512,384]{1,0:T(8,128)(2,1)S(1)}, bf16[512,384]{1,0:T(8,128)(2,1)S(1)}, u32[]{:S(2)}, u32[]{:S(2)}) collective-permute-start(bf16[512,384]{1,0:T(8,128)(2,1)S(1)} %get-tuple-element.40), channel_id=1, source_target_pairs={{1,2},{3,4},{5,6},{7,8},{9,10},{11,12},{13,14},{2,1},{4,3},{6,5},{... | collective-permute-start | bytes 1179656 | tf_op jit(solution)/shard_map/halo_a/ppermute | solution.py:315
  22.7 1.4 %collective-permute-start.4 = (bf16[576,128]{1,0:T(8,128)(2,1)S(1)}, bf16[576,128]{1,0:T(8,128)(2,1)S(1)}, u32[]{:S(2)}, u32[]{:S(2)}) collective-permute-start(bf16[576,128]{1,0:T(8,128)(2,1)S(1)} %get-tuple-element.32), channel_id=1, source_target_pairs={{0,1},{1,0},{2,3},{3,2},{4,5},{5,4},{6,7},{7,6},{8,9},{9,8},{10,11... | collective-permute-start | bytes 442376 | tf_op jit(solution)/shard_map/ppermute | solution.py:327
  24.3 4.5 %collective-permute-start.5 = (bf16[432,128]{1,0:T(8,128)(2,1)S(1)}, bf16[432,128]{1,0:T(8,128)(2,1)S(1)}, u32[]{:S(2)}, u32[]{:S(2)}) collective-permute-start(bf16[432,128]{1,0:T(8,128)(2,1)S(1)} %pad_maximum_fusion.2), channel_id=1, source_target_pairs={{0,2},{1,3},{2,0},{3,1},{4,6},{5,7},{6,4},{7,5},{8,10},{9,11},{10,... | collective-permute-start | bytes 331784 | tf_op jit(solution)/shard_map/ppermute | solution.py:327
  28.9 4.6 %collective-permute-start.6 = (bf16[360,128]{1,0:T(8,128)(2,1)S(1)}, bf16[360,128]{1,0:T(8,128)(2,1)S(1)}, u32[]{:S(2)}, u32[]{:S(2)}) collective-permute-start(bf16[360,128]{1,0:T(8,128)(2,1)S(1)} %pad_maximum_fusion.3), channel_id=1, source_target_pairs={{0,4},{1,5},{2,6},{3,7},{4,0},{5,1},{6,2},{7,3},{8,12},{9,13},{10,... | collective-permute-start | bytes 276488 | tf_op jit(solution)/shard_map/ppermute | solution.py:327
  30.3 4.2 %collective-permute-start.2 = (bf16[640,256]{1,0:T(8,128)(2,1)S(1)}, bf16[640,256]{1,0:T(8,128)(2,1)S(1)}, u32[]{:S(2)}, u32[]{:S(2)}) collective-permute-start(bf16[640,256]{1,0:T(8,128)(2,1)S(1)} %get-tuple-element.23), channel_id=1, source_target_pairs={{0,1},{2,3},{4,5},{6,7},{8,9},{10,11},{12,13},{14,15},{1,0},{3,2},... | collective-permute-start | bytes 983048 | tf_op jit(solution)/shard_map/halo_b/ppermute | solution.py:317
  31.6 11.9 %collective-permute-start.3 = (bf16[640,256]{1,0:T(8,128)(2,1)S(1)}, bf16[640,256]{1,0:T(8,128)(2,1)S(1)}, u32[]{:S(2)}, u32[]{:S(2)}) collective-permute-start(bf16[640,256]{1,0:T(8,128)(2,1)S(1)} %get-tuple-element.24), channel_id=1, source_target_pairs={{1,2},{3,4},{5,6},{7,8},{9,10},{11,12},{13,14},{2,1},{4,3},{6,5},{... | collective-permute-start | bytes 983048 | tf_op jit(solution)/shard_map/halo_b/ppermute | solution.py:315
  33.6 12.9 %collective-permute-start.7 = (bf16[324,128]{1,0:T(8,128)(2,1)S(1)}, bf16[324,128]{1,0:T(8,128)(2,1)S(1)}, u32[]{:S(2)}, u32[]{:S(2)}) collective-permute-start(bf16[324,128]{1,0:T(8,128)(2,1)S(1)} %pad_maximum_fusion.4), channel_id=1, source_target_pairs={{0,8},{1,9},{2,10},{3,11},{4,12},{5,13},{6,14},{7,15},{8,0},{9,1},... | collective-permute-start | bytes 248840 | tf_op jit(solution)/shard_map/ppermute | solution.py:327

commit v2 on v1

v2 whole, which is shorter than its diff:
```python
import functools

import jax
import jax.numpy as jnp
from jax import lax
from jax.experimental import pallas as pl
from jax.experimental.pallas import tpu as pltpu
from jax.sharding import PartitionSpec as P


BF = jnp.bfloat16
F32 = jnp.float32
LANES = 128
VMEM = pl.BlockSpec(memory_space=pltpu.VMEM)


def dot(a, b):
    return jnp.dot(a, b, preferred_element_type=F32)


def dot_nt(a, b):
    return lax.dot_general(a, b, (((1,), (1,)), ((), ())), preferred_element_type=F32)


def iota(shape, dim):
    return lax.broadcasted_iota(jnp.int32, shape, dim)


def place(rows, lanes, offset):
    return (iota((rows, lanes), 1) == iota((rows, lanes), 0) + offset).astype(F32).astype(BF)


def moved(x, step, width):
    lanes = x.shape[1]
    w = iota(x.shape, 1) % width
    rolled = pltpu.roll(x, (-step) % lanes, 1)
    edge = width - 1 if step > 0 else 0
    return jnp.where(w == edge, 0.0, rolled)


def taps_sum(y, rows, width):
    return y[rows : 2 * rows] + moved(y[:rows], -1, width) + moved(y[2 * rows :], 1, width)


def tap(d, h, w):
    return d * 9 + h * 3 + w


def unpack(src_ref, f_ref, halves, scale=None):
    for half in range(halves):
        part = src_ref[:, half * LANES : (half + 1) * LANES].astype(F32)
        f_ref[half] = part if scale is None else part * scale


def row_of(f_ref, start, count, stride, first, last):
    parts = [f_ref[half, pl.ds(start, count, stride=stride), :] for half in range(first, last)]
    whole = parts[0] if len(parts) == 1 else jnp.concatenate(parts, axis=1)
    return whole.astype(BF)


def windows(h, pairs):
    return [(b, h + 1 - 2 * b) for b in range(pairs) if 0 <= h + 1 - 2 * b < 4]


def parity():
    return lax.axis_index("gx") % 2


def inside():
    index = lax.axis_index("gx")
    return jnp.where((index == 0) | (index == lax.axis_size("gx") - 1), 0.0, 1.0)


def fill_plane(dst, tile_of, rows, pairs, planes, plane, height, width):
    for h in range(rows):
        tile = tile_of(h)
        for b, j in windows(h, pairs):
            at = pl.multiple_of((j * planes + plane) * height, height)
            dst[pl.ds(at, height), b * width : b * width + width] = tile


def clear_ends(dst, planes, height, pairs, width):
    dst[: planes * height, :width] = jnp.zeros((planes * height, width), BF)
    dst[3 * planes * height :, (pairs - 1) * width :] = jnp.zeros((planes * height, width), BF)


def near_kernel(C, F, H, W, w2, near, far, a1, ka, vv, slope, means, xf):
    span = 4 * C
    halves, low = W // LANES, H // 2
    odd = parity()
    ka[...] = jnp.zeros(ka.shape, BF)
    stacks = [w2[dt * 9 : dt * 9 + 9].reshape(9 * C, C) for dt in range(3)]
    for d in range(2):
        tiles = sum(dot(stacks[dt], place(C, span, (dt + d) * C)) for dt in range(3)).astype(BF)
        for wt in range(3):
            for h in range(2):
                at = (wt * 2 + h) * C
                for ht in range(3):
                    lane = (h + ht) * span
                    g = ht * 3 + wt
                    ka[d, at : at + C, lane : lane + span] = tiles[g * C : g * C + C]
    for src, plane in ((near, 2 - odd), (far, 1 + odd), (a1, 3 - 3 * odd)):
        unpack(src, xf, halves)
        fill_plane(vv, lambda h: row_of(xf, h, C, H, 0, halves), H, low, 4, plane, C, W)
    zero = jnp.zeros((C, W), BF)
    fill_plane(vv, lambda h: zero, H, low, 4, 3 * odd, C, W)
    clear_ends(vv, 4, C, low, W)
    forward_plane(C, H, W, ka, 1 - odd, vv, slope, lambda b, mean: means.__setitem__(b, mean))


def forward_plane(C, H, W, ka, d, vv, slope, put):
    wide = W // 2
    eighth = jnp.where(iota((W, wide), 0) // 2 == iota((W, wide), 1), 0.125, 0.0).astype(BF)
    for b in range(H // 2):
        value = taps_sum(dot(ka[d], vv[:, b * W : b * W + W]), 2 * C, W)
        sigma = jax.nn.sigmoid(value)
        slope[b] = sigma * (1.0 + value * (1.0 - sigma))
        sums = dot((value * sigma).astype(BF), eighth)
        put(b, sums[:C] + sums[C:])


def far_kernel(C, F, H, W, a2, ka, means, vv_in, slope, pooled, vv, xf):
    halves, low, wide = W // LANES, H // 2, W // 2
    odd = parity()
    unpack(a2, xf, halves, inside())
    fill_plane(vv, lambda h: row_of(xf, h, C, H, 0, halves), H, low, 4, 3 * odd, C, W)
    quarter = low // 2

    def put(b, mean):
        at, lane = (b % quarter) * C, (b // quarter) * wide
        pooled[at : at + C, lane : lane + wide] = (mean + means[b]).astype(BF)

    forward_plane(C, H, W, ka, odd, vv, slope, put)


def prep_kernel(C, F, H, W, w2, w3, cot, kb, k3f, k3b, cc, cf):
    span, low, wide = 4 * C, H // 2, W // 2
    kb[...] = jnp.zeros(kb.shape, BF)
    k3f[...] = jnp.zeros(k3f.shape, BF)
    eye_c = place(C, C, 0)
    zero_c = jnp.zeros((C, C), BF)
    for d in range(2):
        rows = []
        for wt in range(3):
            for ht in range(3):
                three = [w2[tap(2 - dt, 2 - ht, 2 - wt)] for dt in range(3)]
                rows += ([zero_c] + three) if d else (three + [zero_c])
        tiles = dot_nt(eye_c, jnp.concatenate(rows, axis=0)).astype(BF)
        for wt in range(3):
            for h in range(2):
                at = (wt * 2 + h) * C
                for ht in range(3):
                    lane = (h + ht) * span
                    q = wt * 3 + ht
                    kb[d, at : at + C, lane : lane + span] = tiles[:, q * span : q * span + span]
    zero_f = jnp.zeros((C, F), BF)
    rows = []
    for wt in range(3):
        for ht in range(3):
            rows += [w3[tap(dt, ht, wt)] for dt in range(3)] + [zero_f]
    tiles = dot_nt(place(F, F, 0), jnp.concatenate(rows, axis=0)).astype(BF)
    for wt in range(3):
        for h in range(2):
            at = (wt * 2 + h) * F
            for ht in range(3):
                lane = (h + ht) * span
                q = wt * 3 + ht
                k3f[at : at + F, lane : lane + span] = tiles[:, q * span : q * span + span]
    four = 4 * F
    picked = [
        jnp.concatenate([w3[tap(2 - dt, 2 - ht, 2 - wt)] for wt in range(3) for dt in range(3)], axis=0)
        for ht in range(3)
    ]
    for h in range(2):
        tiles = sum(dot(picked[ht], place(F, four, (ht + h) * F)) for ht in range(3)).astype(BF)
        for wt in range(3):
            at = (wt * 2 + h) * C
            for dt in range(3):
                q = wt * 3 + dt
                k3b[at : at + C, dt * four : dt * four + four] = tiles[q * C : q * C + C]
    unpack(cot, cf, wide // LANES)
    fill_cot(F, H, W, cc, cf, 1)
    for plane in range(3):
        cc[plane * four : plane * four + F, :wide] = jnp.zeros((F, wide), BF)
        cc[plane * four + 3 * F : plane * four + four, (low // 2 - 1) * wide :] = jnp.zeros((F, wide), BF)


def fill_cot(F, H, W, cc, cf, plane):
    low, wide = H // 2, W // 2
    for h in range(low):
        tile = row_of(cf, h, F, low, 0, wide // LANES)
        for b, j in windows(h, low // 2):
            at = pl.multiple_of((plane * 4 + j) * F, F)
            cc[pl.ds(at, F), b * wide : b * wide + wide] = tile


def slope_kernel(C, F, H, W, c1, c2, slope_near, slope_far, pooled, k3b, cc_in, p1, p2, cc, cf, bp):
    low, wide = H // 2, W // 2
    odd = parity()
    for src, plane, scale in ((c1, 2 - 2 * odd, None), (c2, 2 * odd, inside())):
        unpack(src, cf, wide // LANES, scale)
        fill_cot(F, H, W, cc, cf, plane)
    bp[...] = taps_sum(dot(k3b[...], cc[...]), 2 * C, wide).astype(BF)
    spread = jnp.where(iota((wide, W), 1) // 2 == iota((wide, W), 0), 0.125, 0.0).astype(BF)
    for b in range(low):
        back = dot(bp[(b % 2) * C : (b % 2) * C + C, (b // 2) * wide : (b // 2) * wide + wide], spread)
        back = jnp.concatenate([back, back], axis=0)
        for out, slope in ((p1, slope_near), (p2, slope_far)):
            out[b * 2 * C : (b + 1) * 2 * C, :] = (back * slope[b]).astype(BF)
    for out in (p1, p2):
        out[H * C :, :] = pooled[...]


def grads_kernel(C, F, H, W, count, p1, p2, vv, cc, packet, keep, gg, ps, r2, r3):
    low, wide = H // 2, W // 2
    odd = parity()
    for b in range(low):
        for d, src in ((1 - odd, p1), (odd, p2)):
            tile = src[b * 2 * C : (b + 1) * 2 * C, :]
            up = tile.astype(F32)
            for wt in range(3):
                val = tile if wt == 1 else moved(up, 1 - wt, W).astype(BF)
                at = pl.multiple_of((wt * 2 + d) * 2 * C, 2 * C)
                gg[pl.ds(at, 2 * C), b * W : b * W + W] = val
    both = dot_nt(gg[...], vv[...])
    span = 4 * C
    twos = []
    for wt in range(3):
        for ht in range(3):
            parts = []
            for d in range(2):
                at = (wt * 4 + d * 2) * C
                parts.append(
                    both[at : at + C, ht * span : ht * span + span]
                    + both[at + C : at + 2 * C, (ht + 1) * span : (ht + 2) * span]
                )
            twos.append(parts[0] + pltpu.roll(parts[1], span - C, 1))
    r2[...] = jnp.concatenate(dense(twos, C), axis=1)
    quarter = low // 2
    ps[...] = jnp.zeros(ps.shape, BF)
    for b in range(low // 2):
        for q in range(2):
            h = 2 * b + q
            at, lane = H * C + (h % quarter) * C, (h // quarter) * wide
            tile = p1[at : at + C, lane : lane + wide]
            up = tile.astype(F32)
            for wt in range(3):
                val = tile if wt == 1 else moved(up, wt - 1, wide).astype(BF)
                to = (q * 4 + wt) * C
                ps[to : to + C, b * wide : b * wide + wide] = val
    p3 = dot_nt(cc[...], ps[...])
    tiles = []
    for dt in range(3):
        for ht in range(3):
            first = ((2 - dt) * 4 + 2 - ht) * F
            second = first + F
            tiles.append(p3[first : first + F, :span] + p3[second : second + F, span:])
    tiles = dense(tiles, C)
    each, bits = F // count, count.bit_length() - 1
    row, col = iota((F, F), 0), iota((F, F), 1)
    chunk = row // each
    lowest, index = (chunk >> (bits - 1)) & 1, jnp.zeros((F, F), jnp.int32)
    for bit in range(1, bits):
        value = (chunk >> (bits - 1 - bit)) & 1
        lowest, index = lowest ^ value, index + (value << bit)
    order = (col == (index + lowest) * each + row % each).astype(F32).astype(BF)
    r3[...] = dot(order, jnp.concatenate(tiles, axis=1).astype(BF))
    first, own = 0, lax.axis_index("gx")
    for bit in range(bits):
        first = first ^ ((own >> bit) & 1)
    start = 0
    for src, half in ((r2, C // 2), (r3, F // 2)):
        for q in range(len(tiles)):
            lanes = slice(q * span, q * span + span)
            give = src[pl.ds(pl.multiple_of((1 - first) * half, half), half), lanes]
            packet[q, start : start + half, :] = give.astype(BF)
            keep[q, start : start + half, :] = src[pl.ds(pl.multiple_of(first * half, half), half), lanes]
        start += half


def dense(tiles, C):
    lane = iota(tiles[0].shape, 1)
    out = [None] * (-(-len(tiles) * 3 // 4))
    for q, tile in enumerate(tiles):
        first, offset = divmod(3 * q, 4)
        tile = jnp.where(lane < 3 * C, tile, 0.0)
        if offset:
            tile = pltpu.roll(tile, offset * C, 1)
        low = tile if offset < 2 else jnp.where(lane >= offset * C, tile, 0.0)
        out[first] = low if out[first] is None else out[first] + low
        if offset > 1:
            out[first + 1] = jnp.where(lane < offset * C, tile, 0.0)
    return out


def finish_kernel(C, count, own_half, got_half, part, two, three):
    span, half = 4 * C, C // 2
    first, own = 0, lax.axis_index("gx")
    for bit in range(count.bit_length() - 1):
        first = first ^ ((own >> bit) & 1)
    for t in range(27):
        dt, ht, wt = t // 9, t // 3 % 3, t % 3
        q, group = divmod(wt * 9 + ht * 3 + dt, 4)
        for src, at in ((own_half, first), (got_half, 1 - first)):
            tile = src[q]
            if group:
                tile = pltpu.roll(tile, span - group * C, 1)
            two[t, pl.ds(pl.multiple_of(at * half, half), half), :] = tile[:, :C]
        q, group = divmod(t, 4)
        tile = part[q]
        if group:
            tile = pltpu.roll(tile, span - group * C, 1)
        three[t] = tile[:, :C]


def backward_plane(C, H, W, kb, d, gw, zf):
    for b in range(H // 2):
        out = taps_sum(dot(kb[d], gw[:, b * W : b * W + W]), 2 * C, W)
        for q in range(2):
            for half in range(W // LANES):
                lanes = slice(half * LANES, (half + 1) * LANES)
                zf[half, pl.ds(2 * b + q, C, stride=H), :] = out[q * C : q * C + C, lanes]


def back_near_kernel(C, F, H, W, b1, p1, p2, kb, plane_near, gw, zf):
    low, halves = H // 2, W // LANES
    odd = parity()
    for src, plane in ((p1, 2 - odd), (p2, 1 + odd), (b1, 3 - 3 * odd)):
        fill_plane(gw, lambda h: src[h * C : h * C + C, :], H, low, 4, plane, C, W)
    zero = jnp.zeros((C, W), BF)
    fill_plane(gw, lambda h: zero, H, low, 4, 3 * odd, C, W)
    clear_ends(gw, 4, C, low, W)
    backward_plane(C, H, W, kb, 1 - odd, gw, zf)
    for half in range(halves):
        plane_near[:, half * LANES : (half + 1) * LANES] = zf[half].astype(BF)


def back_far_kernel(C, F, H, W, b1, b2, p1, kb, k3f, plane_near, gw_in, gv, ft, gw, pp, zf, ff):
    low, wide = H // 2, W // 2
    quarter, halves, low_halves = low // 2, W // LANES, wide // LANES
    odd = parity()
    scale = inside().astype(BF)
    fill_plane(gw, lambda h: b2[h * C : h * C + C, :] * scale, H, low, 4, 3 * odd, C, W)
    backward_plane(C, H, W, kb, odd, gw, zf)
    for c in range(C):
        rows = slice(c * H, c * H + H)
        gv[c, 1 - odd] = plane_near[rows, :]
        gv[c, odd] = jnp.concatenate([zf[half, rows, :] for half in range(halves)], axis=1).astype(BF)
    pp[...] = jnp.zeros(pp.shape, BF)
    for src, plane in ((b1, 2 - 2 * odd), (b2, 2 * odd), (p1, 1)):

        def tile_of(h):
            at, lane = H * C + (h % quarter) * C, (h // quarter) * wide
            tile = src[at : at + C, lane : lane + wide]
            return tile * scale if src is b2 else tile

        fill_plane(pp, tile_of, low, quarter, 4, plane, C, wide)
    out = taps_sum(dot(k3f[...], pp[...]), 2 * F, wide)
    for b in range(quarter):
        for q in range(2):
            for half in range(low_halves):
                lane = b * wide + half * LANES
                ff[half, pl.ds(2 * b + q, F, stride=low), :] = out[q * F : q * F + F, lane : lane + LANES]
    for half in range(low_halves):
        ft[:, half * LANES : (half + 1) * LANES] = ff[half].astype(BF)


def call(body, outs, scratch, flops, aliases, *args):
    return pl.pallas_call(
        body,
        out_shape=outs,
        in_specs=[VMEM] * len(args),
        out_specs=jax.tree.map(lambda _: VMEM, outs),
        scratch_shapes=scratch,
        cost_estimate=pl.CostEstimate(flops=flops // 1000, bytes_accessed=1024, transcendentals=0),
        compiler_params=pltpu.CompilerParams(vmem_limit_bytes=12 * 2**20),
        input_output_aliases=aliases,
    )(*args)


def swap(near, far, axis):
    count = lax.axis_size(axis)
    groups = lax.axis_size("groups")
    pairs = [(i, i + 1) for i in range(1, count - 1, 2)]
    pairs = [(g * count + a, g * count + b) for g in range(groups) for a, b in pairs]
    pairs += [(g * count + e, (g + 1) * count + e) for g in range(0, groups - 1, 2) for e in (0, count - 1)]
    got_far = lax.ppermute(far, ("groups", axis), pairs + [(b, a) for a, b in pairs])
    pairs = [(i, i + 1) for i in range(0, count - 1, 2)]
    got_near = lax.ppermute(near, axis, pairs + [(b, a) for a, b in pairs])
    return got_near, got_far


def reduce_both(packet, keep, shared, axis):
    count = lax.axis_size(axis)
    index = lax.axis_index(axis)
    exchange = lambda v, mask: lax.ppermute(v, axis, [(i, i ^ mask) for i in range(count)])
    keep = keep + exchange(packet, 1).astype(F32)
    full, part = keep[:, :shared], keep[:, shared:]
    step = 2
    while step < count:
        half = part.shape[1] // 2
        bit = (index // step) % 2
        give = lax.dynamic_slice_in_dim(part, (1 - bit) * half, half, 1).astype(BF)
        part = lax.dynamic_slice_in_dim(part, bit * half, half, 1)
        full = full.astype(BF)
        got = exchange(jnp.concatenate([full, give], axis=1), step | 1)
        full = full.astype(F32) + got[:, :shared].astype(F32)
        part = part + got[:, shared:].astype(F32)
        step *= 2
    other = exchange(full, 1)
    return full, other, part


def program(volume, weight_two, weight_three, cotangent):
    C, planes, H, W = volume.shape
    F, _, low, wide = cotangent.shape
    count = lax.axis_size("gx")
    assert planes == 2 and 2 * low == H and 2 * wide == W
    assert count > 1 and count & (count - 1) == 0 and F % count == 0
    sds = jax.ShapeDtypeStruct
    odd = lax.axis_index("gx") % 2
    w2 = jnp.transpose(weight_two, (2, 3, 4, 0, 1)).reshape(27, C, C)
    w3 = jnp.transpose(weight_three, (2, 3, 4, 1, 0)).reshape(27, C, F)
    cot = cotangent.reshape(F * low, wide)
    near = lax.dynamic_index_in_dim(volume, 1 - odd, 1, keepdims=False).reshape(C * H, W)
    far = lax.dynamic_index_in_dim(volume, odd, 1, keepdims=False).reshape(C * H, W)
    a1, a2 = swap(near, far, "gx")
    halves, low_halves = W // LANES, wide // LANES
    bind = lambda body: functools.partial(body, C, F, H, W)
    window, window_cot = sds((16 * C, low * W), BF), sds((12 * F, low // 2 * wide), BF)
    filters, slopes = sds((2, 6 * C, 16 * C), BF), sds((low, 2 * C, W), F32)
    plane_f32 = pltpu.VMEM((halves, C * H, LANES), F32)
    plane_low_f32 = pltpu.VMEM((low_halves, F * low, LANES), F32)
    ka, vv, slope_near, means = call(
        bind(near_kernel),
        (filters, window, slopes, sds((low, C, wide), F32)),
        [plane_f32],
        900_000_000,
        {},
        w2,
        near,
        far,
        a1,
    )
    c1, c2 = swap(cot, cot, "gx")
    kb, k3f, k3b, cc = call(
        bind(prep_kernel),
        (filters, sds((6 * F, 16 * C), BF), sds((6 * C, 12 * F), BF), window_cot),
        [plane_low_f32],
        400_000_000,
        {},
        w2,
        w3,
        cot,
    )
    rows = low // 2 * C
    slope_far, pooled, vv = call(
        bind(far_kernel),
        (slopes, sds((rows, W), BF), window),
        [plane_f32],
        700_000_000,
        {3: 2},
        a2,
        ka,
        means,
        vv,
    )
    rows = H * C + rows
    p1, p2, cc = call(
        bind(slope_kernel),
        (sds((rows, W), BF), sds((rows, W), BF), window_cot),
        [plane_low_f32, pltpu.VMEM((2 * C, low // 2 * wide), BF)],
        400_000_000,
        {6: 2},
        c1,
        c2,
        slope_near,
        slope_far,
        pooled,
        k3b,
        cc,
    )
    b1, b2 = swap(p1, p2, "gx")
    tiles, shared = 7, C // 2
    packet, keep = call(
        lambda *refs: grads_kernel(C, F, H, W, count, *refs),
        (sds((tiles, shared + F // 2, 4 * C), BF), sds((tiles, shared + F // 2, 4 * C), F32)),
        [
            pltpu.VMEM((12 * C, low * W), BF),
            pltpu.VMEM((8 * C, low // 2 * wide), BF),
            pltpu.VMEM((C, tiles * 4 * C), F32),
            pltpu.VMEM((F, tiles * 4 * C), F32),
        ],
        1_200_000_000,
        {},
        p1,
        p2,
        vv,
        cc,
    )
    full, other, part = reduce_both(packet, keep, shared, "gx")
    plane_near, gw = call(
        bind(back_near_kernel),
        (sds((C * H, W), BF), window),
        [plane_f32],
        500_000_000,
        {},
        b1,
        p1,
        p2,
        kb,
    )
    gv, ft, _ = call(
        bind(back_far_kernel),
        (sds((C, 2, H, W), BF), sds((F * low, wide), BF), window),
        [pltpu.VMEM((16 * C, low // 2 * wide), BF), plane_f32, plane_low_f32],
        700_000_000,
        {6: 2},
        b1,
        b2,
        p1,
        kb,
        k3f,
        plane_near,
        gw,
    )
    two, three = call(
        lambda *refs: finish_kernel(C, count, *refs),
        (sds((27, C, C), F32), sds((27, F // count, C), F32)),
        [],
        100_000,
        {},
        full,
        other,
        part,
    )
    unfold = lambda v: jnp.transpose(v.reshape(3, 3, 3, v.shape[1], C), (3, 4, 0, 1, 2))
    return (
        ft.reshape(F, 1, low, wide),
        unfold(three),
        unfold(two),
        gv,
    )


def solution(mesh):
    return jax.shard_map(
        program,
        mesh=mesh,
        in_specs=(
            P(None, ("groups", "gx"), None, None),
            P(),
            P(),
            P(None, ("groups", "gx"), None, None),
        ),
        out_specs=(
            P(None, ("groups", "gx"), None, None),
            P(("groups", "gx"), None, None, None, None),
            P("groups", None, None, None, None),
            P(None, ("groups", "gx"), None, None),
        ),
        check_vma=False,
    )
```

time: 48.6 us -> 40.6 us (0.84)
  the two profiles are of different devices: /device:TPU:19 before, /device:TPU:11 now
where the time goes in v2:
time: 40.6 us; the launch traced here: 40.4 us
  waiting for transfers between devices  14.3 us (35%)
  Pallas kernels  12.3 us (30%)
  starting transfers between devices  8.91 us (22%)
  local copies, waits for them, and re-layouts  3.91 us (10%)
  between operations  0.91 us (2%)
    pallas_call x8, Pallas kernels, call(): pl.pallas_call(body, out_shape=outs, in_specs=[VMEM] * len(args), out_spe...  12.3 us
    ppermute x5, waiting for transfers between devices, reduce_both(): lax.ppermute(v, axis, [(i, i ^ mask) for i in range(count)])  9.18 us
    ppermute x3, waiting for transfers between devices, swap(): lax.ppermute(far, ('groups', axis), pairs + [(b, a) for a, b in pairs])  5.12 us
    ppermute x5, starting transfers between devices, reduce_both(): lax.ppermute(v, axis, [(i, i ^ mask) for i in range(count)])  4.52 us
    ppermute x3, starting transfers between devices, swap(): lax.ppermute(far, ('groups', axis), pairs + [(b, a) for a, b in pairs])  2.97 us
    unnamed x6, local copies, waits for them, and re-layouts  2.77 us
    ppermute x3, starting transfers between devices, swap(): got_near = lax.ppermute(near, axis, pairs + [(b, a) for a, b in pairs])  1.42 us
    dynamic_slice x1, local copies, waits for them, and re-layouts, program(): lax.dynamic_index_in_dim(volume, odd, 1, keepdims=False).reshape(C * H, W)  1.08 us
  transfers between devices with their start and end apart: 11, of which 7 were waited for; matrix products, arithmetic and copies ran while one was open for 0% of the time, Pallas kernels for 20%

profile of v2, /device:TPU:11, one launch (start us, length us, event | category | flops | bytes accessed | tf_op | source)
XLA Modules:
  0.0 40.4 jit_solution(12332445785088169328)
XLA Ops:
  0.7 1.1 %constant_dynamic-slice_fusion = (bf16[32,1,16,256]{3,2,1,0:T(8,128)(2,1)S(1)}, bf16[32,1,16,256]{3,2,1,0:T(8,128)(2,1)S(1)}) fusion(bf16[32,2,16,256]{3,2,1,0:T(8,128)(2,1)} %param.4, s32[]{:T(128)S(6)} %select_n.56, s32[]{:T(128)S(6)} %select_n.55), kind=kLoop, calls=%fused_computation.14 | loop fusion | bytes 1048584 | tf_op jit(solution)/shard_map/jit(dynamic_index_in_dim)/dynamic_slice | solution.py:426
  1.7 0.7 %collective-permute-start.2 = (bf16[512,256]{1,0:T(8,128)(2,1)S(1)}, bf16[512,256]{1,0:T(8,128)(2,1)S(1)}, u32[]{:S(2)}, u32[]{:S(2)}) collective-permute-start(bf16[512,256]{1,0:T(8,128)(2,1)S(1)} %bitcast.20), channel_id=1, source_target_pairs={{0,1},{2,3},{4,5},{6,7},{8,9},{10,11},{12,13},{14,15},{1,0},{3,2},... | collective-permute-start | bytes 786440 | tf_op jit(solution)/shard_map/ppermute | solution.py:389
  2.5 1.2 %collective-permute-start.3 = (bf16[512,256]{1,0:T(8,128)(2,1)S(1)}, bf16[512,256]{1,0:T(8,128)(2,1)S(1)}, u32[]{:S(2)}, u32[]{:S(2)}) collective-permute-start(bf16[512,256]{1,0:T(8,128)(2,1)S(1)} %bitcast.18), channel_id=1, source_target_pairs={{1,2},{3,4},{5,6},{7,8},{9,10},{11,12},{13,14},{17,18},{19,20},{21... | collective-permute-start | bytes 786440 | tf_op jit(solution)/shard_map/ppermute | solution.py:387
  3.7 0.3 collective-permute-start
  4.0 1.3 %collective-permute-start.1 = (bf16[512,128]{1,0:T(8,128)(2,1)}, bf16[512,128]{1,0:T(8,128)(2,1)S(1)}, u32[]{:S(2)}, u32[]{:S(2)}) collective-permute-start(bf16[512,128]{1,0:T(8,128)(2,1)} %bitcast.26), channel_id=1, source_target_pairs={{1,2},{3,4},{5,6},{7,8},{9,10},{11,12},{13,14},{17,18},{19,20},{21... | collective-permute-start | bytes 393224 | tf_op jit(solution)/shard_map/ppermute | solution.py:387
  5.3 0.9 %copy-done = bf16[32,32,3,3,3]{1,0,4,3,2:T(8,128)(2,1)S(1)} copy-done((bf16[32,32,3,3,3]{1,0,4,3,2:T(8,128)(2,1)S(1)}, bf16[32,32,3,3,3]{1,0,4,3,2:T(8,128)(2,1)}, u32[]{:S(2)}) %copy-start) | copy-done | bytes 55320
  6.3 0.9 %copy-done.1 = bf16[64,32,3,3,3]{0,1,4,3,2:T(8,128)(2,1)S(1)} copy-done((bf16[64,32,3,3,3]{0,1,4,3,2:T(8,128)(2,1)S(1)}, bf16[64,32,3,3,3]{0,1,4,3,2:T(8,128)(2,1)}, u32[]{:S(2)}) %copy-start.1) | copy-done | bytes 110616
  7.2 0.9 %copy-done.2 = bf16[64,1,8,128]{3,2,1,0:T(8,128)(2,1)S(1)} copy-done((bf16[64,1,8,128]{3,2,1,0:T(8,128)(2,1)S(1)}, bf16[64,1,8,128]{3,2,1,0:T(8,128)(2,1)}, u32[]{:S(2)}) %copy-start.2) | copy-done | bytes 131096
  8.1 0.7 %shard_map.77 = (bf16[2,192,512]{2,1,0:T(8,128)(2,1)S(1)}, bf16[384,512]{1,0:T(8,128)(2,1)S(1)}, bf16[192,768]{1,0:T(8,128)(2,1)S(1)}, bf16[768,512]{1,0:T(8,128)(2,1)S(1)}) custom-call(bf16[27,32,32]{2,1,0:T(8,128)(2,1)S(1)} %bitcast.22, bf16[27,32,64]{2,1,0:T(8,128)(2,1)S(1)} %bitcast.24, bf16[512,128]{1,0:T(8,128)(2,1)S(1)} %bitcast.27), custom_call_target="tpu_custom_call" | custom-call | flops 400000 | bytes 1024 | tf_op jit(solution)/shard_map/pallas_call | solution.py:369
  8.8 0.0 collective-permute-done.2.a1
  8.8 3.3 %shard_map.75 = (bf16[2,192,512]{2,1,0:T(8,128)(2,1)S(1)}, bf16[512,2048]{1,0:T(8,128)(2,1)S(1)}, f32[8,64,256]{2,1,0:T(8,128)S(1)}, f32[8,32,128]{2,1,0:T(8,128)S(1)}) custom-call(bf16[27,32,32]{2,1,0:T(8,128)(2,1)S(1)} %bitcast.23, bf16[512,256]{1,0:T(8,128)(2,1)S(1)} %bitcast.21, bf16[512,256]{1,0:T(8,128)(2,1)S(1)} %bitcast.19, ...), custom_call_target="tpu_custom_call" | custom-call | flops 900000 | bytes 1024 | tf_op jit(solution)/shard_map/pallas_call | solution.py:369
  12.2 0.3 collective-permute-done.3.a2
  12.5 2.1 %shard_map.76 = (f32[8,64,256]{2,1,0:T(8,128)S(1)}, bf16[128,256]{1,0:T(8,128)(2,1)S(1)}, bf16[512,2048]{1,0:T(8,128)(2,1)S(1)}) custom-call(bf16[512,256]{1,0:T(8,128)(2,1)S(1)} %collective-permute-done.3.a2, bf16[2,192,512]{2,1,0:T(8,128)(2,1)S(1)} %get-tuple-element.27.ka, ...), custom_call_target="tpu_custom_call", output_to_operand_aliasing={{2}: (3, {})} | custom-call | flops 700000 | bytes 1024 | tf_op jit(solution)/shard_map/pallas_call | solution.py:369
  14.6 0.0 collective-permute-done.1.c2
  14.6 0.7 %shard_map.78 = (bf16[640,256]{1,0:T(8,128)(2,1)S(1)}, bf16[640,256]{1,0:T(8,128)(2,1)S(1)}, bf16[768,512]{1,0:T(8,128)(2,1)S(1)}) custom-call(bf16[512,128]{1,0:T(8,128)(2,1)S(1)} %collective-permute-done.c1, bf16[512,128]{1,0:T(8,128)(2,1)S(1)} %collective-permute-done.1.c2, ...), custom_call_target="tpu_custom_call", output_to_operand_aliasing={{2}: (6, {})} | custom-call | flops 400000 | bytes 1024 | tf_op jit(solution)/shard_map/pallas_call | solution.py:369
  15.3 1.6 %shard_map.81 = (bf16[7,48,128]{2,1,0:T(8,128)(2,1)S(1)}, f32[7,48,128]{2,1,0:T(8,128)S(1)}) custom-call(bf16[640,256]{1,0:T(8,128)(2,1)S(1)} %get-tuple-element.34.p1.refs_0_, bf16[640,256]{1,0:T(8,128)(2,1)S(1)} %get-tuple-element.35.p2.refs_1_, bf16[512,2048]{1,0:T(8,128)(2,1)S(1)} %get-tuple-element.41.refs_2_, ...), custom_call_target="tpu_custom_call" | custom-call | flops 1200000 | bytes 1024 | tf_op jit(solution)/shard_map/pallas_call | solution.py:369
  16.9 0.1 collective-permute-start.6
  17.1 1.2 %collective-permute-done.6 = bf16[7,48,128]{2,1,0:T(8,128)(2,1)S(1)} collective-permute-done((bf16[7,48,128]{2,1,0:T(8,128)(2,1)S(1)}, bf16[7,48,128]{2,1,0:T(8,128)(2,1)S(1)}, u32[]{:S(2)}, u32[]{:S(2)}) %collective-permute-start.6) | collective-permute-done | bytes 86048 | tf_op jit(solution)/shard_map/ppermute | solution.py:396
  18.4 1.3 %collective-permute-start.7 = (bf16[7,32,128]{2,1,0:T(8,128)(2,1)S(1)}, bf16[7,32,128]{2,1,0:T(8,128)(2,1)S(1)}, u32[]{:S(2)}, u32[]{:S(2)}) collective-permute-start(bf16[7,32,128]{2,1,0:T(8,128)(2,1)S(1)} %pad_maximum_fusion), channel_id=1, source_target_pairs={{0,3},{1,2},{2,1},{3,0},{4,7},{5,6},{6,5},{7,4},{8,11},{9,10},{10,... | collective-permute-start | bytes 172040 | tf_op jit(solution)/shard_map/ppermute | solution.py:396
  19.7 2.5 %collective-permute-done.7 = bf16[7,32,128]{2,1,0:T(8,128)(2,1)S(1)} collective-permute-done((bf16[7,32,128]{2,1,0:T(8,128)(2,1)S(1)}, bf16[7,32,128]{2,1,0:T(8,128)(2,1)S(1)}, u32[]{:S(2)}, u32[]{:S(2)}) %collective-permute-start.7) | collective-permute-done | bytes 57376 | tf_op jit(solution)/shard_map/ppermute | solution.py:396
  22.2 0.1 collective-permute-start.8
  22.3 3.4 %collective-permute-done.8 = bf16[7,24,128]{2,1,0:T(8,128)(2,1)S(1)} collective-permute-done((bf16[7,24,128]{2,1,0:T(8,128)(2,1)S(1)}, bf16[7,24,128]{2,1,0:T(8,128)(2,1)S(1)}, u32[]{:S(2)}, u32[]{:S(2)}) %collective-permute-start.8) | collective-permute-done | bytes 43040 | tf_op jit(solution)/shard_map/ppermute | solution.py:396
  25.8 2.4 %collective-permute-start.9 = (bf16[7,20,128]{2,1,0:T(8,128)(2,1)S(1)}, bf16[7,20,128]{2,1,0:T(8,128)(2,1)S(1)}, u32[]{:S(2)}, u32[]{:S(2)}) collective-permute-start(bf16[7,20,128]{2,1,0:T(8,128)(2,1)S(1)} %pad_maximum_fusion.2), channel_id=1, source_target_pairs={{0,9},{1,8},{2,11},{3,10},{4,13},{5,12},{6,15},{7,14},{8,1},{9,0},... | collective-permute-start | bytes 107528 | tf_op jit(solution)/shard_map/ppermute | solution.py:396
  28.2 0.4 collective-permute-start.4
  28.5 0.5 %collective-permute-start.5 = (bf16[640,256]{1,0:T(8,128)(2,1)S(1)}, bf16[640,256]{1,0:T(8,128)(2,1)S(1)}, u32[]{:S(2)}, u32[]{:S(2)}) collective-permute-start(bf16[640,256]{1,0:T(8,128)(2,1)S(1)} %get-tuple-element.35.p2.refs_1_), channel_id=1, source_target_pairs={{1,2},{3,4},{5,6},{7,8},{9,10},{11,12},{13,14},{17,18},{19,20},{21... | collective-permute-start | bytes 983048 | tf_op jit(solution)/shard_map/ppermute | solution.py:387
  29.0 1.2 %collective-permute-done.9 = bf16[7,20,128]{2,1,0:T(8,128)(2,1)S(1)} collective-permute-done((bf16[7,20,128]{2,1,0:T(8,128)(2,1)S(1)}, bf16[7,20,128]{2,1,0:T(8,128)(2,1)S(1)}, u32[]{:S(2)}, u32[]{:S(2)}) %collective-permute-start.9) | collective-permute-done | bytes 35872 | tf_op jit(solution)/shard_map/ppermute | solution.py:396
  30.2 0.7 %collective-permute-start.10 = (f32[7,16,128]{2,1,0:T(8,128)S(1)}, f32[7,16,128]{2,1,0:T(8,128)S(1)}, u32[]{:S(2)}, u32[]{:S(2)}) collective-permute-start(f32[7,16,128]{2,1,0:T(8,128)S(1)} %convert_add_fusion.1.refs_0_), channel_id=1, source_target_pairs={{0,1},{1,0},{2,3},{3,2},{4,5},{5,4},{6,7},{7,6},{8,9},{9,8},{10,11... | collective-permute-start | bytes 172040 | tf_op jit(solution)/shard_map/ppermute | solution.py:396
  30.9 0.9 %collective-permute-done.10.refs_1_ = f32[7,16,128]{2,1,0:T(8,128)S(1)} collective-permute-done((f32[7,16,128]{2,1,0:T(8,128)S(1)}, f32[7,16,128]{2,1,0:T(8,128)S(1)}, u32[]{:S(2)}, u32[]{:S(2)}) %collective-permute-start.10) | collective-permute-done | bytes 57376 | tf_op jit(solution)/shard_map/ppermute | solution.py:396
  31.8 0.9 %shard_map.82 = (f32[27,32,32]{2,1,0:T(8,128)}, f32[27,4,32]{2,1,0:T(4,128)}) custom-call(f32[7,16,128]{2,1,0:T(8,128)S(1)} %convert_add_fusion.1.refs_0_, f32[7,16,128]{2,1,0:T(8,128)S(1)} %collective-permute-done.10.refs_1_, f32[7,4,128]{2,1,0:T(4,128)S(1)} %convert_add_fusion.4.refs_2_), custom_call_target="tpu_custom_call" | custom-call | flops 100 | bytes 1024 | tf_op jit(solution)/shard_map/pallas_call | solution.py:369
  32.7 1.0 %shard_map.79 = (bf16[512,256]{1,0:T(8,128)(2,1)S(1)}, bf16[512,2048]{1,0:T(8,128)(2,1)S(1)}) custom-call(bf16[640,256]{1,0:T(8,128)(2,1)S(1)} %collective-permute-done.4.b1, bf16[640,256]{1,0:T(8,128)(2,1)S(1)} %get-tuple-element.34.p1.refs_0_, bf16[640,256]{1,0:T(8,128)(2,1)S(1)} %get-tuple-element.35.p2.refs_1_, bf16[2,192,512]{2,1,0:T(8,128)(2,1)S(1)} %get-tuple-element.36.kb), custom_call_target="tpu_custom_call" | custom-call | flops 500000 | bytes 1024 | tf_op jit(solution)/shard_map/pallas_call | solution.py:369
  33.8 4.8 %collective-permute-done.5.b2 = bf16[640,256]{1,0:T(8,128)(2,1)S(1)} collective-permute-done((bf16[640,256]{1,0:T(8,128)(2,1)S(1)}, bf16[640,256]{1,0:T(8,128)(2,1)S(1)}, u32[]{:S(2)}, u32[]{:S(2)}) %collective-permute-start.5) | collective-permute-done | bytes 327712 | tf_op jit(solution)/shard_map/ppermute | solution.py:387
  38.5 1.9 %shard_map.80 = (bf16[32,2,16,256]{3,2,1,0:T(8,128)(2,1)}, bf16[512,128]{1,0:T(8,128)(2,1)}, bf16[512,2048]{1,0:T(8,128)(2,1)S(1)}) custom-call(bf16[640,256]{1,0:T(8,128)(2,1)S(1)} %collective-permute-done.4.b1, bf16[640,256]{1,0:T(8,128)(2,1)S(1)} %collective-permute-done.5.b2, ...), custom_call_target="tpu_custom_call", output_to_operand_aliasing={{2}: (6, {})} | custom-call | flops 700000 | bytes 1024 | tf_op jit(solution)/shard_map/pallas_call | solution.py:369
  (19 shorter events, 0.2 us)
Async XLA Ops:
  1.7 7.1 %collective-permute-start.2 = (bf16[512,256]{1,0:T(8,128)(2,1)S(1)}, bf16[512,256]{1,0:T(8,128)(2,1)S(1)}, u32[]{:S(2)}, u32[]{:S(2)}) collective-permute-start(bf16[512,256]{1,0:T(8,128)(2,1)S(1)} %bitcast.20), channel_id=1, source_target_pairs={{0,1},{2,3},{4,5},{6,7},{8,9},{10,11},{12,13},{14,15},{1,0},{3,2},... | collective-permute-start | bytes 786440 | tf_op jit(solution)/shard_map/ppermute | solution.py:389
  2.5 10.0 %collective-permute-start.3 = (bf16[512,256]{1,0:T(8,128)(2,1)S(1)}, bf16[512,256]{1,0:T(8,128)(2,1)S(1)}, u32[]{:S(2)}, u32[]{:S(2)}) collective-permute-start(bf16[512,256]{1,0:T(8,128)(2,1)S(1)} %bitcast.18), channel_id=1, source_target_pairs={{1,2},{3,4},{5,6},{7,8},{9,10},{11,12},{13,14},{17,18},{19,20},{21... | collective-permute-start | bytes 786440 | tf_op jit(solution)/shard_map/ppermute | solution.py:387
  3.7 10.9 %collective-permute-start = (bf16[512,128]{1,0:T(8,128)(2,1)}, bf16[512,128]{1,0:T(8,128)(2,1)S(1)}, u32[]{:S(2)}, u32[]{:S(2)}) collective-permute-start(bf16[512,128]{1,0:T(8,128)(2,1)} %bitcast.25), channel_id=1, source_target_pairs={{0,1},{2,3},{4,5},{6,7},{8,9},{10,11},{12,13},{14,15},{1,0},{3,2},... | collective-permute-start | bytes 393224 | tf_op jit(solution)/shard_map/ppermute | solution.py:389
  4.0 10.6 %collective-permute-start.1 = (bf16[512,128]{1,0:T(8,128)(2,1)}, bf16[512,128]{1,0:T(8,128)(2,1)S(1)}, u32[]{:S(2)}, u32[]{:S(2)}) collective-permute-start(bf16[512,128]{1,0:T(8,128)(2,1)} %bitcast.26), channel_id=1, source_target_pairs={{1,2},{3,4},{5,6},{7,8},{9,10},{11,12},{13,14},{17,18},{19,20},{21... | collective-permute-start | bytes 393224 | tf_op jit(solution)/shard_map/ppermute | solution.py:387
  5.3 0.9 %copy-start = (bf16[32,32,3,3,3]{1,0,4,3,2:T(8,128)(2,1)S(1)}, bf16[32,32,3,3,3]{1,0,4,3,2:T(8,128)(2,1)}, u32[]{:S(2)}) copy-start(bf16[32,32,3,3,3]{1,0,4,3,2:T(8,128)(2,1)} %param.5) | copy-start | bytes 165892
  6.3 0.9 %copy-start.1 = (bf16[64,32,3,3,3]{0,1,4,3,2:T(8,128)(2,1)S(1)}, bf16[64,32,3,3,3]{0,1,4,3,2:T(8,128)(2,1)}, u32[]{:S(2)}) copy-start(bf16[64,32,3,3,3]{0,1,4,3,2:T(8,128)(2,1)} %param.6) | copy-start | bytes 331780
  7.2 0.9 %copy-start.2 = (bf16[64,1,8,128]{3,2,1,0:T(8,128)(2,1)S(1)}, bf16[64,1,8,128]{3,2,1,0:T(8,128)(2,1)}, u32[]{:S(2)}) copy-start(bf16[64,1,8,128]{3,2,1,0:T(8,128)(2,1)} %param.7) | copy-start | bytes 393220
  16.9 1.3 %collective-permute-start.6 = (bf16[7,48,128]{2,1,0:T(8,128)(2,1)S(1)}, bf16[7,48,128]{2,1,0:T(8,128)(2,1)S(1)}, u32[]{:S(2)}, u32[]{:S(2)}) collective-permute-start(bf16[7,48,128]{2,1,0:T(8,128)(2,1)S(1)} %get-tuple-element.44), channel_id=1, source_target_pairs={{0,1},{1,0},{2,3},{3,2},{4,5},{5,4},{6,7},{7,6},{8,9},{9,8},{10,11... | collective-permute-start | bytes 258056 | tf_op jit(solution)/shard_map/ppermute | solution.py:396
  18.4 3.7 %collective-permute-start.7 = (bf16[7,32,128]{2,1,0:T(8,128)(2,1)S(1)}, bf16[7,32,128]{2,1,0:T(8,128)(2,1)S(1)}, u32[]{:S(2)}, u32[]{:S(2)}) collective-permute-start(bf16[7,32,128]{2,1,0:T(8,128)(2,1)S(1)} %pad_maximum_fusion), channel_id=1, source_target_pairs={{0,3},{1,2},{2,1},{3,0},{4,7},{5,6},{6,5},{7,4},{8,11},{9,10},{10,... | collective-permute-start | bytes 172040 | tf_op jit(solution)/shard_map/ppermute | solution.py:396
  22.2 3.5 %collective-permute-start.8 = (bf16[7,24,128]{2,1,0:T(8,128)(2,1)S(1)}, bf16[7,24,128]{2,1,0:T(8,128)(2,1)S(1)}, u32[]{:S(2)}, u32[]{:S(2)}) collective-permute-start(bf16[7,24,128]{2,1,0:T(8,128)(2,1)S(1)} %pad_maximum_fusion.1), channel_id=1, source_target_pairs={{0,5},{1,4},{2,7},{3,6},{4,1},{5,0},{6,3},{7,2},{8,13},{9,12},{10,... | collective-permute-start | bytes 129032 | tf_op jit(solution)/shard_map/ppermute | solution.py:396
  25.8 4.4 %collective-permute-start.9 = (bf16[7,20,128]{2,1,0:T(8,128)(2,1)S(1)}, bf16[7,20,128]{2,1,0:T(8,128)(2,1)S(1)}, u32[]{:S(2)}, u32[]{:S(2)}) collective-permute-start(bf16[7,20,128]{2,1,0:T(8,128)(2,1)S(1)} %pad_maximum_fusion.2), channel_id=1, source_target_pairs={{0,9},{1,8},{2,11},{3,10},{4,13},{5,12},{6,15},{7,14},{8,1},{9,0},... | collective-permute-start | bytes 107528 | tf_op jit(solution)/shard_map/ppermute | solution.py:396
  28.2 4.6 %collective-permute-start.4 = (bf16[640,256]{1,0:T(8,128)(2,1)S(1)}, bf16[640,256]{1,0:T(8,128)(2,1)S(1)}, u32[]{:S(2)}, u32[]{:S(2)}) collective-permute-start(bf16[640,256]{1,0:T(8,128)(2,1)S(1)} %get-tuple-element.34.p1.refs_0_), channel_id=1, source_target_pairs={{0,1},{2,3},{4,5},{6,7},{8,9},{10,11},{12,13},{14,15},{1,0},{3,2},... | collective-permute-start | bytes 983048 | tf_op jit(solution)/shard_map/ppermute | solution.py:389
  28.5 10.0 %collective-permute-start.5 = (bf16[640,256]{1,0:T(8,128)(2,1)S(1)}, bf16[640,256]{1,0:T(8,128)(2,1)S(1)}, u32[]{:S(2)}, u32[]{:S(2)}) collective-permute-start(bf16[640,256]{1,0:T(8,128)(2,1)S(1)} %get-tuple-element.35.p2.refs_1_), channel_id=1, source_target_pairs={{1,2},{3,4},{5,6},{7,8},{9,10},{11,12},{13,14},{17,18},{19,20},{21... | collective-permute-start | bytes 983048 | tf_op jit(solution)/shard_map/ppermute | solution.py:387
  30.2 1.6 %collective-permute-start.10 = (f32[7,16,128]{2,1,0:T(8,128)S(1)}, f32[7,16,128]{2,1,0:T(8,128)S(1)}, u32[]{:S(2)}, u32[]{:S(2)}) collective-permute-start(f32[7,16,128]{2,1,0:T(8,128)S(1)} %convert_add_fusion.1.refs_0_), channel_id=1, source_target_pairs={{0,1},{1,0},{2,3},{3,2},{4,5},{5,4},{6,7},{7,6},{8,9},{9,8},{10,11... | collective-permute-start | bytes 172040 | tf_op jit(solution)/shard_map/ppermute | solution.py:396

commit v3 on v2

--- a/solution.py
+++ b/solution.py
@@ -84,7 +84,7 @@
     dst[3 * planes * height :, (pairs - 1) * width :] = jnp.zeros((planes * height, width), BF)
 
 
-def near_kernel(C, F, H, W, w2, near, far, a1, ka, vv, slope, means, xf):
+def setup_kernel(C, F, H, W, w2, near, far, ka, vv, xf):
     span = 4 * C
     halves, low = W // LANES, H // 2
     odd = parity()
@@ -99,12 +99,19 @@
                     lane = (h + ht) * span
                     g = ht * 3 + wt
                     ka[d, at : at + C, lane : lane + span] = tiles[g * C : g * C + C]
-    for src, plane in ((near, 2 - odd), (far, 1 + odd), (a1, 3 - 3 * odd)):
+    for src, plane in ((near, 2 - odd), (far, 1 + odd)):
         unpack(src, xf, halves)
         fill_plane(vv, lambda h: row_of(xf, h, C, H, 0, halves), H, low, 4, plane, C, W)
     zero = jnp.zeros((C, W), BF)
     fill_plane(vv, lambda h: zero, H, low, 4, 3 * odd, C, W)
     clear_ends(vv, 4, C, low, W)
+
+
+def near_kernel(C, F, H, W, a1, ka, vv_in, slope, means, vv, xf):
+    halves, low = W // LANES, H // 2
+    odd = parity()
+    unpack(a1, xf, halves)
+    fill_plane(vv, lambda h: row_of(xf, h, C, H, 0, halves), H, low, 4, 3 - 3 * odd, C, W)
     forward_plane(C, H, W, ka, 1 - odd, vv, slope, lambda b, mean: means.__setitem__(b, mean))
 
 
@@ -260,8 +267,8 @@
     row, col = iota((F, F), 0), iota((F, F), 1)
     chunk = row // each
     lowest, index = (chunk >> (bits - 1)) & 1, jnp.zeros((F, F), jnp.int32)
-    for bit in range(1, bits):
-        value = (chunk >> (bits - 1 - bit)) & 1
+    for place_of, bit in enumerate(step_bits(count)):
+        value = (chunk >> (bits - 2 - place_of)) & 1
         lowest, index = lowest ^ value, index + (value << bit)
     order = (col == (index + lowest) * each + row % each).astype(F32).astype(BF)
     r3[...] = dot(order, jnp.concatenate(tiles, axis=1).astype(BF))
@@ -276,6 +283,11 @@
             packet[q, start : start + half, :] = give.astype(BF)
             keep[q, start : start + half, :] = src[pl.ds(pl.multiple_of(first * half, half), half), lanes]
         start += half
+
+
+def step_bits(count):
+    bits = list(range(2, count.bit_length() - 1))
+    return bits + [1] if count > 2 else bits
 
 
 def dense(tiles, C):
@@ -335,12 +347,15 @@
         plane_near[:, half * LANES : (half + 1) * LANES] = zf[half].astype(BF)
 
 
-def back_far_kernel(C, F, H, W, b1, b2, p1, kb, k3f, plane_near, gw_in, gv, ft, gw, pp, zf, ff):
+def back_far_kernel(C, F, H, W, b1, b2, p1, p2, kb, k3f, plane_near, gv, ft, gw, pp, zf, ff):
     low, wide = H // 2, W // 2
     quarter, halves, low_halves = low // 2, W // LANES, wide // LANES
     odd = parity()
     scale = inside().astype(BF)
+    for src, plane in ((p1, 2 - odd), (p2, 1 + odd), (b1, 3 - 3 * odd)):
+        fill_plane(gw, lambda h: src[h * C : h * C + C, :], H, low, 4, plane, C, W)
     fill_plane(gw, lambda h: b2[h * C : h * C + C, :] * scale, H, low, 4, 3 * odd, C, W)
+    clear_ends(gw, 4, C, low, W)
     backward_plane(C, H, W, kb, odd, gw, zf)
     for c in range(C):
         rows = slice(c * H, c * H + H)
@@ -396,17 +411,15 @@
     exchange = lambda v, mask: lax.ppermute(v, axis, [(i, i ^ mask) for i in range(count)])
     keep = keep + exchange(packet, 1).astype(F32)
     full, part = keep[:, :shared], keep[:, shared:]
-    step = 2
-    while step < count:
+    for bit in step_bits(count):
         half = part.shape[1] // 2
-        bit = (index // step) % 2
-        give = lax.dynamic_slice_in_dim(part, (1 - bit) * half, half, 1).astype(BF)
-        part = lax.dynamic_slice_in_dim(part, bit * half, half, 1)
+        own = (index >> bit) & 1
+        give = lax.dynamic_slice_in_dim(part, (1 - own) * half, half, 1).astype(BF)
+        part = lax.dynamic_slice_in_dim(part, own * half, half, 1)
         full = full.astype(BF)
-        got = exchange(jnp.concatenate([full, give], axis=1), step | 1)
+        got = exchange(jnp.concatenate([full, give], axis=1), (1 << bit) | 1)
         full = full.astype(F32) + got[:, :shared].astype(F32)
         part = part + got[:, shared:].astype(F32)
-        step *= 2
     other = exchange(full, 1)
     return full, other, part
 
@@ -431,16 +444,18 @@
     filters, slopes = sds((2, 6 * C, 16 * C), BF), sds((low, 2 * C, W), F32)
     plane_f32 = pltpu.VMEM((halves, C * H, LANES), F32)
     plane_low_f32 = pltpu.VMEM((low_halves, F * low, LANES), F32)
-    ka, vv, slope_near, means = call(
+    ka, vv = call(
+        bind(setup_kernel), (filters, window), [plane_f32], 200_000_000, {}, w2, near, far
+    )
+    slope_near, means, vv = call(
         bind(near_kernel),
-        (filters, window, slopes, sds((low, C, wide), F32)),
+        (slopes, sds((low, C, wide), F32), window),
         [plane_f32],
-        900_000_000,
-        {},
-        w2,
-        near,
-        far,
+        700_000_000,
+        {2: 2},
         a1,
+        ka,
+        vv,
     )
     c1, c2 = swap(cot, cot, "gx")
     kb, k3f, k3b, cc = call(
@@ -499,10 +514,10 @@
         cc,
     )
     full, other, part = reduce_both(packet, keep, shared, "gx")
-    plane_near, gw = call(
+    plane_near = call(
         bind(back_near_kernel),
-        (sds((C * H, W), BF), window),
-        [plane_f32],
+        sds((C * H, W), BF),
+        [pltpu.VMEM(window.shape, BF), plane_f32],
         500_000_000,
         {},
         b1,
@@ -510,19 +525,19 @@
         p2,
         kb,
     )
-    gv, ft, _ = call(
+    gv, ft = call(
         bind(back_far_kernel),
-        (sds((C, 2, H, W), BF), sds((F * low, wide), BF), window),
-        [pltpu.VMEM((16 * C, low // 2 * wide), BF), plane_f32, plane_low_f32],
+        (sds((C, 2, H, W), BF), sds((F * low, wide), BF)),
+        [pltpu.VMEM(window.shape, BF), pltpu.VMEM((16 * C, low // 2 * wide), BF), plane_f32, plane_low_f32],
         700_000_000,
-        {6: 2},
+        {},
         b1,
         b2,
         p1,
+        p2,
         kb,
         k3f,
         plane_near,
-        gw,
     )
     two, three = call(
         lambda *refs: finish_kernel(C, count, *refs),

time: 40.6 us -> 40.7 us (level)
  the two profiles are of different devices: /device:TPU:11 before, /device:TPU:17 now
where the time goes in v3:
time: 40.7 us; the launch traced here: 40.5 us
  waiting for transfers between devices  16.3 us (40%)
  Pallas kernels  11.9 us (29%)
  starting transfers between devices  7.47 us (18%)
  local copies, waits for them, and re-layouts  3.9 us (10%)
  between operations  0.84 us (2%)
    pallas_call x9, Pallas kernels, call(): pl.pallas_call(body, out_shape=outs, in_specs=[VMEM] * len(args), out_spe...  11.9 us
    ppermute x5, waiting for transfers between devices, reduce_both(): lax.ppermute(v, axis, [(i, i ^ mask) for i in range(count)])  10.4 us
    ppermute x3, waiting for transfers between devices, swap(): lax.ppermute(far, ('groups', axis), pairs + [(b, a) for a, b in pairs])  5.89 us
    ppermute x5, starting transfers between devices, reduce_both(): lax.ppermute(v, axis, [(i, i ^ mask) for i in range(count)])  3.5 us
    unnamed x6, local copies, waits for them, and re-layouts  2.77 us
    ppermute x3, starting transfers between devices, swap(): lax.ppermute(far, ('groups', axis), pairs + [(b, a) for a, b in pairs])  2.76 us
    ppermute x3, starting transfers between devices, swap(): got_near = lax.ppermute(near, axis, pairs + [(b, a) for a, b in pairs])  1.21 us
    dynamic_slice x1, local copies, waits for them, and re-layouts, program(): lax.dynamic_index_in_dim(volume, odd, 1, keepdims=False).reshape(C * H, W)  1.08 us
  transfers between devices with their start and end apart: 11, of which 7 were waited for; matrix products, arithmetic and copies ran while one was open for 0% of the time, Pallas kernels for 19%

profile of v3, /device:TPU:17, one launch (start us, length us, event | category | flops | bytes accessed | tf_op | source)
XLA Modules:
  0.0 40.5 jit_solution(192609216099641856)
XLA Ops:
  0.6 1.1 %constant_dynamic-slice_fusion = (bf16[32,1,16,256]{3,2,1,0:T(8,128)(2,1)S(1)}, bf16[32,1,16,256]{3,2,1,0:T(8,128)(2,1)S(1)}) fusion(bf16[32,2,16,256]{3,2,1,0:T(8,128)(2,1)} %param.4, s32[]{:T(128)S(6)} %select_n.34, s32[]{:T(128)S(6)} %select_n.33), kind=kLoop, calls=%fused_computation.14 | loop fusion | bytes 1048584 | tf_op jit(solution)/shard_map/jit(dynamic_index_in_dim)/dynamic_slice | solution.py:439
  1.7 0.7 %collective-permute-start.2 = (bf16[512,256]{1,0:T(8,128)(2,1)S(1)}, bf16[512,256]{1,0:T(8,128)(2,1)S(1)}, u32[]{:S(2)}, u32[]{:S(2)}) collective-permute-start(bf16[512,256]{1,0:T(8,128)(2,1)S(1)} %bitcast.20), channel_id=1, source_target_pairs={{0,1},{2,3},{4,5},{6,7},{8,9},{10,11},{12,13},{14,15},{1,0},{3,2},... | collective-permute-start | bytes 786440 | tf_op jit(solution)/shard_map/ppermute | solution.py:404
  2.5 1.2 %collective-permute-start.3 = (bf16[512,256]{1,0:T(8,128)(2,1)S(1)}, bf16[512,256]{1,0:T(8,128)(2,1)S(1)}, u32[]{:S(2)}, u32[]{:S(2)}) collective-permute-start(bf16[512,256]{1,0:T(8,128)(2,1)S(1)} %bitcast.18), channel_id=1, source_target_pairs={{1,2},{3,4},{5,6},{7,8},{9,10},{11,12},{13,14},{17,18},{19,20},{21... | collective-permute-start | bytes 786440 | tf_op jit(solution)/shard_map/ppermute | solution.py:402
  3.7 0.3 collective-permute-start
  4.0 1.3 %collective-permute-start.1 = (bf16[512,128]{1,0:T(8,128)(2,1)}, bf16[512,128]{1,0:T(8,128)(2,1)S(1)}, u32[]{:S(2)}, u32[]{:S(2)}) collective-permute-start(bf16[512,128]{1,0:T(8,128)(2,1)} %bitcast.26), channel_id=1, source_target_pairs={{1,2},{3,4},{5,6},{7,8},{9,10},{11,12},{13,14},{17,18},{19,20},{21... | collective-permute-start | bytes 393224 | tf_op jit(solution)/shard_map/ppermute | solution.py:402
  5.3 0.9 %copy-done = bf16[32,32,3,3,3]{1,0,4,3,2:T(8,128)(2,1)S(1)} copy-done((bf16[32,32,3,3,3]{1,0,4,3,2:T(8,128)(2,1)S(1)}, bf16[32,32,3,3,3]{1,0,4,3,2:T(8,128)(2,1)}, u32[]{:S(2)}) %copy-start) | copy-done | bytes 55320
  6.2 0.6 %shard_map.75 = (bf16[2,192,512]{2,1,0:T(8,128)(2,1)S(1)}, bf16[512,2048]{1,0:T(8,128)(2,1)S(1)}) custom-call(bf16[27,32,32]{2,1,0:T(8,128)(2,1)S(1)} %bitcast.22, bf16[512,256]{1,0:T(8,128)(2,1)S(1)} %bitcast.21, bf16[512,256]{1,0:T(8,128)(2,1)S(1)} %bitcast.19), custom_call_target="tpu_custom_call" | custom-call | flops 200000 | bytes 1024 | tf_op jit(solution)/shard_map/pallas_call | solution.py:384
  6.9 0.0 copy-start.1
  6.9 0.9 %copy-done.1 = bf16[64,32,3,3,3]{0,1,4,3,2:T(8,128)(2,1)S(1)} copy-done((bf16[64,32,3,3,3]{0,1,4,3,2:T(8,128)(2,1)S(1)}, bf16[64,32,3,3,3]{0,1,4,3,2:T(8,128)(2,1)}, u32[]{:S(2)}) %copy-start.1) | copy-done | bytes 110616
  7.8 0.9 %copy-done.2 = bf16[64,1,8,128]{3,2,1,0:T(8,128)(2,1)S(1)} copy-done((bf16[64,1,8,128]{3,2,1,0:T(8,128)(2,1)S(1)}, bf16[64,1,8,128]{3,2,1,0:T(8,128)(2,1)}, u32[]{:S(2)}) %copy-start.2) | copy-done | bytes 131096
  8.7 0.7 %shard_map.78 = (bf16[2,192,512]{2,1,0:T(8,128)(2,1)S(1)}, bf16[384,512]{1,0:T(8,128)(2,1)S(1)}, bf16[192,768]{1,0:T(8,128)(2,1)S(1)}, bf16[768,512]{1,0:T(8,128)(2,1)S(1)}) custom-call(bf16[27,32,32]{2,1,0:T(8,128)(2,1)S(1)} %bitcast.23, bf16[27,32,64]{2,1,0:T(8,128)(2,1)S(1)} %bitcast.24, bf16[512,128]{1,0:T(8,128)(2,1)S(1)} %bitcast.27), custom_call_target="tpu_custom_call" | custom-call | flops 400000 | bytes 1024 | tf_op jit(solution)/shard_map/pallas_call | solution.py:384
  9.4 2.1 %shard_map.76 = (f32[8,64,256]{2,1,0:T(8,128)S(1)}, f32[8,32,128]{2,1,0:T(8,128)S(1)}, bf16[512,2048]{1,0:T(8,128)(2,1)S(1)}) custom-call(bf16[512,256]{1,0:T(8,128)(2,1)S(1)} %collective-permute-done.2.a1, bf16[2,192,512]{2,1,0:T(8,128)(2,1)S(1)} %get-tuple-element.25.ka, bf16[512,2048]{1,0:T(8,128)(2,1)S(1)} %get-tuple-element.26.vv_in), custom_call_target="tpu_custom_call", output_to_operand_aliasing={{2}: (2, {})} | custom-call | flops 700000 | bytes 1024 | tf_op jit(solution)/shard_map/pallas_call | solution.py:384
  11.6 0.9 %collective-permute-done.3.a2 = bf16[512,256]{1,0:T(8,128)(2,1)S(1)} collective-permute-done((bf16[512,256]{1,0:T(8,128)(2,1)S(1)}, bf16[512,256]{1,0:T(8,128)(2,1)S(1)}, u32[]{:S(2)}, u32[]{:S(2)}) %collective-permute-start.3) | collective-permute-done | bytes 262176 | tf_op jit(solution)/shard_map/ppermute | solution.py:402
  12.5 2.1 %shard_map.77 = (f32[8,64,256]{2,1,0:T(8,128)S(1)}, bf16[128,256]{1,0:T(8,128)(2,1)S(1)}, bf16[512,2048]{1,0:T(8,128)(2,1)S(1)}) custom-call(bf16[512,256]{1,0:T(8,128)(2,1)S(1)} %collective-permute-done.3.a2, bf16[2,192,512]{2,1,0:T(8,128)(2,1)S(1)} %get-tuple-element.25.ka, ...), custom_call_target="tpu_custom_call", output_to_operand_aliasing={{2}: (3, {})} | custom-call | flops 700000 | bytes 1024 | tf_op jit(solution)/shard_map/pallas_call | solution.py:384
  14.6 0.7 %shard_map.79 = (bf16[640,256]{1,0:T(8,128)(2,1)S(1)}, bf16[640,256]{1,0:T(8,128)(2,1)S(1)}, bf16[768,512]{1,0:T(8,128)(2,1)S(1)}) custom-call(bf16[512,128]{1,0:T(8,128)(2,1)S(1)} %collective-permute-done.c1, bf16[512,128]{1,0:T(8,128)(2,1)S(1)} %collective-permute-done.1.c2, ...), custom_call_target="tpu_custom_call", output_to_operand_aliasing={{2}: (6, {})} | custom-call | flops 400000 | bytes 1024 | tf_op jit(solution)/shard_map/pallas_call | solution.py:384
  15.4 1.6 %shard_map.82 = (bf16[7,48,128]{2,1,0:T(8,128)(2,1)S(1)}, f32[7,48,128]{2,1,0:T(8,128)S(1)}) custom-call(bf16[640,256]{1,0:T(8,128)(2,1)S(1)} %get-tuple-element.34.p1.refs_0_, bf16[640,256]{1,0:T(8,128)(2,1)S(1)} %get-tuple-element.35.p2.refs_1_, bf16[512,2048]{1,0:T(8,128)(2,1)S(1)} %get-tuple-element.39.refs_2_, ...), custom_call_target="tpu_custom_call" | custom-call | flops 1200000 | bytes 1024 | tf_op jit(solution)/shard_map/pallas_call | solution.py:384
  17.0 0.1 collective-permute-start.6
  17.1 1.3 %collective-permute-done.6 = bf16[7,48,128]{2,1,0:T(8,128)(2,1)S(1)} collective-permute-done((bf16[7,48,128]{2,1,0:T(8,128)(2,1)S(1)}, bf16[7,48,128]{2,1,0:T(8,128)(2,1)S(1)}, u32[]{:S(2)}, u32[]{:S(2)}) %collective-permute-start.6) | collective-permute-done | bytes 86048 | tf_op jit(solution)/shard_map/ppermute | solution.py:411
  18.5 1.4 %collective-permute-start.7 = (bf16[7,32,128]{2,1,0:T(8,128)(2,1)S(1)}, bf16[7,32,128]{2,1,0:T(8,128)(2,1)S(1)}, u32[]{:S(2)}, u32[]{:S(2)}) collective-permute-start(bf16[7,32,128]{2,1,0:T(8,128)(2,1)S(1)} %pad_maximum_fusion), channel_id=1, source_target_pairs={{0,5},{1,4},{2,7},{3,6},{4,1},{5,0},{6,3},{7,2},{8,13},{9,12},{10,... | collective-permute-start | bytes 172040 | tf_op jit(solution)/shard_map/ppermute | solution.py:411
  19.9 2.3 %collective-permute-done.7 = bf16[7,32,128]{2,1,0:T(8,128)(2,1)S(1)} collective-permute-done((bf16[7,32,128]{2,1,0:T(8,128)(2,1)S(1)}, bf16[7,32,128]{2,1,0:T(8,128)(2,1)S(1)}, u32[]{:S(2)}, u32[]{:S(2)}) %collective-permute-start.7) | collective-permute-done | bytes 57376 | tf_op jit(solution)/shard_map/ppermute | solution.py:411
  22.3 0.2 collective-permute-start.8
  22.4 4.3 %collective-permute-done.8 = bf16[7,24,128]{2,1,0:T(8,128)(2,1)S(1)} collective-permute-done((bf16[7,24,128]{2,1,0:T(8,128)(2,1)S(1)}, bf16[7,24,128]{2,1,0:T(8,128)(2,1)S(1)}, u32[]{:S(2)}, u32[]{:S(2)}) %collective-permute-start.8) | collective-permute-done | bytes 43040 | tf_op jit(solution)/shard_map/ppermute | solution.py:411
  26.7 1.6 %collective-permute-start.9 = (bf16[7,20,128]{2,1,0:T(8,128)(2,1)S(1)}, bf16[7,20,128]{2,1,0:T(8,128)(2,1)S(1)}, u32[]{:S(2)}, u32[]{:S(2)}) collective-permute-start(bf16[7,20,128]{2,1,0:T(8,128)(2,1)S(1)} %pad_maximum_fusion.2), channel_id=1, source_target_pairs={{0,3},{1,2},{2,1},{3,0},{4,7},{5,6},{6,5},{7,4},{8,11},{9,10},{10,... | collective-permute-start | bytes 107528 | tf_op jit(solution)/shard_map/ppermute | solution.py:411
  28.3 0.2 collective-permute-start.4
  28.5 0.2 collective-permute-start.5
  28.7 1.5 %collective-permute-done.9 = bf16[7,20,128]{2,1,0:T(8,128)(2,1)S(1)} collective-permute-done((bf16[7,20,128]{2,1,0:T(8,128)(2,1)S(1)}, bf16[7,20,128]{2,1,0:T(8,128)(2,1)S(1)}, u32[]{:S(2)}, u32[]{:S(2)}) %collective-permute-start.9) | collective-permute-done | bytes 35872 | tf_op jit(solution)/shard_map/ppermute | solution.py:411
  30.3 0.3 collective-permute-start.10
  30.6 1.0 %collective-permute-done.10.refs_1_ = f32[7,16,128]{2,1,0:T(8,128)S(1)} collective-permute-done((f32[7,16,128]{2,1,0:T(8,128)S(1)}, f32[7,16,128]{2,1,0:T(8,128)S(1)}, u32[]{:S(2)}, u32[]{:S(2)}) %collective-permute-start.10) | collective-permute-done | bytes 57376 | tf_op jit(solution)/shard_map/ppermute | solution.py:411
  31.6 0.9 %shard_map.83 = (f32[27,32,32]{2,1,0:T(8,128)}, f32[27,4,32]{2,1,0:T(4,128)}) custom-call(f32[7,16,128]{2,1,0:T(8,128)S(1)} %convert_add_fusion.1.refs_0_, f32[7,16,128]{2,1,0:T(8,128)S(1)} %collective-permute-done.10.refs_1_, f32[7,4,128]{2,1,0:T(4,128)S(1)} %convert_add_fusion.4.refs_2_), custom_call_target="tpu_custom_call" | custom-call | flops 100 | bytes 1024 | tf_op jit(solution)/shard_map/pallas_call | solution.py:384
  32.5 1.0 %shard_map.80.plane_near = bf16[512,256]{1,0:T(8,128)(2,1)S(1)} custom-call(bf16[640,256]{1,0:T(8,128)(2,1)S(1)} %collective-permute-done.4.b1, bf16[640,256]{1,0:T(8,128)(2,1)S(1)} %get-tuple-element.34.p1.refs_0_, bf16[640,256]{1,0:T(8,128)(2,1)S(1)} %get-tuple-element.35.p2.refs_1_, bf16[2,192,512]{2,1,0:T(8,128)(2,1)S(1)} %get-tuple-element.36.kb), custom_call_target="tpu_custom_call" | custom-call | flops 500000 | bytes 1024 | tf_op jit(solution)/shard_map/pallas_call | solution.py:384
  33.5 5.0 %collective-permute-done.5.b2 = bf16[640,256]{1,0:T(8,128)(2,1)S(1)} collective-permute-done((bf16[640,256]{1,0:T(8,128)(2,1)S(1)}, bf16[640,256]{1,0:T(8,128)(2,1)S(1)}, u32[]{:S(2)}, u32[]{:S(2)}) %collective-permute-start.5) | collective-permute-done | bytes 327712 | tf_op jit(solution)/shard_map/ppermute | solution.py:402
  38.5 2.0 %shard_map.81 = (bf16[32,2,16,256]{3,2,1,0:T(8,128)(2,1)}, bf16[512,128]{1,0:T(8,128)(2,1)}) custom-call(bf16[640,256]{1,0:T(8,128)(2,1)S(1)} %collective-permute-done.4.b1, bf16[640,256]{1,0:T(8,128)(2,1)S(1)} %collective-permute-done.5.b2, bf16[640,256]{1,0:T(8,128)(2,1)S(1)} %get-tuple-element.34.p1.refs_0_, ...), custom_call_target="tpu_custom_call" | custom-call | flops 700000 | bytes 1024 | tf_op jit(solution)/shard_map/pallas_call | solution.py:384
  (20 shorter events, 0.2 us)
Async XLA Ops:
  1.7 7.7 %collective-permute-start.2 = (bf16[512,256]{1,0:T(8,128)(2,1)S(1)}, bf16[512,256]{1,0:T(8,128)(2,1)S(1)}, u32[]{:S(2)}, u32[]{:S(2)}) collective-permute-start(bf16[512,256]{1,0:T(8,128)(2,1)S(1)} %bitcast.20), channel_id=1, source_target_pairs={{0,1},{2,3},{4,5},{6,7},{8,9},{10,11},{12,13},{14,15},{1,0},{3,2},... | collective-permute-start | bytes 786440 | tf_op jit(solution)/shard_map/ppermute | solution.py:404
  2.5 10.0 %collective-permute-start.3 = (bf16[512,256]{1,0:T(8,128)(2,1)S(1)}, bf16[512,256]{1,0:T(8,128)(2,1)S(1)}, u32[]{:S(2)}, u32[]{:S(2)}) collective-permute-start(bf16[512,256]{1,0:T(8,128)(2,1)S(1)} %bitcast.18), channel_id=1, source_target_pairs={{1,2},{3,4},{5,6},{7,8},{9,10},{11,12},{13,14},{17,18},{19,20},{21... | collective-permute-start | bytes 786440 | tf_op jit(solution)/shard_map/ppermute | solution.py:402
  3.7 10.9 %collective-permute-start = (bf16[512,128]{1,0:T(8,128)(2,1)}, bf16[512,128]{1,0:T(8,128)(2,1)S(1)}, u32[]{:S(2)}, u32[]{:S(2)}) collective-permute-start(bf16[512,128]{1,0:T(8,128)(2,1)} %bitcast.25), channel_id=1, source_target_pairs={{0,1},{2,3},{4,5},{6,7},{8,9},{10,11},{12,13},{14,15},{1,0},{3,2},... | collective-permute-start | bytes 393224 | tf_op jit(solution)/shard_map/ppermute | solution.py:404
  4.0 10.6 %collective-permute-start.1 = (bf16[512,128]{1,0:T(8,128)(2,1)}, bf16[512,128]{1,0:T(8,128)(2,1)S(1)}, u32[]{:S(2)}, u32[]{:S(2)}) collective-permute-start(bf16[512,128]{1,0:T(8,128)(2,1)} %bitcast.26), channel_id=1, source_target_pairs={{1,2},{3,4},{5,6},{7,8},{9,10},{11,12},{13,14},{17,18},{19,20},{21... | collective-permute-start | bytes 393224 | tf_op jit(solution)/shard_map/ppermute | solution.py:402
  5.3 0.9 %copy-start = (bf16[32,32,3,3,3]{1,0,4,3,2:T(8,128)(2,1)S(1)}, bf16[32,32,3,3,3]{1,0,4,3,2:T(8,128)(2,1)}, u32[]{:S(2)}) copy-start(bf16[32,32,3,3,3]{1,0,4,3,2:T(8,128)(2,1)} %param.5) | copy-start | bytes 165892
  6.9 0.9 %copy-start.1 = (bf16[64,32,3,3,3]{0,1,4,3,2:T(8,128)(2,1)S(1)}, bf16[64,32,3,3,3]{0,1,4,3,2:T(8,128)(2,1)}, u32[]{:S(2)}) copy-start(bf16[64,32,3,3,3]{0,1,4,3,2:T(8,128)(2,1)} %param.6) | copy-start | bytes 331780
  7.8 0.9 %copy-start.2 = (bf16[64,1,8,128]{3,2,1,0:T(8,128)(2,1)S(1)}, bf16[64,1,8,128]{3,2,1,0:T(8,128)(2,1)}, u32[]{:S(2)}) copy-start(bf16[64,1,8,128]{3,2,1,0:T(8,128)(2,1)} %param.7) | copy-start | bytes 393220
  17.0 1.3 %collective-permute-start.6 = (bf16[7,48,128]{2,1,0:T(8,128)(2,1)S(1)}, bf16[7,48,128]{2,1,0:T(8,128)(2,1)S(1)}, u32[]{:S(2)}, u32[]{:S(2)}) collective-permute-start(bf16[7,48,128]{2,1,0:T(8,128)(2,1)S(1)} %get-tuple-element.42), channel_id=1, source_target_pairs={{0,1},{1,0},{2,3},{3,2},{4,5},{5,4},{6,7},{7,6},{8,9},{9,8},{10,11... | collective-permute-start | bytes 258056 | tf_op jit(solution)/shard_map/ppermute | solution.py:411
  18.5 3.7 %collective-permute-start.7 = (bf16[7,32,128]{2,1,0:T(8,128)(2,1)S(1)}, bf16[7,32,128]{2,1,0:T(8,128)(2,1)S(1)}, u32[]{:S(2)}, u32[]{:S(2)}) collective-permute-start(bf16[7,32,128]{2,1,0:T(8,128)(2,1)S(1)} %pad_maximum_fusion), channel_id=1, source_target_pairs={{0,5},{1,4},{2,7},{3,6},{4,1},{5,0},{6,3},{7,2},{8,13},{9,12},{10,... | collective-permute-start | bytes 172040 | tf_op jit(solution)/shard_map/ppermute | solution.py:411
  22.3 4.4 %collective-permute-start.8 = (bf16[7,24,128]{2,1,0:T(8,128)(2,1)S(1)}, bf16[7,24,128]{2,1,0:T(8,128)(2,1)S(1)}, u32[]{:S(2)}, u32[]{:S(2)}) collective-permute-start(bf16[7,24,128]{2,1,0:T(8,128)(2,1)S(1)} %pad_maximum_fusion.1), channel_id=1, source_target_pairs={{0,9},{1,8},{2,11},{3,10},{4,13},{5,12},{6,15},{7,14},{8,1},{9,0},... | collective-permute-start | bytes 129032 | tf_op jit(solution)/shard_map/ppermute | solution.py:411
  26.7 3.5 %collective-permute-start.9 = (bf16[7,20,128]{2,1,0:T(8,128)(2,1)S(1)}, bf16[7,20,128]{2,1,0:T(8,128)(2,1)S(1)}, u32[]{:S(2)}, u32[]{:S(2)}) collective-permute-start(bf16[7,20,128]{2,1,0:T(8,128)(2,1)S(1)} %pad_maximum_fusion.2), channel_id=1, source_target_pairs={{0,3},{1,2},{2,1},{3,0},{4,7},{5,6},{6,5},{7,4},{8,11},{9,10},{10,... | collective-permute-start | bytes 107528 | tf_op jit(solution)/shard_map/ppermute | solution.py:411
  28.3 4.2 %collective-permute-start.4 = (bf16[640,256]{1,0:T(8,128)(2,1)S(1)}, bf16[640,256]{1,0:T(8,128)(2,1)S(1)}, u32[]{:S(2)}, u32[]{:S(2)}) collective-permute-start(bf16[640,256]{1,0:T(8,128)(2,1)S(1)} %get-tuple-element.34.p1.refs_0_), channel_id=1, source_target_pairs={{0,1},{2,3},{4,5},{6,7},{8,9},{10,11},{12,13},{14,15},{1,0},{3,2},... | collective-permute-start | bytes 983048 | tf_op jit(solution)/shard_map/ppermute | solution.py:404
  28.5 10.0 %collective-permute-start.5 = (bf16[640,256]{1,0:T(8,128)(2,1)S(1)}, bf16[640,256]{1,0:T(8,128)(2,1)S(1)}, u32[]{:S(2)}, u32[]{:S(2)}) collective-permute-start(bf16[640,256]{1,0:T(8,128)(2,1)S(1)} %get-tuple-element.35.p2.refs_1_), channel_id=1, source_target_pairs={{1,2},{3,4},{5,6},{7,8},{9,10},{11,12},{13,14},{17,18},{19,20},{21... | collective-permute-start | bytes 983048 | tf_op jit(solution)/shard_map/ppermute | solution.py:402
  30.3 1.3 %collective-permute-start.10 = (f32[7,16,128]{2,1,0:T(8,128)S(1)}, f32[7,16,128]{2,1,0:T(8,128)S(1)}, u32[]{:S(2)}, u32[]{:S(2)}) collective-permute-start(f32[7,16,128]{2,1,0:T(8,128)S(1)} %convert_add_fusion.1.refs_0_), channel_id=1, source_target_pairs={{0,1},{1,0},{2,3},{3,2},{4,5},{5,4},{6,7},{7,6},{8,9},{9,8},{10,11... | collective-permute-start | bytes 172040 | tf_op jit(solution)/shard_map/ppermute | solution.py:411

commit v4 on v3

--- a/solution.py
+++ b/solution.py
@@ -71,108 +71,111 @@
     return jnp.where((index == 0) | (index == lax.axis_size("gx") - 1), 0.0, 1.0)
 
 
-def fill_plane(dst, tile_of, rows, pairs, planes, plane, height, width):
+def fill_plane(dst, tile_of, rows, pairs, plane, height, width):
     for h in range(rows):
         tile = tile_of(h)
         for b, j in windows(h, pairs):
-            at = pl.multiple_of((j * planes + plane) * height, height)
+            at = pl.multiple_of((plane * 4 + j) * height, height)
             dst[pl.ds(at, height), b * width : b * width + width] = tile
 
 
 def clear_ends(dst, planes, height, pairs, width):
-    dst[: planes * height, :width] = jnp.zeros((planes * height, width), BF)
-    dst[3 * planes * height :, (pairs - 1) * width :] = jnp.zeros((planes * height, width), BF)
+    for plane in range(planes):
+        at = plane * 4 * height
+        dst[at : at + height, :width] = jnp.zeros((height, width), BF)
+        dst[at + 3 * height : at + 4 * height, (pairs - 1) * width :] = jnp.zeros((height, width), BF)
 
 
 def setup_kernel(C, F, H, W, w2, near, far, ka, vv, xf):
     span = 4 * C
     halves, low = W // LANES, H // 2
     odd = parity()
-    ka[...] = jnp.zeros(ka.shape, BF)
-    stacks = [w2[dt * 9 : dt * 9 + 9].reshape(9 * C, C) for dt in range(3)]
-    for d in range(2):
-        tiles = sum(dot(stacks[dt], place(C, span, (dt + d) * C)) for dt in range(3)).astype(BF)
+    stacks = [
+        jnp.concatenate([w2[tap(dt, ht, wt)] for dt in range(3) for wt in range(3)], axis=0) for ht in range(3)
+    ]
+    for h in range(2):
+        tiles = sum(dot(stacks[ht], place(C, span, (ht + h) * C)) for ht in range(3)).astype(BF)
         for wt in range(3):
-            for h in range(2):
-                at = (wt * 2 + h) * C
-                for ht in range(3):
-                    lane = (h + ht) * span
-                    g = ht * 3 + wt
-                    ka[d, at : at + C, lane : lane + span] = tiles[g * C : g * C + C]
+            at = (wt * 2 + h) * C
+            for dt in range(3):
+                g = dt * 3 + wt
+                ka[at : at + C, dt * span : dt * span + span] = tiles[g * C : g * C + C]
     for src, plane in ((near, 2 - odd), (far, 1 + odd)):
         unpack(src, xf, halves)
-        fill_plane(vv, lambda h: row_of(xf, h, C, H, 0, halves), H, low, 4, plane, C, W)
-    zero = jnp.zeros((C, W), BF)
-    fill_plane(vv, lambda h: zero, H, low, 4, 3 * odd, C, W)
+        fill_plane(vv, lambda h: row_of(xf, h, C, H, 0, halves), H, low, plane, C, W)
     clear_ends(vv, 4, C, low, W)
 
 
-def near_kernel(C, F, H, W, a1, ka, vv_in, slope, means, vv, xf):
+def near_kernel(C, F, H, W, a1, ka, vv_in, slope, means, vv, xf, y):
     halves, low = W // LANES, H // 2
     odd = parity()
     unpack(a1, xf, halves)
-    fill_plane(vv, lambda h: row_of(xf, h, C, H, 0, halves), H, low, 4, 3 - 3 * odd, C, W)
-    forward_plane(C, H, W, ka, 1 - odd, vv, slope, lambda b, mean: means.__setitem__(b, mean))
-
-
-def forward_plane(C, H, W, ka, d, vv, slope, put):
+    fill_plane(vv, lambda h: row_of(xf, h, C, H, 0, halves), H, low, 3 - 3 * odd, C, W)
+    forward_plane(C, H, W, ka, 1 - odd, vv, y, slope, lambda b, mean: means.__setitem__(b, mean))
+
+
+def overlapped(pairs, produce, consume):
+    produce(0)
+    for b in range(pairs):
+        if b + 1 < pairs:
+            produce(b + 1)
+        consume(b)
+
+
+def product(C, W, filters, d, window, y):
+    start = pl.multiple_of(d * 4 * C, 4 * C)
+
+    def produce(b):
+        y[b] = dot(filters[...], window[pl.ds(start, 12 * C), b * W : b * W + W])
+
+    return produce
+
+
+def forward_plane(C, H, W, ka, d, vv, y, slope, put):
     wide = W // 2
     eighth = jnp.where(iota((W, wide), 0) // 2 == iota((W, wide), 1), 0.125, 0.0).astype(BF)
-    for b in range(H // 2):
-        value = taps_sum(dot(ka[d], vv[:, b * W : b * W + W]), 2 * C, W)
+
+    def consume(b):
+        value = taps_sum(y.at[b], 2 * C, W)
         sigma = jax.nn.sigmoid(value)
         slope[b] = sigma * (1.0 + value * (1.0 - sigma))
         sums = dot((value * sigma).astype(BF), eighth)
         put(b, sums[:C] + sums[C:])
 
-
-def far_kernel(C, F, H, W, a2, ka, means, vv_in, slope, pooled, vv, xf):
+    overlapped(H // 2, product(C, W, ka, d, vv, y), consume)
+
+
+def far_kernel(C, F, H, W, a2, ka, means, vv_in, slope, pooled, vv, xf, y):
     halves, low, wide = W // LANES, H // 2, W // 2
     odd = parity()
     unpack(a2, xf, halves, inside())
-    fill_plane(vv, lambda h: row_of(xf, h, C, H, 0, halves), H, low, 4, 3 * odd, C, W)
+    fill_plane(vv, lambda h: row_of(xf, h, C, H, 0, halves), H, low, 3 * odd, C, W)
     quarter = low // 2
 
     def put(b, mean):
         at, lane = (b % quarter) * C, (b // quarter) * wide
         pooled[at : at + C, lane : lane + wide] = (mean + means[b]).astype(BF)
 
-    forward_plane(C, H, W, ka, odd, vv, slope, put)
+    forward_plane(C, H, W, ka, odd, vv, y, slope, put)
 
 
 def prep_kernel(C, F, H, W, w2, w3, cot, kb, k3f, k3b, cc, cf):
     span, low, wide = 4 * C, H // 2, W // 2
-    kb[...] = jnp.zeros(kb.shape, BF)
-    k3f[...] = jnp.zeros(k3f.shape, BF)
-    eye_c = place(C, C, 0)
-    zero_c = jnp.zeros((C, C), BF)
-    for d in range(2):
-        rows = []
-        for wt in range(3):
-            for ht in range(3):
-                three = [w2[tap(2 - dt, 2 - ht, 2 - wt)] for dt in range(3)]
-                rows += ([zero_c] + three) if d else (three + [zero_c])
-        tiles = dot_nt(eye_c, jnp.concatenate(rows, axis=0)).astype(BF)
-        for wt in range(3):
-            for h in range(2):
-                at = (wt * 2 + h) * C
-                for ht in range(3):
-                    lane = (h + ht) * span
-                    q = wt * 3 + ht
-                    kb[d, at : at + C, lane : lane + span] = tiles[:, q * span : q * span + span]
-    zero_f = jnp.zeros((C, F), BF)
-    rows = []
-    for wt in range(3):
-        for ht in range(3):
-            rows += [w3[tap(dt, ht, wt)] for dt in range(3)] + [zero_f]
-    tiles = dot_nt(place(F, F, 0), jnp.concatenate(rows, axis=0)).astype(BF)
-    for wt in range(3):
+    fine = lambda dt, ht, wt: w2[tap(2 - dt, 2 - ht, 2 - wt)]
+    coarse = lambda dt, ht, wt: w3[tap(dt, ht, wt)]
+    for size, pick, out in ((C, fine, kb), (F, coarse, k3f)):
+        zero = jnp.zeros((C, size), BF)
         for h in range(2):
-            at = (wt * 2 + h) * F
-            for ht in range(3):
-                lane = (h + ht) * span
-                q = wt * 3 + ht
-                k3f[at : at + F, lane : lane + span] = tiles[:, q * span : q * span + span]
+            rows = []
+            for wt in range(3):
+                for dt in range(3):
+                    three = [pick(dt, ht, wt) for ht in range(3)]
+                    rows += ([zero] + three) if h else (three + [zero])
+            tiles = dot_nt(place(size, size, 0), jnp.concatenate(rows, axis=0)).astype(BF)
+            for wt in range(3):
+                at = (wt * 2 + h) * size
+                lane = wt * 3 * span
+                out[at : at + size, :] = tiles[:, lane : lane + 3 * span]
     four = 4 * F
     picked = [
         jnp.concatenate([w3[tap(2 - dt, 2 - ht, 2 - wt)] for wt in range(3) for dt in range(3)], axis=0)
@@ -187,75 +190,72 @@
                 k3b[at : at + C, dt * four : dt * four + four] = tiles[q * C : q * C + C]
     unpack(cot, cf, wide // LANES)
     fill_cot(F, H, W, cc, cf, 1)
-    for plane in range(3):
-        cc[plane * four : plane * four + F, :wide] = jnp.zeros((F, wide), BF)
-        cc[plane * four + 3 * F : plane * four + four, (low // 2 - 1) * wide :] = jnp.zeros((F, wide), BF)
+    clear_ends(cc, 3, F, low // 2, wide)
 
 
 def fill_cot(F, H, W, cc, cf, plane):
     low, wide = H // 2, W // 2
-    for h in range(low):
-        tile = row_of(cf, h, F, low, 0, wide // LANES)
-        for b, j in windows(h, low // 2):
-            at = pl.multiple_of((plane * 4 + j) * F, F)
-            cc[pl.ds(at, F), b * wide : b * wide + wide] = tile
-
-
-def slope_kernel(C, F, H, W, c1, c2, slope_near, slope_far, pooled, k3b, cc_in, p1, p2, cc, cf, bp):
+    fill_plane(cc, lambda h: row_of(cf, h, F, low, 0, wide // LANES), low, low // 2, plane, F, wide)
+
+
+def early_kernel(C, F, H, W, c1, pooled, cc_in, cc, ps, p3, cf):
     low, wide = H // 2, W // 2
     odd = parity()
-    for src, plane, scale in ((c1, 2 - 2 * odd, None), (c2, 2 * odd, inside())):
-        unpack(src, cf, wide // LANES, scale)
-        fill_cot(F, H, W, cc, cf, plane)
-    bp[...] = taps_sum(dot(k3b[...], cc[...]), 2 * C, wide).astype(BF)
-    spread = jnp.where(iota((wide, W), 1) // 2 == iota((wide, W), 0), 0.125, 0.0).astype(BF)
-    for b in range(low):
-        back = dot(bp[(b % 2) * C : (b % 2) * C + C, (b // 2) * wide : (b // 2) * wide + wide], spread)
-        back = jnp.concatenate([back, back], axis=0)
-        for out, slope in ((p1, slope_near), (p2, slope_far)):
-            out[b * 2 * C : (b + 1) * 2 * C, :] = (back * slope[b]).astype(BF)
-    for out in (p1, p2):
-        out[H * C :, :] = pooled[...]
-
-
-def grads_kernel(C, F, H, W, count, p1, p2, vv, cc, packet, keep, gg, ps, r2, r3):
-    low, wide = H // 2, W // 2
-    odd = parity()
-    for b in range(low):
-        for d, src in ((1 - odd, p1), (odd, p2)):
-            tile = src[b * 2 * C : (b + 1) * 2 * C, :]
-            up = tile.astype(F32)
-            for wt in range(3):
-                val = tile if wt == 1 else moved(up, 1 - wt, W).astype(BF)
-                at = pl.multiple_of((wt * 2 + d) * 2 * C, 2 * C)
-                gg[pl.ds(at, 2 * C), b * W : b * W + W] = val
-    both = dot_nt(gg[...], vv[...])
-    span = 4 * C
-    twos = []
-    for wt in range(3):
-        for ht in range(3):
-            parts = []
-            for d in range(2):
-                at = (wt * 4 + d * 2) * C
-                parts.append(
-                    both[at : at + C, ht * span : ht * span + span]
-                    + both[at + C : at + 2 * C, (ht + 1) * span : (ht + 2) * span]
-                )
-            twos.append(parts[0] + pltpu.roll(parts[1], span - C, 1))
-    r2[...] = jnp.concatenate(dense(twos, C), axis=1)
+    plane = 2 - 2 * odd
+    unpack(c1, cf, wide // LANES)
+    fill_cot(F, H, W, cc, cf, plane)
     quarter = low // 2
     ps[...] = jnp.zeros(ps.shape, BF)
     for b in range(low // 2):
         for q in range(2):
             h = 2 * b + q
-            at, lane = H * C + (h % quarter) * C, (h // quarter) * wide
-            tile = p1[at : at + C, lane : lane + wide]
+            at, lane = (h % quarter) * C, (h // quarter) * wide
+            tile = pooled[at : at + C, lane : lane + wide]
             up = tile.astype(F32)
             for wt in range(3):
                 val = tile if wt == 1 else moved(up, wt - 1, wide).astype(BF)
                 to = (q * 4 + wt) * C
                 ps[to : to + C, b * wide : b * wide + wide] = val
-    p3 = dot_nt(cc[...], ps[...])
+    for at in (4 * F, pl.multiple_of(plane * 4 * F, 4 * F)):
+        p3[pl.ds(at, 4 * F), :] = dot_nt(cc[pl.ds(at, 4 * F), :], ps[...])
+
+
+def grads_kernel(C, F, H, W, count, *refs):
+    c2, slope_near, slope_far, pooled, k3b, vv, ps, _, _ = refs[:9]
+    p1, p2, packet, keep, cc, p3 = refs[9:15]
+    cf, bp, gg, r2, r3 = refs[15:]
+    low, wide, span = H // 2, W // 2, 4 * C
+    odd = parity()
+    plane = 2 * odd
+    unpack(c2, cf, wide // LANES, inside())
+    fill_cot(F, H, W, cc, cf, plane)
+    bp[...] = taps_sum(dot(k3b[...], cc[...]), 2 * C, wide).astype(BF)
+    at = pl.multiple_of(plane * 4 * F, 4 * F)
+    p3[pl.ds(at, 4 * F), :] = dot_nt(cc[pl.ds(at, 4 * F), :], ps[...])
+    spread = jnp.where(iota((wide, W), 1) // 2 == iota((wide, W), 0), 0.125, 0.0).astype(BF)
+    for b in range(low):
+        back = dot(bp[(b % 2) * C : (b % 2) * C + C, (b // 2) * wide : (b // 2) * wide + wide], spread)
+        back = jnp.concatenate([back, back], axis=0)
+        for d, out, slope in ((1 - odd, p1, slope_near), (odd, p2, slope_far)):
+            tile = (back * slope[b]).astype(BF)
+            out[b * 2 * C : (b + 1) * 2 * C, :] = tile
+            up = tile.astype(F32)
+            for wt in range(3):
+                val = tile if wt == 1 else moved(up, 1 - wt, W).astype(BF)
+                at = pl.multiple_of((d * 3 + wt) * 2 * C, 2 * C)
+                gg[pl.ds(at, 2 * C), b * W : b * W + W] = val
+    for out in (p1, p2):
+        out[H * C :, :] = pooled[...]
+    planes = [dot_nt(gg[d * 6 * C : (d + 1) * 6 * C, :], vv[d * span : d * span + 3 * span, :]) for d in range(2)]
+    twos = []
+    for wt in range(3):
+        for dt in range(3):
+            parts = []
+            for h in range(2):
+                at = (wt * 2 + h) * C
+                parts.append(sum(both[at : at + C, dt * span : dt * span + span] for both in planes))
+            twos.append(parts[0] + pltpu.roll(parts[1], span - C, 1))
+    r2[...] = jnp.concatenate(dense(twos, C), axis=1)
     tiles = []
     for dt in range(3):
         for ht in range(3):
@@ -312,7 +312,7 @@
         first = first ^ ((own >> bit) & 1)
     for t in range(27):
         dt, ht, wt = t // 9, t // 3 % 3, t % 3
-        q, group = divmod(wt * 9 + ht * 3 + dt, 4)
+        q, group = divmod(wt * 9 + dt * 3 + ht, 4)
         for src, at in ((own_half, first), (got_half, 1 - first)):
             tile = src[q]
             if group:
@@ -325,43 +325,43 @@
         three[t] = tile[:, :C]
 
 
-def backward_plane(C, H, W, kb, d, gw, zf):
-    for b in range(H // 2):
-        out = taps_sum(dot(kb[d], gw[:, b * W : b * W + W]), 2 * C, W)
+def backward_plane(C, H, W, kb, d, gw, y, zf):
+    def consume(b):
+        out = taps_sum(y.at[b], 2 * C, W)
         for q in range(2):
             for half in range(W // LANES):
                 lanes = slice(half * LANES, (half + 1) * LANES)
                 zf[half, pl.ds(2 * b + q, C, stride=H), :] = out[q * C : q * C + C, lanes]
 
-
-def back_near_kernel(C, F, H, W, b1, p1, p2, kb, plane_near, gw, zf):
+    overlapped(H // 2, product(C, W, kb, d, gw, y), consume)
+
+
+def back_near_kernel(C, F, H, W, b1, p1, p2, kb, plane_near, gw, zf, y):
     low, halves = H // 2, W // LANES
     odd = parity()
     for src, plane in ((p1, 2 - odd), (p2, 1 + odd), (b1, 3 - 3 * odd)):
-        fill_plane(gw, lambda h: src[h * C : h * C + C, :], H, low, 4, plane, C, W)
-    zero = jnp.zeros((C, W), BF)
-    fill_plane(gw, lambda h: zero, H, low, 4, 3 * odd, C, W)
+        fill_plane(gw, lambda h: src[h * C : h * C + C, :], H, low, plane, C, W)
     clear_ends(gw, 4, C, low, W)
-    backward_plane(C, H, W, kb, 1 - odd, gw, zf)
+    backward_plane(C, H, W, kb, 1 - odd, gw, y, zf)
     for half in range(halves):
         plane_near[:, half * LANES : (half + 1) * LANES] = zf[half].astype(BF)
 
 
-def back_far_kernel(C, F, H, W, b1, b2, p1, p2, kb, k3f, plane_near, gv, ft, gw, pp, zf, ff):
+def back_far_kernel(C, F, H, W, b1, b2, p1, p2, kb, k3f, plane_near, gv, ft, gw, pp, zf, ff, y):
     low, wide = H // 2, W // 2
     quarter, halves, low_halves = low // 2, W // LANES, wide // LANES
     odd = parity()
     scale = inside().astype(BF)
-    for src, plane in ((p1, 2 - odd), (p2, 1 + odd), (b1, 3 - 3 * odd)):
-        fill_plane(gw, lambda h: src[h * C : h * C + C, :], H, low, 4, plane, C, W)
-    fill_plane(gw, lambda h: b2[h * C : h * C + C, :] * scale, H, low, 4, 3 * odd, C, W)
+    for src, plane in ((p1, 2 - odd), (p2, 1 + odd)):
+        fill_plane(gw, lambda h: src[h * C : h * C + C, :], H, low, plane, C, W)
+    fill_plane(gw, lambda h: b2[h * C : h * C + C, :] * scale, H, low, 3 * odd, C, W)
     clear_ends(gw, 4, C, low, W)
-    backward_plane(C, H, W, kb, odd, gw, zf)
+    backward_plane(C, H, W, kb, odd, gw, y, zf)
     for c in range(C):
         rows = slice(c * H, c * H + H)
         gv[c, 1 - odd] = plane_near[rows, :]
         gv[c, odd] = jnp.concatenate([zf[half, rows, :] for half in range(halves)], axis=1).astype(BF)
-    pp[...] = jnp.zeros(pp.shape, BF)
+    clear_ends(pp, 3, C, quarter, wide)
     for src, plane in ((b1, 2 - 2 * odd), (b2, 2 * odd), (p1, 1)):
 
         def tile_of(h):
@@ -369,7 +369,7 @@
             tile = src[at : at + C, lane : lane + wide]
             return tile * scale if src is b2 else tile
 
-        fill_plane(pp, tile_of, low, quarter, 4, plane, C, wide)
+        fill_plane(pp, tile_of, low, quarter, plane, C, wide)
     out = taps_sum(dot(k3f[...], pp[...]), 2 * F, wide)
     for b in range(quarter):
         for q in range(2):
@@ -441,7 +441,8 @@
     halves, low_halves = W // LANES, wide // LANES
     bind = lambda body: functools.partial(body, C, F, H, W)
     window, window_cot = sds((16 * C, low * W), BF), sds((12 * F, low // 2 * wide), BF)
-    filters, slopes = sds((2, 6 * C, 16 * C), BF), sds((low, 2 * C, W), F32)
+    filters, slopes = sds((6 * C, 12 * C), BF), sds((low, 2 * C, W), F32)
+    products = pltpu.VMEM((low, 6 * C, W), F32)
     plane_f32 = pltpu.VMEM((halves, C * H, LANES), F32)
     plane_low_f32 = pltpu.VMEM((low_halves, F * low, LANES), F32)
     ka, vv = call(
@@ -450,7 +451,7 @@
     slope_near, means, vv = call(
         bind(near_kernel),
         (slopes, sds((low, C, wide), F32), window),
-        [plane_f32],
+        [plane_f32, products],
         700_000_000,
         {2: 2},
         a1,
@@ -460,7 +461,7 @@
     c1, c2 = swap(cot, cot, "gx")
     kb, k3f, k3b, cc = call(
         bind(prep_kernel),
-        (filters, sds((6 * F, 16 * C), BF), sds((6 * C, 12 * F), BF), window_cot),
+        (filters, sds((6 * F, 12 * C), BF), sds((6 * C, 12 * F), BF), window_cot),
         [plane_low_f32],
         400_000_000,
         {},
@@ -472,7 +473,7 @@
     slope_far, pooled, vv = call(
         bind(far_kernel),
         (slopes, sds((rows, W), BF), window),
-        [plane_f32],
+        [plane_f32, products],
         700_000_000,
         {3: 2},
         a2,
@@ -480,44 +481,54 @@
         means,
         vv,
     )
+    tiles, shared = 7, C // 2
+    shifted, partial = sds((8 * C, low // 2 * wide), BF), sds((12 * F, 8 * C), F32)
+    cc, ps, p3 = call(
+        bind(early_kernel),
+        (window_cot, shifted, partial),
+        [plane_low_f32],
+        100_000_000,
+        {2: 0},
+        c1,
+        pooled,
+        cc,
+    )
     rows = H * C + rows
-    p1, p2, cc = call(
-        bind(slope_kernel),
-        (sds((rows, W), BF), sds((rows, W), BF), window_cot),
-        [plane_low_f32, pltpu.VMEM((2 * C, low // 2 * wide), BF)],
-        400_000_000,
-        {6: 2},
-        c1,
+    p1, p2, packet, keep, _, _ = call(
+        lambda *refs: grads_kernel(C, F, H, W, count, *refs),
+        (
+            sds((rows, W), BF),
+            sds((rows, W), BF),
+            sds((tiles, shared + F // 2, 4 * C), BF),
+            sds((tiles, shared + F // 2, 4 * C), F32),
+            window_cot,
+            partial,
+        ),
+        [
+            plane_low_f32,
+            pltpu.VMEM((2 * C, low // 2 * wide), BF),
+            pltpu.VMEM((12 * C, low * W), BF),
+            pltpu.VMEM((C, tiles * 4 * C), F32),
+            pltpu.VMEM((F, tiles * 4 * C), F32),
+        ],
+        1_200_000_000,
+        {7: 4, 8: 5},
         c2,
         slope_near,
         slope_far,
         pooled,
         k3b,
+        vv,
+        ps,
         cc,
+        p3,
     )
     b1, b2 = swap(p1, p2, "gx")
-    tiles, shared = 7, C // 2
-    packet, keep = call(
-        lambda *refs: grads_kernel(C, F, H, W, count, *refs),
-        (sds((tiles, shared + F // 2, 4 * C), BF), sds((tiles, shared + F // 2, 4 * C), F32)),
-        [
-            pltpu.VMEM((12 * C, low * W), BF),
-            pltpu.VMEM((8 * C, low // 2 * wide), BF),
-            pltpu.VMEM((C, tiles * 4 * C), F32),
-            pltpu.VMEM((F, tiles * 4 * C), F32),
-        ],
-        1_200_000_000,
-        {},
-        p1,
-        p2,
-        vv,
-        cc,
-    )
     full, other, part = reduce_both(packet, keep, shared, "gx")
     plane_near = call(
         bind(back_near_kernel),
         sds((C * H, W), BF),
-        [pltpu.VMEM(window.shape, BF), plane_f32],
+        [pltpu.VMEM(window.shape, BF), plane_f32, products],
         500_000_000,
         {},
         b1,
@@ -528,7 +539,7 @@
     gv, ft = call(
         bind(back_far_kernel),
         (sds((C, 2, H, W), BF), sds((F * low, wide), BF)),
-        [pltpu.VMEM(window.shape, BF), pltpu.VMEM((16 * C, low // 2 * wide), BF), plane_f32, plane_low_f32],
+        [pltpu.VMEM(window.shape, BF), pltpu.VMEM((12 * C, low // 2 * wide), BF), plane_f32, plane_low_f32, products],
         700_000_000,
         {},
         b1,

time: 40.7 us -> 40.5 us (level)
  Pallas kernels: 11.9 us -> 10.9 us
  local copies, waits for them, and re-layouts: 3.9 us -> 4.84 us
    pallas_call x9, Pallas kernels: 11.9 us -> 10.9 us  [call(): pl.pallas_call(body, out_shape=outs, in_specs=[VMEM] * len(args), out_spe...]
    unnamed x6 -> x8, local copies, waits for them, and re-layouts: 2.77 us -> 3.71 us
  transfers between devices with their start and end apart: 11 -> 11, of which waited for: 7 -> 7; matrix products, arithmetic and copies ran while one was open for 0% -> 0% of each run, Pallas kernels for 19% -> 17%
where the time goes in v4:
time: 40.5 us; the launch traced here: 40.2 us
  waiting for transfers between devices  16 us (40%)
  Pallas kernels  10.9 us (27%)
  starting transfers between devices  7.49 us (18%)
  local copies, waits for them, and re-layouts  4.84 us (12%)
  between operations  0.84 us (2%)
    pallas_call x9, Pallas kernels, call(): pl.pallas_call(body, out_shape=outs, in_specs=[VMEM] * len(args), out_spe...  10.9 us
    ppermute x5, waiting for transfers between devices, reduce_both(): lax.ppermute(v, axis, [(i, i ^ mask) for i in range(count)])  10.4 us
    ppermute x3, waiting for transfers between devices, swap(): lax.ppermute(far, ('groups', axis), pairs + [(b, a) for a, b in pairs])  5.6 us
    unnamed x8, local copies, waits for them, and re-layouts  3.71 us
    ppermute x5, starting transfers between devices, reduce_both(): lax.ppermute(v, axis, [(i, i ^ mask) for i in range(count)])  3.54 us
    ppermute x3, starting transfers between devices, swap(): lax.ppermute(far, ('groups', axis), pairs + [(b, a) for a, b in pairs])  2.74 us
    ppermute x3, starting transfers between devices, swap(): got_near = lax.ppermute(near, axis, pairs + [(b, a) for a, b in pairs])  1.21 us
    dynamic_slice x1, local copies, waits for them, and re-layouts, program(): lax.dynamic_index_in_dim(volume, odd, 1, keepdims=False).reshape(C * H, W)  1.08 us
  transfers between devices with their start and end apart: 11, of which 7 were waited for; matrix products, arithmetic and copies ran while one was open for 0% of the time, Pallas kernels for 17%

profile of v4, /device:TPU:17, one launch (start us, length us, event | category | flops | bytes accessed | tf_op | source)
XLA Modules:
  0.0 40.2 jit_solution(11784769116101670347)
XLA Ops:
  0.6 1.1 %constant_dynamic-slice_fusion = (bf16[32,1,16,256]{3,2,1,0:T(8,128)(2,1)S(1)}, bf16[32,1,16,256]{3,2,1,0:T(8,128)(2,1)S(1)}) fusion(bf16[32,2,16,256]{3,2,1,0:T(8,128)(2,1)} %param.4, s32[]{:T(128)S(6)} %select_n.34, s32[]{:T(128)S(6)} %select_n.33), kind=kLoop, calls=%fused_computation.14 | loop fusion | bytes 1048584 | tf_op jit(solution)/shard_map/jit(dynamic_index_in_dim)/dynamic_slice | solution.py:439
  1.7 0.7 %collective-permute-start.1 = (bf16[512,256]{1,0:T(8,128)(2,1)S(1)}, bf16[512,256]{1,0:T(8,128)(2,1)S(1)}, u32[]{:S(2)}, u32[]{:S(2)}) collective-permute-start(bf16[512,256]{1,0:T(8,128)(2,1)S(1)} %bitcast.20), channel_id=1, source_target_pairs={{0,1},{2,3},{4,5},{6,7},{8,9},{10,11},{12,13},{14,15},{1,0},{3,2},... | collective-permute-start | bytes 786440 | tf_op jit(solution)/shard_map/ppermute | solution.py:404
  2.5 1.2 %collective-permute-start.2 = (bf16[512,256]{1,0:T(8,128)(2,1)S(1)}, bf16[512,256]{1,0:T(8,128)(2,1)S(1)}, u32[]{:S(2)}, u32[]{:S(2)}) collective-permute-start(bf16[512,256]{1,0:T(8,128)(2,1)S(1)} %bitcast.18), channel_id=1, source_target_pairs={{1,2},{3,4},{5,6},{7,8},{9,10},{11,12},{13,14},{17,18},{19,20},{21... | collective-permute-start | bytes 786440 | tf_op jit(solution)/shard_map/ppermute | solution.py:402
  3.7 0.3 collective-permute-start.3
  4.0 1.3 %collective-permute-start = (bf16[512,128]{1,0:T(8,128)(2,1)}, bf16[512,128]{1,0:T(8,128)(2,1)S(1)}, u32[]{:S(2)}, u32[]{:S(2)}) collective-permute-start(bf16[512,128]{1,0:T(8,128)(2,1)} %bitcast.26), channel_id=1, source_target_pairs={{1,2},{3,4},{5,6},{7,8},{9,10},{11,12},{13,14},{17,18},{19,20},{21... | collective-permute-start | bytes 393224 | tf_op jit(solution)/shard_map/ppermute | solution.py:402
  5.3 0.9 %copy-done = bf16[32,32,3,3,3]{1,0,4,3,2:T(8,128)(2,1)S(1)} copy-done((bf16[32,32,3,3,3]{1,0,4,3,2:T(8,128)(2,1)S(1)}, bf16[32,32,3,3,3]{1,0,4,3,2:T(8,128)(2,1)}, u32[]{:S(2)}) %copy-start) | copy-done | bytes 55320
  6.2 0.6 %shard_map.75 = (bf16[192,384]{1,0:T(8,128)(2,1)S(1)}, bf16[512,2048]{1,0:T(8,128)(2,1)S(1)}) custom-call(bf16[27,32,32]{2,1,0:T(8,128)(2,1)S(1)} %bitcast.22, bf16[512,256]{1,0:T(8,128)(2,1)S(1)} %bitcast.21, bf16[512,256]{1,0:T(8,128)(2,1)S(1)} %bitcast.19), custom_call_target="tpu_custom_call" | custom-call | flops 200000 | bytes 1024 | tf_op jit(solution)/shard_map/pallas_call | solution.py:384
  6.8 0.9 %copy-done.1 = bf16[32,32,3,3,3]{1,0,4,3,2:T(8,128)(2,1)S(1)} copy-done((bf16[32,32,3,3,3]{1,0,4,3,2:T(8,128)(2,1)S(1)}, bf16[32,32,3,3,3]{1,0,4,3,2:T(8,128)(2,1)}, u32[]{:S(2)}) %copy-start.1) | copy-done | bytes 55320
  7.8 0.9 %copy-done.2 = bf16[64,32,3,3,3]{0,1,4,3,2:T(8,128)(2,1)S(1)} copy-done((bf16[64,32,3,3,3]{0,1,4,3,2:T(8,128)(2,1)S(1)}, bf16[64,32,3,3,3]{0,1,4,3,2:T(8,128)(2,1)}, u32[]{:S(2)}) %copy-start.2) | copy-done | bytes 110616
  8.7 0.9 %copy-done.3 = bf16[64,1,8,128]{3,2,1,0:T(8,128)(2,1)S(1)} copy-done((bf16[64,1,8,128]{3,2,1,0:T(8,128)(2,1)S(1)}, bf16[64,1,8,128]{3,2,1,0:T(8,128)(2,1)}, u32[]{:S(2)}) %copy-start.3) | copy-done | bytes 131096
  9.6 0.8 %shard_map.78 = (bf16[192,384]{1,0:T(8,128)(2,1)S(1)}, bf16[384,384]{1,0:T(8,128)(2,1)S(1)}, bf16[192,768]{1,0:T(8,128)(2,1)S(1)}, bf16[768,512]{1,0:T(8,128)(2,1)S(1)}) custom-call(bf16[27,32,32]{2,1,0:T(8,128)(2,1)S(1)} %bitcast.23, bf16[27,32,64]{2,1,0:T(8,128)(2,1)S(1)} %bitcast.24, bf16[512,128]{1,0:T(8,128)(2,1)S(1)} %bitcast.27), custom_call_target="tpu_custom_call" | custom-call | flops 400000 | bytes 1024 | tf_op jit(solution)/shard_map/pallas_call | solution.py:384
  10.4 1.6 %shard_map.76 = (f32[8,64,256]{2,1,0:T(8,128)S(1)}, f32[8,32,128]{2,1,0:T(8,128)S(1)}, bf16[512,2048]{1,0:T(8,128)(2,1)S(1)}) custom-call(bf16[512,256]{1,0:T(8,128)(2,1)S(1)} %collective-permute-done.1.a1, bf16[192,384]{1,0:T(8,128)(2,1)S(1)} %get-tuple-element.27.ka, bf16[512,2048]{1,0:T(8,128)(2,1)S(1)} %get-tuple-element.28.vv_in), custom_call_target="tpu_custom_call", output_to_operand_aliasing={{2}: (2, {})} | custom-call | flops 700000 | bytes 1024 | tf_op jit(solution)/shard_map/pallas_call | solution.py:384
  12.0 0.5 %collective-permute-done.2.a2 = bf16[512,256]{1,0:T(8,128)(2,1)S(1)} collective-permute-done((bf16[512,256]{1,0:T(8,128)(2,1)S(1)}, bf16[512,256]{1,0:T(8,128)(2,1)S(1)}, u32[]{:S(2)}, u32[]{:S(2)}) %collective-permute-start.2) | collective-permute-done | bytes 262176 | tf_op jit(solution)/shard_map/ppermute | solution.py:402
  12.5 1.6 %shard_map.77 = (f32[8,64,256]{2,1,0:T(8,128)S(1)}, bf16[128,256]{1,0:T(8,128)(2,1)S(1)}, bf16[512,2048]{1,0:T(8,128)(2,1)S(1)}) custom-call(bf16[512,256]{1,0:T(8,128)(2,1)S(1)} %collective-permute-done.2.a2, bf16[192,384]{1,0:T(8,128)(2,1)S(1)} %get-tuple-element.27.ka, ...), custom_call_target="tpu_custom_call", output_to_operand_aliasing={{2}: (3, {})} | custom-call | flops 700000 | bytes 1024 | tf_op jit(solution)/shard_map/pallas_call | solution.py:384
  14.1 0.4 %shard_map.79 = (bf16[768,512]{1,0:T(8,128)(2,1)S(1)}, bf16[256,512]{1,0:T(8,128)(2,1)S(1)}, f32[768,256]{1,0:T(8,128)S(1)}) custom-call(bf16[512,128]{1,0:T(8,128)(2,1)S(1)} %collective-permute-done.3.c1, bf16[128,256]{1,0:T(8,128)(2,1)S(1)} %get-tuple-element.33.pooled.refs_3_, ...), custom_call_target="tpu_custom_call", output_to_operand_aliasing={{0}: (2, {})} | custom-call | flops 100000 | bytes 1024 | tf_op jit(solution)/shard_map/pallas_call | solution.py:384
  14.5 2.3 %shard_map.80 = (bf16[640,256]{1,0:T(8,128)(2,1)S(1)}, bf16[640,256]{1,0:T(8,128)(2,1)S(1)}, bf16[7,48,128]{2,1,0:T(8,128)(2,1)S(1)}, f32[7,48,128]{2,1,0:T(8,12...) custom-call(bf16[512,128]{1,0:T(8,128)(2,1)S(1)} %collective-permute-d, ...), custom_call_target="tpu_custom_call", output_to_operand_aliasing={{4}: (7, {}), {5}: (8, {})} | custom-call | flops 1200000 | bytes 1024 | tf_op jit(solution)/shard_map/pallas_call | solution.py:384
  16.8 0.1 collective-permute-start.6
  16.9 1.3 %collective-permute-done.6 = bf16[7,48,128]{2,1,0:T(8,128)(2,1)S(1)} collective-permute-done((bf16[7,48,128]{2,1,0:T(8,128)(2,1)S(1)}, bf16[7,48,128]{2,1,0:T(8,128)(2,1)S(1)}, u32[]{:S(2)}, u32[]{:S(2)}) %collective-permute-start.6) | collective-permute-done | bytes 86048 | tf_op jit(solution)/shard_map/ppermute | solution.py:411
  18.2 1.4 %collective-permute-start.7 = (bf16[7,32,128]{2,1,0:T(8,128)(2,1)S(1)}, bf16[7,32,128]{2,1,0:T(8,128)(2,1)S(1)}, u32[]{:S(2)}, u32[]{:S(2)}) collective-permute-start(bf16[7,32,128]{2,1,0:T(8,128)(2,1)S(1)} %pad_maximum_fusion), channel_id=1, source_target_pairs={{0,5},{1,4},{2,7},{3,6},{4,1},{5,0},{6,3},{7,2},{8,13},{9,12},{10,... | collective-permute-start | bytes 172040 | tf_op jit(solution)/shard_map/ppermute | solution.py:411
  19.6 2.3 %collective-permute-done.7 = bf16[7,32,128]{2,1,0:T(8,128)(2,1)S(1)} collective-permute-done((bf16[7,32,128]{2,1,0:T(8,128)(2,1)S(1)}, bf16[7,32,128]{2,1,0:T(8,128)(2,1)S(1)}, u32[]{:S(2)}, u32[]{:S(2)}) %collective-permute-start.7) | collective-permute-done | bytes 57376 | tf_op jit(solution)/shard_map/ppermute | solution.py:411
  22.0 0.2 collective-permute-start.8
  22.2 4.3 %collective-permute-done.8 = bf16[7,24,128]{2,1,0:T(8,128)(2,1)S(1)} collective-permute-done((bf16[7,24,128]{2,1,0:T(8,128)(2,1)S(1)}, bf16[7,24,128]{2,1,0:T(8,128)(2,1)S(1)}, u32[]{:S(2)}, u32[]{:S(2)}) %collective-permute-start.8) | collective-permute-done | bytes 43040 | tf_op jit(solution)/shard_map/ppermute | solution.py:411
  26.5 1.6 %collective-permute-start.9 = (bf16[7,20,128]{2,1,0:T(8,128)(2,1)S(1)}, bf16[7,20,128]{2,1,0:T(8,128)(2,1)S(1)}, u32[]{:S(2)}, u32[]{:S(2)}) collective-permute-start(bf16[7,20,128]{2,1,0:T(8,128)(2,1)S(1)} %pad_maximum_fusion.2), channel_id=1, source_target_pairs={{0,3},{1,2},{2,1},{3,0},{4,7},{5,6},{6,5},{7,4},{8,11},{9,10},{10,... | collective-permute-start | bytes 107528 | tf_op jit(solution)/shard_map/ppermute | solution.py:411
  28.1 0.2 collective-permute-start.4
  28.3 0.2 collective-permute-start.5
  28.5 1.5 %collective-permute-done.9 = bf16[7,20,128]{2,1,0:T(8,128)(2,1)S(1)} collective-permute-done((bf16[7,20,128]{2,1,0:T(8,128)(2,1)S(1)}, bf16[7,20,128]{2,1,0:T(8,128)(2,1)S(1)}, u32[]{:S(2)}, u32[]{:S(2)}) %collective-permute-start.9) | collective-permute-done | bytes 35872 | tf_op jit(solution)/shard_map/ppermute | solution.py:411
  30.1 0.3 collective-permute-start.10
  30.4 1.0 %collective-permute-done.10.refs_1_ = f32[7,16,128]{2,1,0:T(8,128)S(1)} collective-permute-done((f32[7,16,128]{2,1,0:T(8,128)S(1)}, f32[7,16,128]{2,1,0:T(8,128)S(1)}, u32[]{:S(2)}, u32[]{:S(2)}) %collective-permute-start.10) | collective-permute-done | bytes 57376 | tf_op jit(solution)/shard_map/ppermute | solution.py:411
  31.4 0.9 %shard_map.83 = (f32[27,32,32]{2,1,0:T(8,128)}, f32[27,4,32]{2,1,0:T(4,128)}) custom-call(f32[7,16,128]{2,1,0:T(8,128)S(1)} %convert_add_fusion.1.refs_0_, f32[7,16,128]{2,1,0:T(8,128)S(1)} %collective-permute-done.10.refs_1_, f32[7,4,128]{2,1,0:T(4,128)S(1)} %convert_add_fusion.4.refs_2_), custom_call_target="tpu_custom_call" | custom-call | flops 100 | bytes 1024 | tf_op jit(solution)/shard_map/pallas_call | solution.py:384
  32.3 0.9 %shard_map.81.plane_near = bf16[512,256]{1,0:T(8,128)(2,1)S(1)} custom-call(bf16[640,256]{1,0:T(8,128)(2,1)S(1)} %collective-permute-done.4.b1, bf16[640,256]{1,0:T(8,128)(2,1)S(1)} %get-tuple-element.40.p1, bf16[640,256]{1,0:T(8,128)(2,1)S(1)} %get-tuple-element.41.p2, bf16[192,384]{1,0:T(8,128)(2,1)S(1)} %get-tuple-element.42.kb), custom_call_target="tpu_custom_call" | custom-call | flops 500000 | bytes 1024 | tf_op jit(solution)/shard_map/pallas_call | solution.py:384
  33.2 5.1 %collective-permute-done.5.b2 = bf16[640,256]{1,0:T(8,128)(2,1)S(1)} collective-permute-done((bf16[640,256]{1,0:T(8,128)(2,1)S(1)}, bf16[640,256]{1,0:T(8,128)(2,1)S(1)}, u32[]{:S(2)}, u32[]{:S(2)}) %collective-permute-start.5) | collective-permute-done | bytes 327712 | tf_op jit(solution)/shard_map/ppermute | solution.py:402
  38.3 1.9 %shard_map.82 = (bf16[32,2,16,256]{3,2,1,0:T(8,128)(2,1)}, bf16[512,128]{1,0:T(8,128)(2,1)}) custom-call(bf16[640,256]{1,0:T(8,128)(2,1)S(1)} %collective-permute-done.4.b1, bf16[640,256]{1,0:T(8,128)(2,1)S(1)} %collective-permute-done.5.b2, bf16[640,256]{1,0:T(8,128)(2,1)S(1)} %get-tuple-element.40.p1, bf16[640,256]{1,0:T(8,128)(2,1)S(1)} %get-tuple-element.41.p2, ...), custom_call_target="tpu_custom_call" | custom-call | flops 700000 | bytes 1024 | tf_op jit(solution)/shard_map/pallas_call | solution.py:384
  (22 shorter events, 0.2 us)
Async XLA Ops:
  1.7 8.7 %collective-permute-start.1 = (bf16[512,256]{1,0:T(8,128)(2,1)S(1)}, bf16[512,256]{1,0:T(8,128)(2,1)S(1)}, u32[]{:S(2)}, u32[]{:S(2)}) collective-permute-start(bf16[512,256]{1,0:T(8,128)(2,1)S(1)} %bitcast.20), channel_id=1, source_target_pairs={{0,1},{2,3},{4,5},{6,7},{8,9},{10,11},{12,13},{14,15},{1,0},{3,2},... | collective-permute-start | bytes 786440 | tf_op jit(solution)/shard_map/ppermute | solution.py:404
  2.5 10.0 %collective-permute-start.2 = (bf16[512,256]{1,0:T(8,128)(2,1)S(1)}, bf16[512,256]{1,0:T(8,128)(2,1)S(1)}, u32[]{:S(2)}, u32[]{:S(2)}) collective-permute-start(bf16[512,256]{1,0:T(8,128)(2,1)S(1)} %bitcast.18), channel_id=1, source_target_pairs={{1,2},{3,4},{5,6},{7,8},{9,10},{11,12},{13,14},{17,18},{19,20},{21... | collective-permute-start | bytes 786440 | tf_op jit(solution)/shard_map/ppermute | solution.py:402
  3.7 10.4 %collective-permute-start.3 = (bf16[512,128]{1,0:T(8,128)(2,1)}, bf16[512,128]{1,0:T(8,128)(2,1)S(1)}, u32[]{:S(2)}, u32[]{:S(2)}) collective-permute-start(bf16[512,128]{1,0:T(8,128)(2,1)} %bitcast.25), channel_id=1, source_target_pairs={{0,1},{2,3},{4,5},{6,7},{8,9},{10,11},{12,13},{14,15},{1,0},{3,2},... | collective-permute-start | bytes 393224 | tf_op jit(solution)/shard_map/ppermute | solution.py:404
  4.0 10.5 %collective-permute-start = (bf16[512,128]{1,0:T(8,128)(2,1)}, bf16[512,128]{1,0:T(8,128)(2,1)S(1)}, u32[]{:S(2)}, u32[]{:S(2)}) collective-permute-start(bf16[512,128]{1,0:T(8,128)(2,1)} %bitcast.26), channel_id=1, source_target_pairs={{1,2},{3,4},{5,6},{7,8},{9,10},{11,12},{13,14},{17,18},{19,20},{21... | collective-permute-start | bytes 393224 | tf_op jit(solution)/shard_map/ppermute | solution.py:402
  5.3 0.9 %copy-start = (bf16[32,32,3,3,3]{1,0,4,3,2:T(8,128)(2,1)S(1)}, bf16[32,32,3,3,3]{1,0,4,3,2:T(8,128)(2,1)}, u32[]{:S(2)}) copy-start(bf16[32,32,3,3,3]{1,0,4,3,2:T(8,128)(2,1)} %param.5) | copy-start | bytes 165892
  6.8 0.9 %copy-start.1 = (bf16[32,32,3,3,3]{1,0,4,3,2:T(8,128)(2,1)S(1)}, bf16[32,32,3,3,3]{1,0,4,3,2:T(8,128)(2,1)}, u32[]{:S(2)}) copy-start(bf16[32,32,3,3,3]{1,0,4,3,2:T(8,128)(2,1)} %param.5) | copy-start | bytes 165892
  7.8 0.9 %copy-start.2 = (bf16[64,32,3,3,3]{0,1,4,3,2:T(8,128)(2,1)S(1)}, bf16[64,32,3,3,3]{0,1,4,3,2:T(8,128)(2,1)}, u32[]{:S(2)}) copy-start(bf16[64,32,3,3,3]{0,1,4,3,2:T(8,128)(2,1)} %param.6) | copy-start | bytes 331780
  8.7 0.9 %copy-start.3 = (bf16[64,1,8,128]{3,2,1,0:T(8,128)(2,1)S(1)}, bf16[64,1,8,128]{3,2,1,0:T(8,128)(2,1)}, u32[]{:S(2)}) copy-start(bf16[64,1,8,128]{3,2,1,0:T(8,128)(2,1)} %param.7) | copy-start | bytes 393220
  16.8 1.3 %collective-permute-start.6 = (bf16[7,48,128]{2,1,0:T(8,128)(2,1)S(1)}, bf16[7,48,128]{2,1,0:T(8,128)(2,1)S(1)}, u32[]{:S(2)}, u32[]{:S(2)}) collective-permute-start(bf16[7,48,128]{2,1,0:T(8,128)(2,1)S(1)} %get-tuple-element.46), channel_id=1, source_target_pairs={{0,1},{1,0},{2,3},{3,2},{4,5},{5,4},{6,7},{7,6},{8,9},{9,8},{10,11... | collective-permute-start | bytes 258056 | tf_op jit(solution)/shard_map/ppermute | solution.py:411
  18.2 3.7 %collective-permute-start.7 = (bf16[7,32,128]{2,1,0:T(8,128)(2,1)S(1)}, bf16[7,32,128]{2,1,0:T(8,128)(2,1)S(1)}, u32[]{:S(2)}, u32[]{:S(2)}) collective-permute-start(bf16[7,32,128]{2,1,0:T(8,128)(2,1)S(1)} %pad_maximum_fusion), channel_id=1, source_target_pairs={{0,5},{1,4},{2,7},{3,6},{4,1},{5,0},{6,3},{7,2},{8,13},{9,12},{10,... | collective-permute-start | bytes 172040 | tf_op jit(solution)/shard_map/ppermute | solution.py:411
  22.0 4.4 %collective-permute-start.8 = (bf16[7,24,128]{2,1,0:T(8,128)(2,1)S(1)}, bf16[7,24,128]{2,1,0:T(8,128)(2,1)S(1)}, u32[]{:S(2)}, u32[]{:S(2)}) collective-permute-start(bf16[7,24,128]{2,1,0:T(8,128)(2,1)S(1)} %pad_maximum_fusion.1), channel_id=1, source_target_pairs={{0,9},{1,8},{2,11},{3,10},{4,13},{5,12},{6,15},{7,14},{8,1},{9,0},... | collective-permute-start | bytes 129032 | tf_op jit(solution)/shard_map/ppermute | solution.py:411
  26.5 3.5 %collective-permute-start.9 = (bf16[7,20,128]{2,1,0:T(8,128)(2,1)S(1)}, bf16[7,20,128]{2,1,0:T(8,128)(2,1)S(1)}, u32[]{:S(2)}, u32[]{:S(2)}) collective-permute-start(bf16[7,20,128]{2,1,0:T(8,128)(2,1)S(1)} %pad_maximum_fusion.2), channel_id=1, source_target_pairs={{0,3},{1,2},{2,1},{3,0},{4,7},{5,6},{6,5},{7,4},{8,11},{9,10},{10,... | collective-permute-start | bytes 107528 | tf_op jit(solution)/shard_map/ppermute | solution.py:411
  28.1 4.2 %collective-permute-start.4 = (bf16[640,256]{1,0:T(8,128)(2,1)S(1)}, bf16[640,256]{1,0:T(8,128)(2,1)S(1)}, u32[]{:S(2)}, u32[]{:S(2)}) collective-permute-start(bf16[640,256]{1,0:T(8,128)(2,1)S(1)} %get-tuple-element.40.p1), channel_id=1, source_target_pairs={{0,1},{2,3},{4,5},{6,7},{8,9},{10,11},{12,13},{14,15},{1,0},{3,2},... | collective-permute-start | bytes 983048 | tf_op jit(solution)/shard_map/ppermute | solution.py:404
  28.3 10.0 %collective-permute-start.5 = (bf16[640,256]{1,0:T(8,128)(2,1)S(1)}, bf16[640,256]{1,0:T(8,128)(2,1)S(1)}, u32[]{:S(2)}, u32[]{:S(2)}) collective-permute-start(bf16[640,256]{1,0:T(8,128)(2,1)S(1)} %get-tuple-element.41.p2), channel_id=1, source_target_pairs={{1,2},{3,4},{5,6},{7,8},{9,10},{11,12},{13,14},{17,18},{19,20},{21... | collective-permute-start | bytes 983048 | tf_op jit(solution)/shard_map/ppermute | solution.py:402
  30.1 1.3 %collective-permute-start.10 = (f32[7,16,128]{2,1,0:T(8,128)S(1)}, f32[7,16,128]{2,1,0:T(8,128)S(1)}, u32[]{:S(2)}, u32[]{:S(2)}) collective-permute-start(f32[7,16,128]{2,1,0:T(8,128)S(1)} %convert_add_fusion.1.refs_0_), channel_id=1, source_target_pairs={{0,1},{1,0},{2,3},{3,2},{4,5},{5,4},{6,7},{7,6},{8,9},{9,8},{10,11... | collective-permute-start | bytes 172040 | tf_op jit(solution)/shard_map/ppermute | solution.py:411
